TPU v7x, 8 devices: a whole 2x2x1 slice. The times are simulated.
8 devices in a mesh: pp: 2 (over z, y), ep: 4 (over x, core).
Axes of the slice: x: 2, y: 2, z: 1, core: 2. Of those that a mesh axis runs over, the one named last changes fastest.
Arguments:
- x_fwd: bfloat16 [2, 8192, 512], P('pp', 'ep')
- x_bwd: bfloat16 [2, 8192, 512], P('pp', 'ep')
- dy_bwd: bfloat16 [2, 8192, 512], P('pp', 'ep')
- ids_fwd: int32 [2, 8192, 4], P('pp', 'ep')
- gate_fwd: bfloat16 [2, 8192, 4], P('pp', 'ep')
- ids_bwd: int32 [2, 8192, 4], P('pp', 'ep')
- gate_bwd: bfloat16 [2, 8192, 4], P('pp', 'ep')
- w_in: bfloat16 [2, 512, 1280], P('pp')
- w_out: bfloat16 [2, 1280, 512], P('pp')
- w_gate: bfloat16 [2, 16, 512, 1280], P('pp', 'ep')
- w_up: bfloat16 [2, 16, 512, 1280], P('pp', 'ep')
- w_down: bfloat16 [2, 16, 1280, 512], P('pp', 'ep')
Outputs:
- output 1: bfloat16 [2, 8192, 512], P('pp', 'ep')
- output 2: bfloat16 [2, 8192, 512], P('pp', 'ep')
- output 3: float32 [2, 16, 512, 1280], P('pp', 'ep')
- output 4: float32 [2, 16, 512, 1280], P('pp', 'ep')
- output 5: float32 [2, 16, 1280, 512], P('pp', 'ep')
All inputs are finite; a program needn't handle non-finite values.
Results may differ from a plain program's by a relative error of at most 0.0143664.
Values are sent between devices in bfloat16 or wider.
A program may use at most 1 GiB of HBM per device.

v0:
```python
import jax
import jax.numpy as jnp
from jax import lax
from jax.sharding import PartitionSpec as P

EPS_NORM = 1e-6


def rms_norm(rows_in):
    rows_f32 = rows_in.astype(jnp.float32)
    return (rows_f32 * lax.rsqrt(jnp.mean(rows_f32 * rows_f32, axis=-1, keepdims=True) + EPS_NORM)).astype(jnp.bfloat16)


def dense_act(pre_act):
    return jax.nn.silu(pre_act.astype(jnp.float32)).astype(jnp.bfloat16)


def glu_act(gate_pre, up_pre):
    return (jax.nn.silu(gate_pre.astype(jnp.float32)) * up_pre.astype(jnp.float32)).astype(jnp.bfloat16)


def route_slots(ids_tok, n_exp, cap):
    flat_ids = ids_tok.reshape(-1)
    n_route = flat_ids.shape[0]
    onehot = (flat_ids[:, None] == jnp.arange(n_exp)[None, :]).astype(jnp.int32)
    route_rank = jnp.sum(jnp.cumsum(onehot, axis=0) * onehot, axis=1) - 1
    slot_flat = flat_ids * cap + route_rank
    slot_src = jnp.full((n_exp * cap,), n_route, jnp.int32).at[slot_flat].set(jnp.arange(n_route, dtype=jnp.int32))
    return slot_flat, slot_src


def exchange(buf):
    return lax.all_to_all(buf, 'ep', 0, 0, tiled=True)


def solution(mesh):
    n_ep = mesh.shape['ep']
    n_pp = mesh.shape['pp']
    fwd_perm = [(stage_idx, (stage_idx + 1) % n_pp) for stage_idx in range(n_pp)]
    bwd_perm = [(stage_idx, (stage_idx - 1) % n_pp) for stage_idx in range(n_pp)]
    f32 = jnp.float32
    bf16 = jnp.bfloat16

    def device_fn(x_fwd, x_bwd, dy_bwd, ids_fwd, gate_fwd, ids_bwd, gate_bwd, w_in, w_out, w_gate, w_up, w_down):
        fwd_x = x_fwd[0]
        bwd_x = x_bwd[0]
        bwd_dy = dy_bwd[0]
        stage_w_in = w_in[0]
        stage_w_out = w_out[0]
        stage_wg = w_gate[0]
        stage_wu = w_up[0]
        stage_wd = w_down[0]
        n_tok, width = fwd_x.shape
        top_k = ids_fwd.shape[2]
        e_loc = stage_wg.shape[0]
        n_exp = e_loc * n_ep
        cap = 3 * n_tok * top_k // n_exp
        zero_row = jnp.zeros((1, width), bf16)

        def dense_fwd(x_tok):
            norm_in = rms_norm(x_tok)
            pre_act = jnp.dot(norm_in, stage_w_in, preferred_element_type=f32).astype(bf16)
            mid_res = (x_tok.astype(f32) + jnp.dot(dense_act(pre_act), stage_w_out, preferred_element_type=f32)).astype(bf16)
            return pre_act, mid_res

        def expert_up(row_buf):
            gate_pre = jnp.einsum('slch,lhf->slcf', row_buf, stage_wg, preferred_element_type=f32).astype(bf16)
            up_pre = jnp.einsum('slch,lhf->slcf', row_buf, stage_wu, preferred_element_type=f32).astype(bf16)
            return gate_pre, up_pre

        _, mid_f = dense_fwd(fwd_x)
        norm_f = rms_norm(mid_f)
        slot_f, src_f = route_slots(ids_fwd[0], n_exp, cap)
        rows_f = exchange(jnp.concatenate([norm_f, zero_row])[src_f // top_k]).reshape(n_ep, e_loc, cap, width)
        gate_pre_f, up_pre_f = expert_up(rows_f)
        out_f = jnp.einsum('slcf,lfh->slch', glu_act(gate_pre_f, up_pre_f), stage_wd, preferred_element_type=f32).astype(bf16)
        back_f = exchange(out_f.reshape(n_exp * cap, width))
        routed = back_f[slot_f].reshape(n_tok, top_k, width)
        y_val = (mid_f.astype(f32) + jnp.einsum('tk,tkh->th', gate_fwd[0], routed, preferred_element_type=f32)).astype(bf16)

        pre_b, mid_b = dense_fwd(bwd_x)
        norm_b, norm_back = jax.vjp(rms_norm, mid_b)
        slot_b, src_b = route_slots(ids_bwd[0], n_exp, cap)
        tok_b = src_b // top_k
        rows_b = exchange(jnp.concatenate([norm_b, zero_row])[tok_b]).reshape(n_ep, e_loc, cap, width)
        gate_pre_b, up_pre_b = expert_up(rows_b)
        act_b, glu_back = jax.vjp(glu_act, gate_pre_b, up_pre_b)
        gate_slot = jnp.concatenate([gate_bwd[0].reshape(-1), jnp.zeros((1,), bf16)])[src_b]
        dy_rows = jnp.concatenate([bwd_dy, zero_row])[tok_b]
        grad_send = (dy_rows.astype(f32) * gate_slot.astype(f32)[:, None]).astype(bf16)
        d_out = exchange(grad_send).reshape(n_ep, e_loc, cap, width)
        dw_down = jnp.einsum('slcf,slch->lfh', act_b, d_out, preferred_element_type=f32)
        d_act = jnp.einsum('slch,lfh->slcf', d_out, stage_wd, preferred_element_type=f32).astype(bf16)
        d_gate_pre, d_up_pre = glu_back(d_act)
        dw_gate = jnp.einsum('slch,slcf->lhf', rows_b, d_gate_pre, preferred_element_type=f32)
        dw_up = jnp.einsum('slch,slcf->lhf', rows_b, d_up_pre, preferred_element_type=f32)
        d_rows = (jnp.einsum('slcf,lhf->slch', d_gate_pre, stage_wg, preferred_element_type=f32) + jnp.einsum('slcf,lhf->slch', d_up_pre, stage_wu, preferred_element_type=f32)).astype(bf16)
        d_back = exchange(d_rows.reshape(n_exp * cap, width))
        d_norm = jnp.sum(d_back[slot_b].reshape(n_tok, top_k, width).astype(f32), axis=1).astype(bf16)
        d_mid = bwd_dy + norm_back(d_norm)[0]
        d_hidden = jnp.einsum('th,fh->tf', d_mid, stage_w_out, preferred_element_type=f32).astype(bf16)
        _, dense_back = jax.vjp(dense_act, pre_b)
        d_pre = dense_back(d_hidden)[0]
        d_norm_in = jnp.einsum('tf,hf->th', d_pre, stage_w_in, preferred_element_type=f32).astype(bf16)
        _, norm_in_back = jax.vjp(rms_norm, bwd_x)
        dx_val = d_mid + norm_in_back(d_norm_in)[0]

        y_next = lax.ppermute(y_val, 'pp', fwd_perm)
        dx_prev = lax.ppermute(dx_val, 'pp', bwd_perm)
        return y_next[None], dx_prev[None], dw_gate[None], dw_up[None], dw_down[None]

    spec_act = P('pp', 'ep', None)
    spec_dense = P('pp', None, None)
    spec_exp = P('pp', 'ep', None, None)
    return jax.shard_map(device_fn, mesh=mesh, in_specs=(spec_act, spec_act, spec_act, spec_act, spec_act, spec_act, spec_act, spec_dense, spec_dense, spec_exp, spec_exp, spec_exp), out_specs=(spec_act, spec_act, spec_exp, spec_exp, spec_exp), check_vma=False)
```

profile of v0, /device:TPU:0, one launch (start us, length us, event | category | flops | bytes accessed | tf_op | source)
XLA Modules:
  0.0 1708.4 jit_solution(13344794852628215847)
XLA Ops:
  10.9 10.0 reduce-window.16
  25.0 31.1 %scatter_custom_fusion.1 = s32[24576]{0:T(1024)} fusion(s32[8192]{0:T(1024)S(1)} %bitcast.255, s32[8192]{0:T(1024)S(1)} %iota.20, s32[]{:T(128)} %constant.62.clone.1), kind=kCustom, calls=%fused_computation.173 | custom fusion | bytes 98308 | tf_op jit(solution)/shard_map/scatter | solution.py:28
  66.5 98.7 %gather_fusion.4 = bf16[24576,512]{1,0:T(8,128)(2,1)} fusion(bf16[2049,512]{1,0:T(8,128)(2,1)S(1)} %concatenate.15, s32[24576]{0:T(1024)S(1)} %get-tuple-element.8), kind=kCustom, calls=%fused_computation.4 | custom fusion | bytes 50429952 | tf_op jit(solution)/shard_map/gather | solution.py:85
  165.2 8.7 all-to-all-start.3
  184.4 151.1 %gather_fusion.3 = bf16[24576]{0:T(1024)(128)(2,1)S(1)} fusion(bf16[8193]{0:T(1024)(128)(2,1)S(1)} %pad_maximum_fusion, s32[24576]{0:T(1024)S(1)} %copy-done.9), kind=kCustom, calls=%fused_computation.3 | custom fusion | bytes 196608 | tf_op jit(solution)/shard_map/gather | solution.py:88
  339.9 98.6 %gather_fusion.2 = bf16[24576,512]{1,0:T(8,128)(2,1)} fusion(bf16[2049,512]{1,0:T(8,128)(2,1)S(1)} %concatenate.13, s32[24576]{0:T(1024)S(1)} %get-tuple-element.8), kind=kCustom, calls=%fused_computation.2 | custom fusion | bytes 50429952 | tf_op jit(solution)/shard_map/gather | solution.py:89
  440.7 22.3 %fusion.18 = bf16[4,6144,512]{2,1,0:T(8,128)(2,1)} fusion(bf16[4,6144,512]{2,1,0:T(8,128)(2,1)} %bitcast.250, f32[4,6144]{1,0:T(4,128)} %reshape.233), kind=kLoop, calls=%fused_computation.41 | loop fusion | flops 37748736 | bytes 50429952 | tf_op jit(solution)/shard_map/convert_element_type | solution.py:90
  483.1 31.5 %scatter_custom_fusion = s32[24576]{0:T(1024)} fusion(s32[8192]{0:T(1024)S(1)} %bitcast.257, s32[8192]{0:T(1024)S(1)} %iota.19, s32[]{:T(128)} %constant.62.clone.1), kind=kCustom, calls=%fused_computation.175 | custom fusion | bytes 98308 | tf_op jit(solution)/shard_map/scatter | solution.py:28
  515.5 98.6 %gather_fusion = bf16[24576,512]{1,0:T(8,128)(2,1)} fusion(bf16[2049,512]{1,0:T(8,128)(2,1)S(1)} %concatenate.12, s32[24576]{0:T(1024)S(1)} %fusion.116), kind=kCustom, calls=%fused_computation | custom fusion | bytes 50429952 | tf_op jit(solution)/shard_map/gather | solution.py:74
  616.2 41.4 %convolution_convert_fusion = bf16[4,4,1536,1280]{3,2,1,0:T(8,128)(2,1)} fusion(bf16[4,4,1536,512]{3,2,1,0:T(8,128)(2,1)} %bitcast.38, bf16[1,4,512,1280]{3,2,1,0:T(8,128)(2,1)} %param.21), kind=kOutput, calls=%fused_computation.30 | convolution fusion | flops 32243712000 | bytes 93323264 | tf_op jit(solution)/shard_map/slch,lhf->slcf/dot_general | solution.py:67
  657.5 41.4 %convolution_convert_fusion.1 = bf16[4,4,1536,1280]{3,2,1,0:T(8,128)(2,1)} fusion(bf16[4,4,1536,512]{3,2,1,0:T(8,128)(2,1)} %bitcast.38, bf16[1,4,512,1280]{3,2,1,0:T(8,128)(2,1)} %param.22), kind=kOutput, calls=%fused_computation.31 | convolution fusion | flops 32243712000 | bytes 93323264 | tf_op jit(solution)/shard_map/slch,lhf->slcf/dot_general | solution.py:68
  698.9 46.0 %all-to-all-done.2 = bf16[4,6144,512]{2,1,0:T(8,128)(2,1)} async-done(((bf16[4,6144,512]{2,1,0:T(8,128)(2,1)}), bf16[4,6144,512]{2,1,0:T(8,128)(2,1)}, u32[]{:S(2)}, u32[]{:S(2)}) %all-to-all-start.2) | async-done | bytes 25165856 | tf_op jit(solution)/shard_map/all_to_all | solution.py:33
  753.6 101.8 %fusion.7 = (bf16[4,4,1536,1280]{3,2,0,1:T(8,128)(2,1)}, bf16[4,4,1536,1280]{3,2,0,1:T(8,128)(2,1)}) fusion(bf16[4,4,1536,1280]{3,2,1,0:T(8,128)(2,1)} %convolution_convert_fusion, bf16[4,4,1536,1280]{3,2,1,0:T(8,128)(2,1)} %convolution_convert_fusion.1, bf16[1,4,1280,512]{3,2,1,0:T(8,128)(2,1)} %param.23, bf16[4,4,1536,512]{3,2,1,0:T(8,128)(2,1)} %bitcast.32), kind=kOutput, calls=%fused_computation.22 | convolution fusion | flops 32778485760 | bytes 282066944 | tf_op jit(solution)/shard_map/slch,lfh->slcf/dot_general | solution.py:93
  855.3 47.2 %fusion.56 = f32[4,4,1536,512]{3,2,1,0:T(8,128)} fusion(bf16[4,4,1536,1280]{3,2,0,1:T(8,128)(2,1)} %get-tuple-element.6, bf16[1,4,512,1280]{3,2,1,0:T(8,128)(2,1)} %param.21), kind=kOutput, calls=%fused_computation.96 | convolution fusion | flops 32212254720 | bytes 118489088 | tf_op jit(solution)/shard_map/slcf,lhf->slch/dot_general | solution.py:97
  902.6 51.6 %fusion.27 = bf16[4,4,1536,512]{3,2,0,1:T(8,128)(2,1)} fusion(f32[4,4,1536,512]{3,2,1,0:T(8,128)} %fusion.56, bf16[4,4,1536,1280]{3,2,0,1:T(8,128)(2,1)} %get-tuple-element.5, bf16[1,4,512,1280]{3,2,1,0:T(8,128)(2,1)} %param.22), kind=kOutput, calls=%fused_computation.50 | convolution fusion | flops 32237420544 | bytes 143654912 | tf_op jit(solution)/shard_map/slcf,lhf->slch/dot_general | solution.py:97
  954.1 20.5 %copy.33 = bf16[4,4,1536,512]{3,2,1,0:T(8,128)(2,1)} copy(bf16[4,4,1536,512]{3,2,0,1:T(8,128)(2,1)} %fusion.27) | data formatting | bytes 50331648 | tf_op jit(solution)/shard_map/convert_element_type | solution.py:97
  974.6 51.5 %all-to-all-done = bf16[4,6144,512]{2,1,0:T(8,128)(2,1)} async-done(((bf16[4,6144,512]{2,1,0:T(8,128)(2,1)}), bf16[4,6144,512]{2,1,0:T(8,128)(2,1)}, u32[]{:S(2)}, u32[]{:S(2)}) %all-to-all-start) | async-done | bytes 25165856 | tf_op jit(solution)/shard_map/all_to_all | solution.py:33
  1026.2 8.8 all-to-all-start.4
  1035.0 41.4 %convolution_convert_fusion.4 = bf16[4,4,1536,1280]{3,2,1,0:T(8,128)(2,1)} fusion(bf16[4,4,1536,512]{3,2,1,0:T(8,128)(2,1)} %bitcast.8, bf16[1,4,512,1280]{3,2,1,0:T(8,128)(2,1)} %param.21), kind=kOutput, calls=%fused_computation.34 | convolution fusion | flops 32243712000 | bytes 93323264 | tf_op jit(solution)/shard_map/slch,lhf->slcf/dot_general | solution.py:67
  1076.4 79.2 %convert_bitcast_fusion = bf16[4,4,1536,512]{3,2,0,1:T(8,128)(2,1)} fusion(bf16[4,4,1536,1280]{3,2,1,0:T(8,128)(2,1)} %convolution_convert_fusion.4, bf16[4,4,1536,512]{3,2,1,0:T(8,128)(2,1)} %bitcast.8, bf16[1,4,512,1280]{3,2,1,0:T(8,128)(2,1)} %param.22, bf16[1,4,1280,512]{3,2,1,0:T(8,128)(2,1)} %param.23), kind=kOutput, calls=%fused_computation.43 | convolution fusion | flops 64720207872 | bytes 123731968 | tf_op jit(solution)/shard_map/slcf,lfh->slch/dot_general | solution.py:76
  1155.6 20.5 %copy.25 = bf16[4,4,1536,512]{3,2,1,0:T(8,128)(2,1)} copy(bf16[4,4,1536,512]{3,2,0,1:T(8,128)(2,1)} %convert_bitcast_fusion) | data formatting | bytes 50331648 | tf_op jit(solution)/shard_map/convert_element_type | solution.py:76
  1176.1 131.4 %all-to-all-done.4 = bf16[4,6144,512]{2,1,0:T(8,128)(2,1)} async-done(((bf16[4,6144,512]{2,1,0:T(8,128)(2,1)}), bf16[4,6144,512]{2,1,0:T(8,128)(2,1)}, u32[]{:S(2)}, u32[]{:S(2)}) %all-to-all-start.4) | async-done | bytes 25165856 | tf_op jit(solution)/shard_map/all_to_all | solution.py:33
  1316.0 61.1 %fusion.45 = f32[1,4,1280,512]{3,2,1,0:T(8,128)} fusion(bf16[4,4,1536,512]{3,2,1,0:T(8,128)(2,1)} %bitcast.32, bf16[4,4,1536,1280]{3,2,1,0:T(8,128)(2,1)} %convolution_convert_fusion.1, bf16[4,4,1536,1280]{3,2,1,0:T(8,128)(2,1)} %convolution_convert_fusion), kind=kOutput, calls=%fused_computation.78 | convolution fusion | flops 32463912960 | bytes 161480704 | tf_op jit(solution)/shard_map/slcf,slch->lfh/dot_general | solution.py:92
  1377.1 44.2 %fusion.42 = f32[1,4,512,1280]{3,2,1,0:T(8,128)} fusion(bf16[4,4,1536,512]{3,2,1,0:T(8,128)(2,1)} %bitcast.38, bf16[4,4,1536,1280]{3,2,0,1:T(8,128)(2,1)} %get-tuple-element.5), kind=kOutput, calls=%fused_computation.77 | convolution fusion | flops 32212254720 | bytes 98566144 | tf_op jit(solution)/shard_map/slch,slcf->lhf/dot_general | solution.py:96
  1421.3 45.3 %gather_fusion.5 = bf16[8192,512]{1,0:T(8,128)(2,1)} fusion(bf16[24576,512]{1,0:T(8,128)(2,1)} %bitcast.45, s32[8192]{0:T(1024)S(1)} %copy-done.11), kind=kCustom, calls=%fused_computation.5 | custom fusion | bytes 16809984 | tf_op jit(solution)/shard_map/gather | solution.py:99
  1466.6 12.6 reshape.230
  1479.1 15.3 reduce_sum.102
  1500.5 11.0 fusion.75
  1517.8 70.8 %all-to-all-done.1 = bf16[4,6144,512]{2,1,0:T(8,128)(2,1)} async-done(((bf16[4,6144,512]{2,1,0:T(8,128)(2,1)}), bf16[4,6144,512]{2,1,0:T(8,128)(2,1)}, u32[]{:S(2)}, u32[]{:S(2)}) %all-to-all-start.1) | async-done | bytes 25165856 | tf_op jit(solution)/shard_map/all_to_all | solution.py:33
  1588.6 45.3 %gather_fusion.1 = bf16[8192,512]{1,0:T(8,128)(2,1)} fusion(bf16[24576,512]{1,0:T(8,128)(2,1)} %bitcast.22, s32[8192]{0:T(1024)S(1)} %copy-done.10), kind=kCustom, calls=%fused_computation.1 | custom fusion | bytes 16809984 | tf_op jit(solution)/shard_map/gather | solution.py:78
  1633.9 12.5 reshape.226
  1658.2 44.2 %fusion.39 = f32[1,4,512,1280]{3,2,1,0:T(8,128)} fusion(bf16[4,4,1536,512]{3,2,1,0:T(8,128)(2,1)} %bitcast.38, bf16[4,4,1536,1280]{3,2,0,1:T(8,128)(2,1)} %get-tuple-element.6), kind=kOutput, calls=%fused_computation.76 | convolution fusion | flops 32212254720 | bytes 98566144 | tf_op jit(solution)/shard_map/slch,slcf->lhf/dot_general | solution.py:95
  (127 shorter events, 111.2 us)
Async XLA Ops:
  0.6 57.1 %copy-start = (bf16[1,512,1280]{2,1,0:T(8,128)(2,1)S(1)}, bf16[1,512,1280]{2,1,0:T(8,128)(2,1)}, u32[]{:S(2)}) copy-start(bf16[1,512,1280]{2,1,0:T(8,128)(2,1)} %param.19) | copy-start | bytes 3932164
  3.9 53.8 %copy-start.3 = (bf16[1,2048,512]{2,1,0:T(8,128)(2,1)S(1)}, bf16[1,2048,512]{2,1,0:T(8,128)(2,1)}, u32[]{:S(2)}) copy-start(bf16[1,2048,512]{2,1,0:T(8,128)(2,1)} %param.13) | copy-start | bytes 6291460
  6.8 54.2 %copy-start.23 = (f32[2048]{0:T(1024)}, f32[2048]{0:T(1024)S(1)}, u32[]{:S(2)}) copy-start(f32[2048]{0:T(1024)S(1)} %fusion.124) | copy-start | bytes 24580
  57.7 3.2 copy-start.27
  60.9 3.6 copy-start.28
  64.6 1.3 copy-start.1
  64.6 1.3 copy-start.21
  64.6 1.9 copy-start.19
  165.2 8.7 copy-start.13
  165.2 10.4 copy-start.26
  165.2 297.8 %all-to-all-start.3 = ((bf16[4,6144,512]{2,1,0:T(8,128)(2,1)}), bf16[4,6144,512]{2,1,0:T(8,128)(2,1)}, u32[]{:S(2)}, u32[]{:S(2)}) async-start(bf16[4,6144,512]{2,1,0:T(8,128)(2,1)} %bitcast.248), calls=%async_computation.3 | async-start | bytes 50331648 | tf_op jit(solution)/shard_map/all_to_all | solution.py:33
  173.9 10.4 copy-start.9
  184.4 151.8 %copy-start.25 = (bf16[1,2048,4]{1,2,0:T(4,128)(2,1)S(1)}, bf16[1,2048,4]{1,2,0:T(4,128)(2,1)}, u32[]{:S(2)}) copy-start(bf16[1,2048,4]{1,2,0:T(4,128)(2,1)} %param.16) | copy-start | bytes 49156
  463.0 282.0 %all-to-all-start.2 = ((bf16[4,6144,512]{2,1,0:T(8,128)(2,1)}), bf16[4,6144,512]{2,1,0:T(8,128)(2,1)}, u32[]{:S(2)}, u32[]{:S(2)}) async-start(bf16[4,6144,512]{2,1,0:T(8,128)(2,1)} %fusion.18), calls=%async_computation.2 | async-start | bytes 50331648 | tf_op jit(solution)/shard_map/all_to_all | solution.py:33
  479.8 1.3 copy-start.5
  479.8 1.9 copy-start.8
  479.9 2.5 copy-start.12
  515.5 100.0 %copy-start.15 = (s32[8192,1]{0,1:T(1,128)S(1)}, s32[8192,1]{0,1:T(1,128)}, u32[]{:S(2)}) copy-start(s32[8192,1]{0,1:T(1,128)} %copy-done.14) | copy-start | bytes 98308
  744.9 281.2 %all-to-all-start = ((bf16[4,6144,512]{2,1,0:T(8,128)(2,1)}), bf16[4,6144,512]{2,1,0:T(8,128)(2,1)}, u32[]{:S(2)}, u32[]{:S(2)}) async-start(bf16[4,6144,512]{2,1,0:T(8,128)(2,1)} %bitcast.249), calls=%async_computation | async-start | bytes 50331648 | tf_op jit(solution)/shard_map/all_to_all | solution.py:33
  1026.2 281.4 %all-to-all-start.4 = ((bf16[4,6144,512]{2,1,0:T(8,128)(2,1)}), bf16[4,6144,512]{2,1,0:T(8,128)(2,1)}, u32[]{:S(2)}, u32[]{:S(2)}) async-start(bf16[4,6144,512]{2,1,0:T(8,128)(2,1)} %bitcast.247), calls=%async_computation.4 | async-start | bytes 50331648 | tf_op jit(solution)/shard_map/all_to_all | solution.py:33
  1307.5 281.1 %all-to-all-start.1 = ((bf16[4,6144,512]{2,1,0:T(8,128)(2,1)}), bf16[4,6144,512]{2,1,0:T(8,128)(2,1)}, u32[]{:S(2)}, u32[]{:S(2)}) async-start(bf16[4,6144,512]{2,1,0:T(8,128)(2,1)} %bitcast.246), calls=%async_computation.1 | async-start | bytes 50331648 | tf_op jit(solution)/shard_map/all_to_all | solution.py:33
  1377.1 44.2 %copy-start.11 = (s32[8192]{0:T(1024)S(1)}, s32[8192]{0:T(1024)}, u32[]{:S(2)}) copy-start(s32[8192]{0:T(1024)} %broadcast_clamp_fusion) | copy-start | bytes 98308
  1479.1 15.3 copy-start.2
  1479.1 17.5 %copy-start.22 = (f32[2048]{0:T(1024)S(1)}, f32[2048]{0:T(1024)}, u32[]{:S(2)}) copy-start(f32[2048]{0:T(1024)} %copy-done.21) | copy-start | bytes 24580
  1479.1 17.5 %copy-start.20 = (f32[2048]{0:T(1024)S(1)}, f32[2048]{0:T(1024)}, u32[]{:S(2)}) copy-start(f32[2048]{0:T(1024)} %copy-done.19) | copy-start | bytes 24580
  1500.5 11.1 copy-start.18
  1500.5 11.1 copy-start.4
  1500.5 11.1 copy-start.24
  1511.6 77.1 %copy-start.10 = (s32[8192]{0:T(1024)S(1)}, s32[8192]{0:T(1024)}, u32[]{:S(2)}) copy-start(s32[8192]{0:T(1024)} %broadcast_clamp_fusion.1) | copy-start | bytes 98308
  1515.4 186.9 %collective-permute-start.1 = (bf16[2048,512]{1,0:T(8,128)(2,1)}, bf16[2048,512]{1,0:T(8,128)(2,1)S(1)}, u32[]{:S(2)}, u32[]{:S(2)}) collective-permute-start(bf16[2048,512]{1,0:T(8,128)(2,1)} %fusion.89), channel_id=1, source_target_pairs={{0,4},{4,0},{1,5},{5,1},{2,6},{6,2},{3,7},{7,3}} | collective-permute-start | bytes 6291464 | tf_op jit(solution)/shard_map/ppermute | solution.py:109
  1646.5 7.0 copy-start.6
  1655.8 47.8 %collective-permute-start = (bf16[2048,512]{1,0:T(8,128)(2,1)}, bf16[2048,512]{1,0:T(8,128)(2,1)}, u32[]{:S(2)}, u32[]{:S(2)}) collective-permute-start(bf16[2048,512]{1,0:T(8,128)(2,1)} %fusion.79), channel_id=1, source_target_pairs={{0,4},{4,0},{1,5},{5,1},{2,6},{6,2},{3,7},{7,3}} | collective-permute-start | bytes 6291464 | tf_op jit(solution)/shard_map/ppermute | solution.py:108
  (4 other events, 2.6 us)
where the time goes:
time: 1720 us; the launch traced here: 1710 us
  local copies, waits for them, and re-layouts  692 us (40%)
  matrix products  587 us (34%)
  waiting for transfers between devices  301 us (18%)
  other arithmetic  78.8 us (5%)
  starting transfers between devices  47.9 us (3%)
    all_to_all x5, waiting for transfers between devices, exchange(): return lax.all_to_all(buf, 'ep', 0, 0, tiled=True)  300 us
    gather x1, local copies, waits for them, and re-layouts, device_fn(): jnp.concatenate([gate_bwd[0].reshape(-1), jnp.zeros((1,), bf16)])[src_b]  151 us
    dot_general x1, matrix products, device_fn(): jnp.einsum('slch,lfh->slcf', d_out, stage_wd, preferred_element_type=f32)  102 us
    gather x1, local copies, waits for them, and re-layouts, device_fn(): jnp.concatenate([norm_b, zero_row])[tok_b]  98.7 us
    gather x1, local copies, waits for them, and re-layouts, device_fn(): jnp.concatenate([norm_f, zero_row])[src_f // top_k]  98.6 us
    gather x1, local copies, waits for them, and re-layouts, device_fn(): dy_rows = jnp.concatenate([bwd_dy, zero_row])[tok_b]  98.6 us
    dot_general x2, matrix products, expert_up(): jnp.einsum('slch,lhf->slcf', row_buf, stage_wg, preferred_element_type=f32)  82.8 us
    dot_general x1, matrix products, device_fn(): jnp.einsum('slcf,lfh->slch', glu_act(gate_pre_f, up_pre_f), stage_wd, pre...  79.2 us
  transfers between devices with their start and end apart: 7, of which 5 were waited for; matrix products, arithmetic and copies ran while one was open for 69% of the time, Pallas kernels for 0%

commit v1 on v0

v1 whole, which is shorter than its diff:
```python
import functools

import jax
import jax.numpy as jnp
from jax import lax
from jax.experimental import pallas as pl
from jax.experimental.pallas import tpu as pltpu
from jax.sharding import PartitionSpec as P

EPS_NORM = 1e-6
SUB = 256
PER_TILE = 2
WIN = 512
CHUNK = 256
E_RUN = 4

f32 = jnp.float32
bf16 = jnp.bfloat16
i32 = jnp.int32


def rms_norm(rows_in):
    rows_f32 = rows_in.astype(f32)
    return (rows_f32 * lax.rsqrt(jnp.mean(rows_f32 * rows_f32, axis=-1, keepdims=True) + EPS_NORM)).astype(bf16)


def dense_act(pre_act):
    return jax.nn.silu(pre_act.astype(f32)).astype(bf16)


def dot_nn(a, b):
    return lax.dot_general(a, b, (((1,), (0,)), ((), ())), preferred_element_type=f32)


def dot_nt(a, b):
    return lax.dot_general(a, b, (((1,), (1,)), ((), ())), preferred_element_type=f32)


def dot_tn(a, b):
    return lax.dot_general(a, b, (((0,), (0,)), ((), ())), preferred_element_type=f32)


def expert_kernel(bwd, carry, n_sub, *refs):
    refs = list(refs)

    def take(n):
        out = refs[:n]
        del refs[:n]
        return out

    starts, nwins, ntiles, base_ref, rank_ref, gate_ref = take(6)
    tok_in = take(2)
    dy_in = take(2) if bwd else []
    w_own = take(3)
    w_mate = take(3)
    dw_in = take(6) if carry else []
    p_out = take(2)
    dw_out = take(6) if bwd else []
    tok, acc, wg_buf, wu_buf, wd_buf, x_acc = take(6)
    if bwd:
        dyt, d_acc, xt, dt, dg_all, du_all, dwg_buf, dwu_buf, dwd_buf = take(9)
        tok_sem, w_sem, in_sem, out_sem = take(4)
    else:
        (act_all,) = take(1)
        tok_sem, w_sem = take(2)
    half = tok_in[0].shape[0]
    n_tok = 2 * half
    width = tok.shape[1]
    ff = wg_buf.shape[2]
    base = base_ref[0]

    loads = []
    for i, (src, dst) in enumerate([(tok_in, tok)] + ([(dy_in, dyt)] if bwd else [])):
        for j in range(2):
            loads.append(pltpu.make_async_copy(src[j], dst.at[pl.ds(j * half, half), :], tok_sem.at[i, j]))
    for c in loads:
        c.start()

    def w_copies(srcs, idx, slot):
        return [pltpu.make_async_copy(s.at[idx], b.at[slot], w_sem.at[slot, k])
                for k, (s, b) in enumerate(zip(srcs, (wg_buf, wu_buf, wd_buf)))]

    def w_start(e, slot):
        @pl.when(e < 2)
        def _():
            for c in w_copies(w_own, base + e, slot):
                c.start()

        @pl.when(e >= 2)
        def _():
            for c in w_copies(w_mate, base + e - 2, slot):
                c.start()

    def dw_copies(refs6, e, slot, sem, inward):
        bufs = (dwg_buf, dwu_buf, dwd_buf)

        def go(refs3, idx, what):
            for k in range(3):
                hbm, buf = refs3[k].at[idx], bufs[k].at[slot]
                c = pltpu.make_async_copy(hbm, buf, sem.at[slot, k]) if inward else pltpu.make_async_copy(buf, hbm, sem.at[slot, k])
                getattr(c, what)()

        def start():
            @pl.when(e < 2)
            def _():
                go(refs6[:3], base + e, 'start')

            @pl.when(e >= 2)
            def _():
                go(refs6[3:], e - 2, 'start')

        def wait():
            go(refs6[3:], 0, 'wait')

        return start, wait

    w_start(0, 0)
    if carry:
        dw_copies(dw_in, 0, 0, in_sem, True)[0]()
    acc[...] = jnp.zeros_like(acc)
    for c in loads:
        c.wait()

    def window(e, st, k):
        so = starts[e * n_sub + st] + k * WIN
        s = pl.multiple_of(jnp.minimum(so, n_tok - WIN), 128)
        rk = rank_ref[e, :, pl.ds(s, WIN)]
        lane = lax.broadcasted_iota(i32, (1, WIN), 1) + s
        rk = jnp.where(lane >= so, rk, -1) - st * SUB
        mask = lax.broadcasted_iota(i32, (SUB, WIN), 0) == rk
        return s, mask

    def ones(mask):
        return jnp.where(mask, 1.0, 0.0).astype(bf16)

    def gated(mask, e, s):
        return jnp.where(mask, gate_ref[e, :, pl.ds(s, WIN)], 0.0).astype(bf16)

    def expert(e, _):
        slot = lax.rem(e, 2)
        for c in w_copies(w_own, 0, slot):
            c.wait()

        @pl.when(e < E_RUN - 1)
        def _():
            w_start(e + 1, 1 - slot)

        wg, wu, wd = wg_buf.at[slot], wu_buf.at[slot], wd_buf.at[slot]
        if bwd:
            if carry:
                dw_copies(dw_in, e, slot, in_sem, True)[1]()
            else:
                for b in (dwg_buf, dwu_buf, dwd_buf):
                    b[slot] = jnp.zeros(b.shape[1:], f32)
            dwg, dwu, dwd = dwg_buf.at[slot], dwu_buf.at[slot], dwd_buf.at[slot]

        def tile(t, _):
            for h in range(PER_TILE):
                st = t * PER_TILE + h
                rows = pl.ds(h * SUB, SUB)
                s, mask = window(e, st, 0)
                x_acc[rows, :] = dot_nn(ones(mask), tok[pl.ds(s, WIN), :])
                if bwd:
                    d_acc[rows, :] = dot_nn(gated(mask, e, s), dyt[pl.ds(s, WIN), :])
            for h in range(PER_TILE):
                st = t * PER_TILE + h
                rows = pl.ds(h * SUB, SUB)

                @pl.loop(1, nwins[e * n_sub + st])
                def _(k):
                    s, mask = window(e, st, k)
                    x_acc[rows, :] += dot_nn(ones(mask), tok[pl.ds(s, WIN), :])
                    if bwd:
                        d_acc[rows, :] += dot_nn(gated(mask, e, s), dyt[pl.ds(s, WIN), :])

            x = x_acc[...].astype(bf16)
            if bwd:
                d = d_acc[...].astype(bf16)
                xt[...] = x.T
                dt[...] = d.T
            for c in range(0, ff, CHUNK):
                cols = pl.ds(c, CHUNK)
                gp = dot_nn(x, wg[:, cols]).astype(bf16).astype(f32)
                up = dot_nn(x, wu[:, cols]).astype(bf16).astype(f32)
                sig = 1.0 / (1.0 + jnp.exp(-gp))
                silu = gp * sig
                if not bwd:
                    act_all[:, cols] = (silu * up).astype(bf16)
                    continue
                da = dot_nt(d, wd[cols, :]).astype(bf16).astype(f32)
                act = (silu * up).astype(bf16)
                du = (da * silu).astype(bf16)
                dg = (da * up * (sig + silu * (1.0 - sig))).astype(bf16)
                dg_all[:, cols] = dg
                du_all[:, cols] = du
                dwd[:, cols] += dot_nn(dt[...], act)
                dwg[:, cols] += dot_nn(xt[...], dg)
                dwu[:, cols] += dot_nn(xt[...], du)
            if bwd:
                out = (dot_nt(dg_all[...], wg[...]) + dot_nt(du_all[...], wu[...])).astype(bf16)
            else:
                out = dot_nn(act_all[...], wd[...]).astype(bf16)

            def put(st, k, part):
                s, mask = window(e, st, k)
                sel = ones(mask) if bwd else gated(mask, e, s)
                acc[pl.ds(s, WIN), :] += dot_tn(sel, part)

            for h in range(PER_TILE):
                put(t * PER_TILE + h, 0, out[h * SUB:(h + 1) * SUB, :])
            x_acc[...] = out.astype(f32)
            for h in range(PER_TILE):
                st = t * PER_TILE + h

                @pl.loop(1, nwins[e * n_sub + st])
                def _(k):
                    put(st, k, x_acc[h * SUB:(h + 1) * SUB, :].astype(bf16))

            if bwd:
                @pl.when(t == 0)
                def _():
                    @pl.when(e >= 1)
                    def _():
                        dw_copies(dw_out, e - 1, 1 - slot, out_sem, False)[1]()

                    if carry:
                        @pl.when(e < E_RUN - 1)
                        def _():
                            dw_copies(dw_in, e + 1, 1 - slot, in_sem, True)[0]()
            return 0

        lax.fori_loop(0, ntiles[e], tile, 0)
        if bwd:
            dw_copies(dw_out, e, slot, out_sem, False)[0]()
        return 0

    lax.fori_loop(0, E_RUN, expert, 0)
    outs = [pltpu.make_async_copy(acc.at[pl.ds(j * half, half), :], p_out[j], tok_sem.at[0, j]) for j in range(2)]
    for c in outs:
        c.start()
    if bwd:
        dw_copies(dw_out, E_RUN - 1, (E_RUN - 1) % 2, out_sem, False)[1]()
    for c in outs:
        c.wait()


def run_experts(meta, toks, dys, w_own, w_mate, dw_prev):
    starts, nwins, ntiles, base, rank, gate = meta
    bwd = dys is not None
    carry = dw_prev is not None
    half, width = toks[0].shape
    e_loc, _, ff = w_own[0].shape
    smem = pl.BlockSpec(memory_space=pltpu.SMEM)
    vmem = pl.BlockSpec(memory_space=pltpu.VMEM)
    hbm = pl.BlockSpec(memory_space=pl.ANY)
    args = [starts, nwins, ntiles, base, rank, gate, *toks]
    if bwd:
        args += [*dys]
    args += [*w_own, *w_mate]
    if carry:
        args += [*dw_prev]
    in_specs = [smem] * 4 + [vmem] * 2 + [hbm] * (len(args) - 6)
    out_shape = [jax.ShapeDtypeStruct((half, width), f32)] * 2
    if bwd:
        shape_w = (width, ff)
        for n in (e_loc, 2):
            out_shape += [jax.ShapeDtypeStruct((n, *shape_w), f32)] * 3
    rows = SUB * PER_TILE
    scratch = [
        pltpu.VMEM((2 * half, width), bf16),
        pltpu.VMEM((2 * half, width), f32),
        pltpu.VMEM((2, width, ff), bf16),
        pltpu.VMEM((2, width, ff), bf16),
        pltpu.VMEM((2, ff, width), bf16),
        pltpu.VMEM((rows, width), f32),
    ]
    if bwd:
        scratch += [
            pltpu.VMEM((2 * half, width), bf16),
            pltpu.VMEM((rows, width), f32),
            pltpu.VMEM((width, rows), bf16),
            pltpu.VMEM((width, rows), bf16),
            pltpu.VMEM((rows, ff), bf16),
            pltpu.VMEM((rows, ff), bf16),
            pltpu.VMEM((2, width, ff), f32),
            pltpu.VMEM((2, width, ff), f32),
            pltpu.VMEM((2, width, ff), f32),
            pltpu.SemaphoreType.DMA((2, 2)),
            pltpu.SemaphoreType.DMA((2, 3)),
            pltpu.SemaphoreType.DMA((2, 3)),
            pltpu.SemaphoreType.DMA((2, 3)),
        ]
    else:
        scratch += [
            pltpu.VMEM((rows, ff), bf16),
            pltpu.SemaphoreType.DMA((2, 2)),
            pltpu.SemaphoreType.DMA((2, 3)),
        ]
    n_sub = starts.shape[0] // E_RUN
    flops = (8 if bwd else 3) * 2 * 3584 * 2 * width * ff
    return pl.pallas_call(
        functools.partial(expert_kernel, bwd, carry, n_sub),
        out_shape=out_shape,
        in_specs=in_specs,
        out_specs=[hbm] * len(out_shape),
        scratch_shapes=scratch,
        compiler_params=pltpu.CompilerParams(vmem_limit_bytes=60 * 1024 * 1024),
        cost_estimate=pl.CostEstimate(flops=flops, bytes_accessed=60_000_000, transcendentals=0),
        name='experts_bwd' if bwd else 'experts_fwd',
    )(*args)


def solution(mesh):
    n_ep = mesh.shape['ep']
    n_pp = mesh.shape['pp']
    fwd_perm = [(i, (i + 1) % n_pp) for i in range(n_pp)]
    bwd_perm = [(i, (i - 1) % n_pp) for i in range(n_pp)]

    def to_mate(v):
        return lax.ppermute(v, 'ep', [(i, i ^ 1) for i in range(n_ep)])

    def to_cross(v):
        return lax.ppermute(v, 'ep', [(i, i ^ 2) for i in range(n_ep)])

    def device_fn(x_fwd, x_bwd, dy_bwd, ids_fwd, gate_fwd, ids_bwd, gate_bwd, w_in, w_out, w_gate, w_up, w_down):
        fwd_x, bwd_x, bwd_dy = x_fwd[0], x_bwd[0], dy_bwd[0]
        stage_w_in, stage_w_out = w_in[0], w_out[0]
        w_own = (w_gate[0], w_up[0], w_down[0])
        n_tok, width = fwd_x.shape
        top_k = ids_fwd.shape[2]
        e_loc = w_own[0].shape[0]
        n_exp = e_loc * n_ep
        cap = 3 * n_tok * top_k // n_exp
        me = lax.axis_index('ep')
        core = lax.rem(me, 2)
        base = 2 * core
        n_sub = 2 * cap // SUB

        def gather_pair(v):
            far = to_cross(v)
            return (v, to_mate(v)), (far, to_mate(far))

        dy_near, dy_far = gather_pair(bwd_dy)
        w_mate = tuple(to_mate(w) for w in w_own)

        fields = [ids_fwd[0].astype(f32).T, gate_fwd[0].astype(f32).T, ids_bwd[0].astype(f32).T, gate_bwd[0].astype(f32).T]
        table = lax.all_gather(jnp.concatenate(fields), 'ep')
        table = jnp.take(table, jnp.stack([me, me ^ 1, me ^ 2, me ^ 3]), axis=0)
        mine = e_loc * me + base
        mates = e_loc * (me ^ 1) + base
        run_ids = jnp.stack([mine, mine + 1, mates, mates + 1]).astype(f32)
        base_arr = base.reshape(1).astype(i32)
        tri = jnp.triu(jnp.ones((128, 128), bf16))

        def routing(off):
            ids = table[:, off:off + top_k]
            gates = table[:, off + top_k:off + 2 * top_k]
            match = ids[None] == run_ids[:, None, None, None]
            hit = jnp.any(match, axis=2)
            gate = jnp.sum(jnp.where(match, gates[None], 0.0), axis=2)
            n2 = 2 * n_tok
            hit = hit.reshape(E_RUN, 2, n2 // 128, 128)
            within = jnp.dot(hit.astype(bf16), tri, preferred_element_type=f32)
            tot = within[..., -1]
            blk = jnp.arange(n2 // 128)
            before = jnp.sum(jnp.where(blk[:, None] < blk[None, :], tot[..., :, None], 0.0), axis=2)
            incl = (within + before[..., None]).astype(i32)
            rank = jnp.where(hit, incl - 1, -1).reshape(E_RUN, 2, n2)
            incl = incl.reshape(E_RUN, 2, n2)
            cnt = incl[..., -1]
            first = jnp.arange(n_sub, dtype=i32) * SUB
            last = jnp.minimum(first + SUB, cnt[..., None]) - 1
            start = jnp.sum((incl[:, :, None, :] <= first[None, None, :, None]).astype(i32), axis=-1)
            end = jnp.sum((incl[:, :, None, :] <= last[..., None]).astype(i32), axis=-1) + 1
            start = jnp.minimum(start, n2 - 1) // 128 * 128
            nwin = jnp.maximum((end - start + WIN - 1) // WIN, 1)
            rows = SUB * PER_TILE
            ntile = jnp.maximum((cnt + rows - 1) // rows, 1)
            gate = gate.reshape(E_RUN, 2, n2)
            return [(start[:, i].reshape(-1), nwin[:, i].reshape(-1), ntile[:, i], base_arr,
                     rank[:, i][:, None, :], gate[:, i][:, None, :]) for i in range(2)]

        def dense_fwd(x_tok):
            norm_in = rms_norm(x_tok)
            pre_act = jnp.dot(norm_in, stage_w_in, preferred_element_type=f32).astype(bf16)
            mid_res = (x_tok.astype(f32) + jnp.dot(dense_act(pre_act), stage_w_out, preferred_element_type=f32)).astype(bf16)
            return pre_act, mid_res

        def combine_far(parts):
            return to_cross(parts[0] + to_mate(parts[1]))

        _, mid_f = dense_fwd(fwd_x)
        norm_f = rms_norm(mid_f)
        near_f, far_f = gather_pair(norm_f)
        pre_b, mid_b = dense_fwd(bwd_x)
        norm_b, norm_back = jax.vjp(rms_norm, mid_b)
        near_b, far_b = gather_pair(norm_b)
        meta_near_f, meta_far_f = routing(0)
        meta_near_b, meta_far_b = routing(2 * top_k)

        pf_near = run_experts(meta_near_f, near_f, None, w_own, w_mate, None)
        pf_far = run_experts(meta_far_f, far_f, None, w_own, w_mate, None)
        ret_f = combine_far(pf_far)
        pb_far = run_experts(meta_far_b, far_b, dy_far, w_own, w_mate, None)
        ret_b = combine_far(pb_far[:2])
        pb_near = run_experts(meta_near_b, near_b, dy_near, w_own, w_mate, pb_far[2:])
        dw_full, dw_mate = pb_near[2:5], pb_near[5:8]

        y_val = (mid_f.astype(f32) + (pf_near[0] + to_mate(pf_near[1]) + ret_f)).astype(bf16)
        y_next = lax.ppermute(y_val, 'pp', fwd_perm)

        d_norm = (pb_near[0] + to_mate(pb_near[1]) + ret_b).astype(bf16)
        d_mid = bwd_dy + norm_back(d_norm)[0]
        d_hidden = jnp.einsum('th,fh->tf', d_mid, stage_w_out, preferred_element_type=f32).astype(bf16)
        _, dense_back = jax.vjp(dense_act, pre_b)
        d_pre = dense_back(d_hidden)[0]
        d_norm_in = jnp.einsum('tf,hf->th', d_pre, stage_w_in, preferred_element_type=f32).astype(bf16)
        _, norm_in_back = jax.vjp(rms_norm, bwd_x)
        dx_val = d_mid + norm_in_back(d_norm_in)[0]
        dx_prev = lax.ppermute(dx_val, 'pp', bwd_perm)

        back = [to_mate(v) for v in dw_mate]
        zero = jnp.zeros((), i32)
        dw_gate, dw_up, dw_down_t = [lax.dynamic_update_slice(full, part, (2 - base, zero, zero)) for full, part in zip(dw_full, back)]
        dw_down = jnp.swapaxes(dw_down_t, 1, 2)
        return y_next[None], dx_prev[None], dw_gate[None], dw_up[None], dw_down[None]

    spec_act = P('pp', 'ep', None)
    spec_dense = P('pp', None, None)
    spec_exp = P('pp', 'ep', None, None)
    return jax.shard_map(device_fn, mesh=mesh, in_specs=(spec_act,) * 7 + (spec_dense,) * 2 + (spec_exp,) * 3, out_specs=(spec_act, spec_act, spec_exp, spec_exp, spec_exp), check_vma=False)
```

time: 1720 us -> 769 us (0.45)
  local copies, waits for them, and re-layouts: 692 us -> 73.5 us
  matrix products: 587 us -> 27.1 us
  Pallas kernels: 0 us -> 266 us
  waiting for transfers between devices: 301 us -> 82.8 us
  starting transfers between devices: 47.9 us -> 173 us
  blocking collectives: 0 us -> 84.9 us
  other arithmetic: 78.8 us -> 52.4 us
    dot_general x11 -> x2, matrix products: 560 us -> 1.95 us  [routing(): within = jnp.dot(hit.astype(bf16), tri, preferred_element_type=f32)]
    gather x6 -> x1, local copies, waits for them, and re-layouts: 538 us -> 2.41 us  [device_fn(): table = jnp.take(table, jnp.stack([me, me ^ 1, me ^ 2, me ^ 3]), axis=0)]
    all_to_all x5 -> x0, waiting for transfers between devices: 300 us -> none  [exchange(): return lax.all_to_all(buf, 'ep', 0, 0, tiled=True)]
    pallas_call x0 -> x4, Pallas kernels: none -> 266 us  [run_experts(): pl.pallas_call(functools.partial(expert_kernel, bwd, carry, n_sub), out_s...]
    all_gather x0 -> x1, blocking collectives: none -> 84.9 us  [device_fn(): table = lax.all_gather(jnp.concatenate(fields), 'ep')]
    ppermute x0 -> x21, starting transfers between devices: none -> 82.8 us  [the longest x5 78.1 us: to_cross(): return lax.ppermute(v, 'ep', [(i, i ^ 2) for i in range(n_ep)])]
    ppermute x0 -> x21, waiting for transfers between devices: none -> 64.1 us  [the longest x5 64.1 us: to_cross(): return lax.ppermute(v, 'ep', [(i, i ^ 2) for i in range(n_ep)])]
    scatter x2 -> x0, local copies, waits for them, and re-layouts: 62.5 us -> none  [route_slots(): jnp.full((n_exp * cap,), n_route, jnp.int32).at[slot_flat]]
  transfers between devices with their start and end apart: 7 -> 23, of which waited for: 5 -> 3; matrix products, arithmetic and copies ran while one was open for 69% -> 17% of each run, Pallas kernels for 0% -> 35%
where the time goes in v1:
time: 769 us; the launch traced here: 761 us
  Pallas kernels  266 us (35%)
  starting transfers between devices  173 us (22%)
  blocking collectives  84.9 us (11%)
  waiting for transfers between devices  82.8 us (11%)
  local copies, waits for them, and re-layouts  73.5 us (10%)
  other arithmetic  52.4 us (7%)
  matrix products  27.1 us (4%)
    pallas_call x4, Pallas kernels, run_experts(): pl.pallas_call(functools.partial(expert_kernel, bwd, carry, n_sub), out_s...  266 us
    all_gather x1, blocking collectives, device_fn(): table = lax.all_gather(jnp.concatenate(fields), 'ep')  84.9 us
    ppermute x5, starting transfers between devices, to_cross(): return lax.ppermute(v, 'ep', [(i, i ^ 2) for i in range(n_ep)])  78.1 us
    ppermute x5, waiting for transfers between devices, to_cross(): return lax.ppermute(v, 'ep', [(i, i ^ 2) for i in range(n_ep)])  64.1 us
    ppermute x1, starting transfers between devices, device_fn(): y_next = lax.ppermute(y_val, 'pp', fwd_perm)  45.2 us
    ppermute x1, starting transfers between devices, device_fn(): dx_prev = lax.ppermute(dx_val, 'pp', bwd_perm)  45 us
    unnamed x59, local copies, waits for them, and re-layouts  19 us
    ppermute x1, waiting for transfers between devices, device_fn(): dx_prev = lax.ppermute(dx_val, 'pp', bwd_perm)  18.6 us
  transfers between devices with their start and end apart: 23, of which 3 were waited for; matrix products, arithmetic and copies ran while one was open for 17% of the time, Pallas kernels for 35%

profile of v1, /device:TPU:0, one launch (start us, length us, event | category | flops | bytes accessed | tf_op | source)
XLA Modules:
  0.0 761.1 jit_solution(16474908644256018566)
XLA Ops:
  2.8 8.6 %fusion.28 = (f32[2048]{0:T(1024)S(1)}, bf16[2048,512]{1,0:T(8,128)(2,1)S(1)}) fusion(bf16[1,1280,512]{2,1,0:T(8,128)(2,1)} %param.20, bf16[1,2048,512]{2,1,0:T(8,128)(2,1)} %param.12, f32[2048]{0:T(1024)S(1)} %add_rsqrt_fusion.1, bf16[1,512,1280]{2,1,0:T(8,128)(2,1)S(1)} %copy-done), kind=kOutput, calls=%fused_computation.54 | convolution fusion | flops 5396494336 | bytes 6832128 | tf_op jit(solution)/shard_map/dot_general | solution.py:386
  13.2 3.3 collective-permute-start.5
  18.7 3.2 convolution_convert_fusion.1
  22.0 3.6 fusion.33
  28.9 84.9 %all-gather = f32[64,2048]{1,0:T(8,128)} all-gather(f32[16,2048]{1,0:T(8,128)S(1)} %pad_maximum_fusion), channel_id=2, replica_groups=mesh['pp'=2,'ep'=4] {'ep'}, dimensions={0}, use_global_device_ids=true | all-gather | bytes 655360 | tf_op jit(solution)/shard_map/all_gather | solution.py:347
  113.9 2.4 gather_fusion
  118.4 2.3 compare_reduce_fusion
  137.4 3.0 convert_reduce_fusion
  142.9 2.6 fusion.59
  170.7 26.5 %collective-permute-done.14.refs_8_ = bf16[2048,512]{1,0:T(8,128)(2,1)} collective-permute-done((bf16[2048,512]{1,0:T(8,128)(2,1)}, bf16[2048,512]{1,0:T(8,128)(2,1)}, u32[]{:S(2)}, u32[]{:S(2)}) %collective-permute-start.14) | collective-permute-done | bytes 2097184 | tf_op jit(solution)/shard_map/ppermute | solution.py:323
  198.3 60.2 %experts_fwd.3 = (f32[2048,512]{1,0:T(8,128)}, f32[2048,512]{1,0:T(8,128)}) custom-call(s32[48]{0:T(128)} %reshape_squeeze.26.refs_0_, s32[48]{0:T(128)} %reshape_squeeze.27.refs_1_, s32[4]{0:T(128)} %get-tuple-element.103.refs_2_, s32[1]{0:T(128)} %bitcast.30.refs_3_, s32[4,1,4096]{2,1,0:T(1,128)} %get-tuple-element.87.refs_4_, ...), custom_call_target="tpu_custom_call" | custom-call | flops 28185722880 | bytes 60000000 | tf_op jit(solution)/shard_map/experts_fwd/pallas_call | solution.py:301
  259.1 60.1 %experts_fwd.2 = (f32[2048,512]{1,0:T(8,128)}, f32[2048,512]{1,0:T(8,128)}) custom-call(s32[48]{0:T(128)} %reshape_squeeze.24.refs_0_, s32[48]{0:T(128)} %reshape_squeeze.25.refs_1_, s32[4]{0:T(128)} %get-tuple-element.102.refs_2_, s32[1]{0:T(128)} %bitcast.30.refs_3_, s32[4,1,4096]{2,1,0:T(1,128)} %get-tuple-element.86.refs_4_, ...), custom_call_target="tpu_custom_call" | custom-call | flops 28185722880 | bytes 60000000 | tf_op jit(solution)/shard_map/experts_fwd/pallas_call | solution.py:301
  319.2 63.5 %experts_bwd.2 = (f32[2048,512]{1,0:T(8,128)}, f32[2048,512]{1,0:T(8,128)}, f32[4,512,1280]{2,1,0:T(8,128)}, f32[4,512,1280]{2,1,0:T(8,128)}, f32[4,512,1280]{2,...) custom-call(s32[48]{0:T(128)} %reshape_squeeze.30.refs_0_, ...), custom_call_target="tpu_custom_call" | custom-call | flops 75161927680 | bytes 60000000 | tf_op jit(solution)/shard_map/experts_bwd/pallas_call | solution.py:301
  383.9 6.5 add.206
  390.4 18.0 %collective-permute-start.8 = (f32[2048,512]{1,0:T(8,128)}, f32[2048,512]{1,0:T(8,128)}, u32[]{:S(2)}, u32[]{:S(2)}) collective-permute-start(f32[2048,512]{1,0:T(8,128)} %add.206), channel_id=1, source_target_pairs={{0,2},{1,3},{2,0},{3,1},{4,6},{5,7},{6,4},{7,5}} | collective-permute-start | bytes 12582920 | tf_op jit(solution)/shard_map/ppermute | solution.py:323
  408.4 81.9 %experts_bwd.3 = (f32[2048,512]{1,0:T(8,128)}, f32[2048,512]{1,0:T(8,128)}, f32[4,512,1280]{2,1,0:T(8,128)}, f32[4,512,1280]{2,1,0:T(8,128)}, f32[4,512,1280]{2,...) custom-call(s32[48]{0:T(128)} %reshape_squeeze.28.refs_0_, ...), custom_call_target="tpu_custom_call" | custom-call | flops 75161927680 | bytes 60000000 | tf_op jit(solution)/shard_map/experts_bwd/pallas_call | solution.py:301
  491.0 6.6 add.217
  497.6 55.7 %collective-permute-start.18 = (f32[2048,512]{1,0:T(8,128)}, f32[2048,512]{1,0:T(8,128)}, u32[]{:S(2)}, u32[]{:S(2)}) collective-permute-start(f32[2048,512]{1,0:T(8,128)} %add.217), channel_id=1, source_target_pairs={{0,2},{1,3},{2,0},{3,1},{4,6},{5,7},{6,4},{7,5}} | collective-permute-start | bytes 12582920 | tf_op jit(solution)/shard_map/ppermute | solution.py:323
  554.0 8.0 %fusion.30 = bf16[2048,512]{1,0:T(8,128)(2,1)} fusion(bf16[2048,512]{1,0:T(8,128)(2,1)S(1)} %copy-done.6, f32[2048,512]{1,0:T(8,128)} %collective-permute-done.8, f32[2048,512]{1,0:T(8,128)} %get-tuple-element.25, f32[2048,512]{1,0:T(8,128)} %collective-permute-done.4), kind=kLoop, calls=%fused_computation.56 | loop fusion | flops 5242880 | bytes 16777216 | tf_op jit(solution)/shard_map/convert_element_type | solution.py:409
  562.0 45.2 %collective-permute-start.9 = (bf16[2048,512]{1,0:T(8,128)(2,1)}, bf16[2048,512]{1,0:T(8,128)(2,1)}, u32[]{:S(2)}, u32[]{:S(2)}) collective-permute-start(bf16[2048,512]{1,0:T(8,128)(2,1)} %fusion.30), channel_id=1, source_target_pairs={{0,4},{4,0},{1,5},{5,1},{2,6},{6,2},{3,7},{7,3}} | collective-permute-start | bytes 6291464 | tf_op jit(solution)/shard_map/ppermute | solution.py:410
  607.2 37.6 %collective-permute-done.18 = f32[2048,512]{1,0:T(8,128)} collective-permute-done((f32[2048,512]{1,0:T(8,128)}, f32[2048,512]{1,0:T(8,128)}, u32[]{:S(2)}, u32[]{:S(2)}) %collective-permute-start.18) | collective-permute-done | bytes 4194336 | tf_op jit(solution)/shard_map/ppermute | solution.py:323
  644.8 4.6 fusion.35
  649.5 2.6 fusion.41
  652.1 9.9 %fusion.26 = (f32[2048]{0:T(1024)S(1)}, bf16[2048,512]{1,0:T(8,128)(2,1)}) fusion(bf16[1,2048,512]{2,1,0:T(8,128)(2,1)S(1)} %copy-done.4, bf16[1,512,1280]{2,1,0:T(8,128)(2,1)S(1)} %copy-done, bf16[2048,1280]{1,0:T(8,128)(2,1)} %copy-done.26, bf16[2048,512]{1,0:T(8,128)(2,1)} %fusion.41, bf16[1,1280,512]{2,1,0:T(8,128)(2,1)} %param.20), kind=kOutput, calls=%fused_computation.52 | convolution fusion | flops 5408028672 | bytes 14163968 | tf_op jit(solution)/shard_map/tf,hf->th/dot_general | solution.py:417
  662.0 3.8 fusion.40
  665.8 45.0 %collective-permute-start.19 = (bf16[2048,512]{1,0:T(8,128)(2,1)}, bf16[2048,512]{1,0:T(8,128)(2,1)S(1)}, u32[]{:S(2)}, u32[]{:S(2)}) collective-permute-start(bf16[2048,512]{1,0:T(8,128)(2,1)} %fusion.40), channel_id=1, source_target_pairs={{0,4},{4,0},{1,5},{5,1},{2,6},{6,2},{3,7},{7,3}} | collective-permute-start | bytes 6291464 | tf_op jit(solution)/shard_map/ppermute | solution.py:420
  710.8 5.2 constant_dynamic-update-slice_fusion
  716.0 11.2 %copy.48 = f32[1,4,1280,512]{3,2,1,0:T(8,128)} copy(f32[1,4,1280,512]{2,3,1,0:T(8,128)} %bitcast.162) | data formatting | bytes 20971520
  727.2 5.2 bitcast_dynamic-update-slice_fusion.1
  732.4 5.2 bitcast_dynamic-update-slice_fusion
  737.6 18.6 %collective-permute-done.19 = bf16[2048,512]{1,0:T(8,128)(2,1)S(1)} collective-permute-done((bf16[2048,512]{1,0:T(8,128)(2,1)}, bf16[2048,512]{1,0:T(8,128)(2,1)S(1)}, u32[]{:S(2)}, u32[]{:S(2)}) %collective-permute-start.19) | collective-permute-done | bytes 2097184 | tf_op jit(solution)/shard_map/ppermute | solution.py:420
  756.2 3.0 copy.64
  (168 shorter events, 61.4 us)
Async XLA Ops:
  11.4 10.5 %copy-start.5 = (bf16[2048,512]{1,0:T(8,128)(2,1)}, bf16[2048,512]{1,0:T(8,128)(2,1)S(1)}, u32[]{:S(2)}) copy-start(bf16[2048,512]{1,0:T(8,128)(2,1)S(1)} %get-tuple-element.109) | copy-start | bytes 6291460
  13.2 138.1 %collective-permute-start.5 = (bf16[2048,512]{1,0:T(8,128)(2,1)}, bf16[2048,512]{1,0:T(8,128)(2,1)}, u32[]{:S(2)}, u32[]{:S(2)}) collective-permute-start(bf16[2048,512]{1,0:T(8,128)(2,1)} %fusion.29.refs_6_), channel_id=1, source_target_pairs={{0,2},{1,3},{2,0},{3,1},{4,6},{5,7},{6,4},{7,5}} | collective-permute-start | bytes 6291464 | tf_op jit(solution)/shard_map/ppermute | solution.py:323
  16.5 181.2 %collective-permute-start.1 = (bf16[4,512,1280]{2,1,0:T(8,128)(2,1)}, bf16[4,512,1280]{2,1,0:T(8,128)(2,1)}, u32[]{:S(2)}, u32[]{:S(2)}) collective-permute-start(bf16[4,512,1280]{2,1,0:T(8,128)(2,1)} %bitcast.172), channel_id=1, source_target_pairs={{0,1},{1,0},{2,3},{3,2},{4,5},{5,4},{6,7},{7,6}} | collective-permute-start | bytes 15728648 | tf_op jit(solution)/shard_map/ppermute | solution.py:320
  16.5 181.3 %collective-permute-start.2 = (bf16[4,512,1280]{2,1,0:T(8,128)(2,1)}, bf16[4,512,1280]{2,1,0:T(8,128)(2,1)}, u32[]{:S(2)}, u32[]{:S(2)}) collective-permute-start(bf16[4,512,1280]{2,1,0:T(8,128)(2,1)} %bitcast.177), channel_id=1, source_target_pairs={{0,1},{1,0},{2,3},{3,2},{4,5},{5,4},{6,7},{7,6}} | collective-permute-start | bytes 15728648 | tf_op jit(solution)/shard_map/ppermute | solution.py:320
  17.0 181.2 %collective-permute-start.3 = (bf16[4,1280,512]{2,1,0:T(8,128)(2,1)}, bf16[4,1280,512]{2,1,0:T(8,128)(2,1)}, u32[]{:S(2)}, u32[]{:S(2)}) collective-permute-start(bf16[4,1280,512]{2,1,0:T(8,128)(2,1)} %bitcast.182), channel_id=1, source_target_pairs={{0,1},{1,0},{2,3},{3,2},{4,5},{5,4},{6,7},{7,6}} | collective-permute-start | bytes 15728648 | tf_op jit(solution)/shard_map/ppermute | solution.py:320
  27.4 169.9 %copy-start.8 = (bf16[2048,512]{1,0:T(8,128)(2,1)}, bf16[2048,512]{1,0:T(8,128)(2,1)S(1)}, u32[]{:S(2)}) copy-start(bf16[2048,512]{1,0:T(8,128)(2,1)S(1)} %fusion.34.refs_6_) | copy-start | bytes 6291460
  27.4 124.2 %collective-permute-start.12 = (bf16[2048,512]{1,0:T(8,128)(2,1)S(1)}, bf16[2048,512]{1,0:T(8,128)(2,1)}, u32[]{:S(2)}, u32[]{:S(2)}) collective-permute-start(bf16[2048,512]{1,0:T(8,128)(2,1)S(1)} %fusion.34.refs_6_), channel_id=1, source_target_pairs={{0,2},{1,3},{2,0},{3,1},{4,6},{5,7},{6,4},{7,5}} | collective-permute-start | bytes 6291464 | tf_op jit(solution)/shard_map/ppermute | solution.py:323
  118.3 5.7 copy-start.11
  118.4 8.0 %copy-start.24 = (f32[4]{0:T(128)}, f32[4]{0:T(128)S(1)}, u32[]{:S(2)}) copy-start(f32[4]{0:T(128)S(1)} %add_convert_fusion.3) | copy-start | bytes 52
  151.3 46.0 %collective-permute-start.14 = (bf16[2048,512]{1,0:T(8,128)(2,1)}, bf16[2048,512]{1,0:T(8,128)(2,1)}, u32[]{:S(2)}, u32[]{:S(2)}) collective-permute-start(bf16[2048,512]{1,0:T(8,128)(2,1)} %bitcast.165), channel_id=1, source_target_pairs={{0,2},{1,3},{2,0},{3,1},{4,6},{5,7},{6,4},{7,5}} | collective-permute-start | bytes 6291464 | tf_op jit(solution)/shard_map/ppermute | solution.py:323
  151.6 45.7 %collective-permute-start.6 = (bf16[2048,512]{1,0:T(8,128)(2,1)}, bf16[2048,512]{1,0:T(8,128)(2,1)}, u32[]{:S(2)}, u32[]{:S(2)}) collective-permute-start(bf16[2048,512]{1,0:T(8,128)(2,1)} %collective-permute-done.5.refs_6_), channel_id=1, source_target_pairs={{0,1},{1,0},{2,3},{3,2},{4,5},{5,4},{6,7},{7,6}} | collective-permute-start | bytes 6291464 | tf_op jit(solution)/shard_map/ppermute | solution.py:320
  197.2 61.3 %collective-permute-start = (bf16[2048,512]{1,0:T(8,128)(2,1)}, bf16[2048,512]{1,0:T(8,128)(2,1)}, u32[]{:S(2)}, u32[]{:S(2)}) collective-permute-start(bf16[2048,512]{1,0:T(8,128)(2,1)} %fusion.29.refs_6_), channel_id=1, source_target_pairs={{0,1},{1,0},{2,3},{3,2},{4,5},{5,4},{6,7},{7,6}} | collective-permute-start | bytes 6291464 | tf_op jit(solution)/shard_map/ppermute | solution.py:320
  197.2 211.2 %collective-permute-start.10 = (bf16[2048,512]{1,0:T(8,128)(2,1)S(1)}, bf16[2048,512]{1,0:T(8,128)(2,1)}, u32[]{:S(2)}, u32[]{:S(2)}) collective-permute-start(bf16[2048,512]{1,0:T(8,128)(2,1)S(1)} %fusion.34.refs_6_), channel_id=1, source_target_pairs={{0,1},{1,0},{2,3},{3,2},{4,5},{5,4},{6,7},{7,6}} | collective-permute-start | bytes 6291464 | tf_op jit(solution)/shard_map/ppermute | solution.py:320
  197.8 210.6 %collective-permute-start.11 = (bf16[2048,512]{1,0:T(8,128)(2,1)}, bf16[2048,512]{1,0:T(8,128)(2,1)}, u32[]{:S(2)}, u32[]{:S(2)}) collective-permute-start(bf16[2048,512]{1,0:T(8,128)(2,1)} %bitcast.166), channel_id=1, source_target_pairs={{0,1},{1,0},{2,3},{3,2},{4,5},{5,4},{6,7},{7,6}} | collective-permute-start | bytes 6291464 | tf_op jit(solution)/shard_map/ppermute | solution.py:320
  197.8 121.4 %collective-permute-start.13 = (bf16[2048,512]{1,0:T(8,128)(2,1)}, bf16[2048,512]{1,0:T(8,128)(2,1)}, u32[]{:S(2)}, u32[]{:S(2)}) collective-permute-start(bf16[2048,512]{1,0:T(8,128)(2,1)} %collective-permute-done.12.refs_6_), channel_id=1, source_target_pairs={{0,1},{1,0},{2,3},{3,2},{4,5},{5,4},{6,7},{7,6}} | collective-permute-start | bytes 6291464 | tf_op jit(solution)/shard_map/ppermute | solution.py:320
  198.3 121.0 %collective-permute-start.15 = (bf16[2048,512]{1,0:T(8,128)(2,1)}, bf16[2048,512]{1,0:T(8,128)(2,1)}, u32[]{:S(2)}, u32[]{:S(2)}) collective-permute-start(bf16[2048,512]{1,0:T(8,128)(2,1)} %collective-permute-done.14.refs_8_), channel_id=1, source_target_pairs={{0,1},{1,0},{2,3},{3,2},{4,5},{5,4},{6,7},{7,6}} | collective-permute-start | bytes 6291464 | tf_op jit(solution)/shard_map/ppermute | solution.py:320
  258.6 125.3 %collective-permute-start.7 = (f32[2048,512]{1,0:T(8,128)}, f32[2048,512]{1,0:T(8,128)}, u32[]{:S(2)}, u32[]{:S(2)}) collective-permute-start(f32[2048,512]{1,0:T(8,128)} %get-tuple-element.28), channel_id=1, source_target_pairs={{0,1},{1,0},{2,3},{3,2},{4,5},{5,4},{6,7},{7,6}} | collective-permute-start | bytes 12582920 | tf_op jit(solution)/shard_map/ppermute | solution.py:320
  319.2 234.3 %collective-permute-start.4 = (f32[2048,512]{1,0:T(8,128)}, f32[2048,512]{1,0:T(8,128)}, u32[]{:S(2)}, u32[]{:S(2)}) collective-permute-start(f32[2048,512]{1,0:T(8,128)} %get-tuple-element.26), channel_id=1, source_target_pairs={{0,1},{1,0},{2,3},{3,2},{4,5},{5,4},{6,7},{7,6}} | collective-permute-start | bytes 12582920 | tf_op jit(solution)/shard_map/ppermute | solution.py:320
  382.7 108.3 %collective-permute-start.17 = (f32[2048,512]{1,0:T(8,128)}, f32[2048,512]{1,0:T(8,128)}, u32[]{:S(2)}, u32[]{:S(2)}) collective-permute-start(f32[2048,512]{1,0:T(8,128)} %get-tuple-element.38), channel_id=1, source_target_pairs={{0,1},{1,0},{2,3},{3,2},{4,5},{5,4},{6,7},{7,6}} | collective-permute-start | bytes 12582920 | tf_op jit(solution)/shard_map/ppermute | solution.py:320
  390.4 163.4 %collective-permute-start.8 = (f32[2048,512]{1,0:T(8,128)}, f32[2048,512]{1,0:T(8,128)}, u32[]{:S(2)}, u32[]{:S(2)}) collective-permute-start(f32[2048,512]{1,0:T(8,128)} %add.206), channel_id=1, source_target_pairs={{0,2},{1,3},{2,0},{3,1},{4,6},{5,7},{6,4},{7,5}} | collective-permute-start | bytes 12582920 | tf_op jit(solution)/shard_map/ppermute | solution.py:323
  490.3 71.6 %collective-permute-start.16 = (f32[2048,512]{1,0:T(8,128)}, f32[2048,512]{1,0:T(8,128)}, u32[]{:S(2)}, u32[]{:S(2)}) collective-permute-start(f32[2048,512]{1,0:T(8,128)} %get-tuple-element.36), channel_id=1, source_target_pairs={{0,1},{1,0},{2,3},{3,2},{4,5},{5,4},{6,7},{7,6}} | collective-permute-start | bytes 12582920 | tf_op jit(solution)/shard_map/ppermute | solution.py:320
  491.0 63.0 %copy-start.6 = (bf16[2048,512]{1,0:T(8,128)(2,1)S(1)}, bf16[2048,512]{1,0:T(8,128)(2,1)}, u32[]{:S(2)}) copy-start(bf16[2048,512]{1,0:T(8,128)(2,1)} %copy-done.5) | copy-start | bytes 6291460
  497.6 147.2 %collective-permute-start.18 = (f32[2048,512]{1,0:T(8,128)}, f32[2048,512]{1,0:T(8,128)}, u32[]{:S(2)}, u32[]{:S(2)}) collective-permute-start(f32[2048,512]{1,0:T(8,128)} %add.217), channel_id=1, source_target_pairs={{0,2},{1,3},{2,0},{3,1},{4,6},{5,7},{6,4},{7,5}} | collective-permute-start | bytes 12582920 | tf_op jit(solution)/shard_map/ppermute | solution.py:323
  553.3 173.9 %collective-permute-start.20 = (f32[2,512,1280]{2,1,0:T(8,128)}, f32[2,512,1280]{2,1,0:T(8,128)}, u32[]{:S(2)}, u32[]{:S(2)}) collective-permute-start(f32[2,512,1280]{2,1,0:T(8,128)} %get-tuple-element.40), channel_id=1, source_target_pairs={{0,1},{1,0},{2,3},{3,2},{4,5},{5,4},{6,7},{7,6}} | collective-permute-start | bytes 15728648 | tf_op jit(solution)/shard_map/ppermute | solution.py:320
  553.5 178.9 %collective-permute-start.21 = (f32[2,512,1280]{2,1,0:T(8,128)}, f32[2,512,1280]{2,1,0:T(8,128)}, u32[]{:S(2)}, u32[]{:S(2)}) collective-permute-start(f32[2,512,1280]{2,1,0:T(8,128)} %get-tuple-element.42), channel_id=1, source_target_pairs={{0,1},{1,0},{2,3},{3,2},{4,5},{5,4},{6,7},{7,6}} | collective-permute-start | bytes 15728648 | tf_op jit(solution)/shard_map/ppermute | solution.py:320
  553.8 157.0 %collective-permute-start.22 = (f32[2,512,1280]{2,1,0:T(8,128)}, f32[2,512,1280]{2,1,0:T(8,128)}, u32[]{:S(2)}, u32[]{:S(2)}) collective-permute-start(f32[2,512,1280]{2,1,0:T(8,128)} %get-tuple-element.44), channel_id=1, source_target_pairs={{0,1},{1,0},{2,3},{3,2},{4,5},{5,4},{6,7},{7,6}} | collective-permute-start | bytes 15728648 | tf_op jit(solution)/shard_map/ppermute | solution.py:320
  554.0 90.8 %copy-start.2 = (bf16[2048,512]{1,0:T(8,128)(2,1)S(1)}, bf16[2048,512]{1,0:T(8,128)(2,1)}, u32[]{:S(2)}) copy-start(bf16[2048,512]{1,0:T(8,128)(2,1)} %copy-done.1) | copy-start | bytes 6291460
  554.0 90.8 %copy-start.7 = (f32[2048,512]{1,0:T(8,128)S(1)}, f32[2048,512]{1,0:T(8,128)}, u32[]{:S(2)}) copy-start(f32[2048,512]{1,0:T(8,128)} %get-tuple-element.35) | copy-start | bytes 12582916
  562.0 175.6 %collective-permute-start.9 = (bf16[2048,512]{1,0:T(8,128)(2,1)}, bf16[2048,512]{1,0:T(8,128)(2,1)}, u32[]{:S(2)}, u32[]{:S(2)}) collective-permute-start(bf16[2048,512]{1,0:T(8,128)(2,1)} %fusion.30), channel_id=1, source_target_pairs={{0,4},{4,0},{1,5},{5,1},{2,6},{6,2},{3,7},{7,3}} | collective-permute-start | bytes 6291464 | tf_op jit(solution)/shard_map/ppermute | solution.py:410
  652.1 9.9 %copy-start.13 = (f32[2048]{0:T(1024)S(1)}, f32[2048]{0:T(1024)}, u32[]{:S(2)}) copy-start(f32[2048]{0:T(1024)} %copy-done.12) | copy-start | bytes 24580
  652.1 9.9 %copy-start.21 = (f32[2048]{0:T(1024)S(1)}, f32[2048]{0:T(1024)}, u32[]{:S(2)}) copy-start(f32[2048]{0:T(1024)} %copy-done.20) | copy-start | bytes 24580
  665.8 90.4 %collective-permute-start.19 = (bf16[2048,512]{1,0:T(8,128)(2,1)}, bf16[2048,512]{1,0:T(8,128)(2,1)S(1)}, u32[]{:S(2)}, u32[]{:S(2)}) collective-permute-start(bf16[2048,512]{1,0:T(8,128)(2,1)} %fusion.40), channel_id=1, source_target_pairs={{0,4},{4,0},{1,5},{5,1},{2,6},{6,2},{3,7},{7,3}} | collective-permute-start | bytes 6291464 | tf_op jit(solution)/shard_map/ppermute | solution.py:420
  (18 other events, 53.5 us)

commit v2 on v1

--- a/solution.py
+++ b/solution.py
@@ -7,10 +7,12 @@
 from jax.experimental.pallas import tpu as pltpu
 from jax.sharding import PartitionSpec as P
 
+
 EPS_NORM = 1e-6
 SUB = 256
 PER_TILE = 2
 WIN = 512
+WIN_MORE = 1024
 CHUNK = 256
 E_RUN = 4
 
@@ -40,7 +42,7 @@
     return lax.dot_general(a, b, (((0,), (0,)), ((), ())), preferred_element_type=f32)
 
 
-def expert_kernel(bwd, carry, n_sub, *refs):
+def expert_kernel(bwd, carry, row0, *refs):
     refs = list(refs)
 
     def take(n):
@@ -58,14 +60,13 @@
     dw_out = take(6) if bwd else []
     tok, acc, wg_buf, wu_buf, wd_buf, x_acc = take(6)
     if bwd:
-        dyt, d_acc, xt, dt, dg_all, du_all, dwg_buf, dwu_buf, dwd_buf = take(9)
+        dyt, d_acc, xt, dg_all, du_all, dwg_buf, dwu_buf, dwd_buf = take(8)
         tok_sem, w_sem, in_sem, out_sem = take(4)
     else:
         (act_all,) = take(1)
         tok_sem, w_sem = take(2)
     half = tok_in[0].shape[0]
     n_tok = 2 * half
-    width = tok.shape[1]
     ff = wg_buf.shape[2]
     base = base_ref[0]
 
@@ -122,19 +123,22 @@
         c.wait()
 
     def window(e, st, k):
-        so = starts[e * n_sub + st] + k * WIN
-        s = pl.multiple_of(jnp.minimum(so, n_tok - WIN), 128)
-        rk = rank_ref[e, :, pl.ds(s, WIN)]
-        lane = lax.broadcasted_iota(i32, (1, WIN), 1) + s
+        size = WIN_MORE if k is not None else WIN
+        so = starts[row0 + e, st]
+        if k is not None:
+            so += WIN + (k - 1) * WIN_MORE
+        s = pl.multiple_of(jnp.minimum(so, n_tok - size), 128)
+        rk = rank_ref[pl.ds(row0 + e, 1), pl.ds(s, size)]
+        lane = lax.broadcasted_iota(i32, (1, size), 1) + s
         rk = jnp.where(lane >= so, rk, -1) - st * SUB
-        mask = lax.broadcasted_iota(i32, (SUB, WIN), 0) == rk
-        return s, mask
+        mask = lax.broadcasted_iota(i32, (SUB, size), 0) == rk
+        return pl.ds(s, size), mask
 
     def ones(mask):
         return jnp.where(mask, 1.0, 0.0).astype(bf16)
 
-    def gated(mask, e, s):
-        return jnp.where(mask, gate_ref[e, :, pl.ds(s, WIN)], 0.0).astype(bf16)
+    def gated(mask, e, win):
+        return jnp.where(mask, gate_ref[pl.ds(row0 + e, 1), win], 0.0).astype(bf16)
 
     def expert(e, _):
         slot = lax.rem(e, 2)
@@ -158,26 +162,25 @@
             for h in range(PER_TILE):
                 st = t * PER_TILE + h
                 rows = pl.ds(h * SUB, SUB)
-                s, mask = window(e, st, 0)
-                x_acc[rows, :] = dot_nn(ones(mask), tok[pl.ds(s, WIN), :])
+                win, mask = window(e, st, None)
+                x_acc[rows, :] = dot_nn(ones(mask), tok[win, :])
                 if bwd:
-                    d_acc[rows, :] = dot_nn(gated(mask, e, s), dyt[pl.ds(s, WIN), :])
+                    d_acc[rows, :] = dot_nn(gated(mask, e, win), dyt[win, :])
             for h in range(PER_TILE):
                 st = t * PER_TILE + h
                 rows = pl.ds(h * SUB, SUB)
 
-                @pl.loop(1, nwins[e * n_sub + st])
+                @pl.loop(1, nwins[row0 + e, st])
                 def _(k):
-                    s, mask = window(e, st, k)
-                    x_acc[rows, :] += dot_nn(ones(mask), tok[pl.ds(s, WIN), :])
+                    win, mask = window(e, st, k)
+                    x_acc[rows, :] += dot_nn(ones(mask), tok[win, :])
                     if bwd:
-                        d_acc[rows, :] += dot_nn(gated(mask, e, s), dyt[pl.ds(s, WIN), :])
+                        d_acc[rows, :] += dot_nn(gated(mask, e, win), dyt[win, :])
 
             x = x_acc[...].astype(bf16)
             if bwd:
                 d = d_acc[...].astype(bf16)
                 xt[...] = x.T
-                dt[...] = d.T
             for c in range(0, ff, CHUNK):
                 cols = pl.ds(c, CHUNK)
                 gp = dot_nn(x, wg[:, cols]).astype(bf16).astype(f32)
@@ -193,7 +196,7 @@
                 dg = (da * up * (sig + silu * (1.0 - sig))).astype(bf16)
                 dg_all[:, cols] = dg
                 du_all[:, cols] = du
-                dwd[:, cols] += dot_nn(dt[...], act)
+                dwd[cols, :] += dot_tn(act, d)
                 dwg[:, cols] += dot_nn(xt[...], dg)
                 dwu[:, cols] += dot_nn(xt[...], du)
             if bwd:
@@ -202,17 +205,17 @@
                 out = dot_nn(act_all[...], wd[...]).astype(bf16)
 
             def put(st, k, part):
-                s, mask = window(e, st, k)
-                sel = ones(mask) if bwd else gated(mask, e, s)
-                acc[pl.ds(s, WIN), :] += dot_tn(sel, part)
+                win, mask = window(e, st, k)
+                sel = ones(mask) if bwd else gated(mask, e, win)
+                acc[win, :] += dot_tn(sel, part)
 
             for h in range(PER_TILE):
-                put(t * PER_TILE + h, 0, out[h * SUB:(h + 1) * SUB, :])
+                put(t * PER_TILE + h, None, out[h * SUB:(h + 1) * SUB, :])
             x_acc[...] = out.astype(f32)
             for h in range(PER_TILE):
                 st = t * PER_TILE + h
 
-                @pl.loop(1, nwins[e * n_sub + st])
+                @pl.loop(1, nwins[row0 + e, st])
                 def _(k):
                     put(st, k, x_acc[h * SUB:(h + 1) * SUB, :].astype(bf16))
 
@@ -229,7 +232,7 @@
                             dw_copies(dw_in, e + 1, 1 - slot, in_sem, True)[0]()
             return 0
 
-        lax.fori_loop(0, ntiles[e], tile, 0)
+        lax.fori_loop(0, ntiles[row0 + e, 0], tile, 0)
         if bwd:
             dw_copies(dw_out, e, slot, out_sem, False)[0]()
         return 0
@@ -244,7 +247,77 @@
         c.wait()
 
 
-def run_experts(meta, toks, dys, w_own, w_mate, dw_prev):
+def routing_kernel(n_sub, who_ref, tab_ref, rank_ref, gate_ref, start_ref, nwin_ref, ntile_ref, hit_ref):
+    _, fields, n_tok = tab_ref.shape
+    top_k = fields // 4
+    n2 = 2 * n_tok
+    n_blk = n2 // 128
+    r_i = lax.broadcasted_iota(i32, (128, 128), 0)
+    c_i = lax.broadcasted_iota(i32, (128, 128), 1)
+    tri = jnp.where(r_i <= c_i, 1.0, 0.0).astype(bf16)
+    full = jnp.ones((128, 128), bf16)
+    lane = lax.broadcasted_iota(i32, (2 * E_RUN, 128), 1)
+    for mb in range(2):
+        for q in range(4):
+            part = tab_ref[who_ref[q], pl.ds(mb * 2 * top_k, 2 * top_k), :]
+            ids, gates = part[:top_k], part[top_k:]
+            cols = pl.ds((q % 2) * n_tok, n_tok)
+            for e in range(E_RUN):
+                match = ids == who_ref[4 + e].astype(f32)
+                row = (q // 2) * E_RUN + e
+                hit_ref[row:row + 1, cols] = jnp.sum(jnp.where(match, 1.0, 0.0), axis=0, keepdims=True)
+                gate_ref[mb, row:row + 1, cols] = jnp.sum(jnp.where(match, gates, 0.0), axis=0, keepdims=True)
+        hits = [hit_ref[:, b * 128:(b + 1) * 128] for b in range(n_blk)]
+        stacked = jnp.concatenate(hits, axis=0).astype(bf16)
+        within = dot_nn(stacked, tri)
+        totals = dot_nn(stacked, full)
+        carry = jnp.zeros((2 * E_RUN, 128), f32)
+        incl = []
+        for b in range(n_blk):
+            rows = slice(b * 2 * E_RUN, (b + 1) * 2 * E_RUN)
+            v = (within[rows] + carry).astype(i32)
+            rank_ref[mb, :, b * 128:(b + 1) * 128] = jnp.where(hits[b] > 0.5, v - 1, -1)
+            incl.append(v)
+            carry = carry + totals[rows]
+        cnt = carry.astype(i32)
+
+        def tokens_upto(limit):
+            tot = jnp.zeros((2 * E_RUN, 128), f32)
+            for v in incl:
+                tot = tot + jnp.where(v <= limit, 1.0, 0.0)
+            return jnp.sum(tot, axis=1, keepdims=True).astype(i32)
+
+        start = jnp.zeros((2 * E_RUN, 128), i32)
+        nwin = jnp.ones((2 * E_RUN, 128), i32)
+        for j in range(n_sub):
+            lo = jnp.minimum(tokens_upto(j * SUB), n2 - 1) // 128 * 128
+            hi = tokens_upto(jnp.minimum((j + 1) * SUB, cnt) - 1) + 1
+            n = jnp.maximum((hi - lo - WIN + WIN_MORE - 1) // WIN_MORE, 0) + 1
+            start = jnp.where(lane == j, lo, start)
+            nwin = jnp.where(lane == j, n, nwin)
+        start_ref[mb] = start
+        nwin_ref[mb] = nwin
+        tile_rows = SUB * PER_TILE
+        ntile_ref[mb] = jnp.maximum((cnt + tile_rows - 1) // tile_rows, 1)
+
+
+def run_routing(who, table, n_sub):
+    _, _, n_tok = table.shape
+    rows = 2 * E_RUN
+    wide = (2, rows, 2 * n_tok)
+    small = jax.ShapeDtypeStruct((2, rows, 128), i32)
+    vmem = pl.BlockSpec(memory_space=pltpu.VMEM)
+    return pl.pallas_call(
+        functools.partial(routing_kernel, n_sub),
+        out_shape=[jax.ShapeDtypeStruct(wide, i32), jax.ShapeDtypeStruct(wide, f32), small, small, small],
+        in_specs=[pl.BlockSpec(memory_space=pltpu.SMEM), vmem],
+        out_specs=[vmem] * 5,
+        scratch_shapes=[pltpu.VMEM((rows, 2 * n_tok), f32)],
+        name='routing',
+    )(who, table)
+
+
+def run_experts(meta, far, toks, dys, w_own, w_mate, dw_prev):
     starts, nwins, ntiles, base, rank, gate = meta
     bwd = dys is not None
     carry = dw_prev is not None
@@ -262,9 +335,8 @@
     in_specs = [smem] * 4 + [vmem] * 2 + [hbm] * (len(args) - 6)
     out_shape = [jax.ShapeDtypeStruct((half, width), f32)] * 2
     if bwd:
-        shape_w = (width, ff)
         for n in (e_loc, 2):
-            out_shape += [jax.ShapeDtypeStruct((n, *shape_w), f32)] * 3
+            out_shape += [jax.ShapeDtypeStruct((n, *w.shape[1:]), f32) for w in w_own]
     rows = SUB * PER_TILE
     scratch = [
         pltpu.VMEM((2 * half, width), bf16),
@@ -279,12 +351,11 @@
             pltpu.VMEM((2 * half, width), bf16),
             pltpu.VMEM((rows, width), f32),
             pltpu.VMEM((width, rows), bf16),
-            pltpu.VMEM((width, rows), bf16),
             pltpu.VMEM((rows, ff), bf16),
             pltpu.VMEM((rows, ff), bf16),
             pltpu.VMEM((2, width, ff), f32),
             pltpu.VMEM((2, width, ff), f32),
-            pltpu.VMEM((2, width, ff), f32),
+            pltpu.VMEM((2, ff, width), f32),
             pltpu.SemaphoreType.DMA((2, 2)),
             pltpu.SemaphoreType.DMA((2, 3)),
             pltpu.SemaphoreType.DMA((2, 3)),
@@ -296,10 +367,9 @@
             pltpu.SemaphoreType.DMA((2, 2)),
             pltpu.SemaphoreType.DMA((2, 3)),
         ]
-    n_sub = starts.shape[0] // E_RUN
     flops = (8 if bwd else 3) * 2 * 3584 * 2 * width * ff
     return pl.pallas_call(
-        functools.partial(expert_kernel, bwd, carry, n_sub),
+        functools.partial(expert_kernel, bwd, carry, E_RUN if far else 0),
         out_shape=out_shape,
         in_specs=in_specs,
         out_specs=[hbm] * len(out_shape),
@@ -326,7 +396,7 @@
         fwd_x, bwd_x, bwd_dy = x_fwd[0], x_bwd[0], dy_bwd[0]
         stage_w_in, stage_w_out = w_in[0], w_out[0]
         w_own = (w_gate[0], w_up[0], w_down[0])
-        n_tok, width = fwd_x.shape
+        n_tok, _ = fwd_x.shape
         top_k = ids_fwd.shape[2]
         e_loc = w_own[0].shape[0]
         n_exp = e_loc * n_ep
@@ -340,45 +410,19 @@
             far = to_cross(v)
             return (v, to_mate(v)), (far, to_mate(far))
 
-        dy_near, dy_far = gather_pair(bwd_dy)
-        w_mate = tuple(to_mate(w) for w in w_own)
-
         fields = [ids_fwd[0].astype(f32).T, gate_fwd[0].astype(f32).T, ids_bwd[0].astype(f32).T, gate_bwd[0].astype(f32).T]
         table = lax.all_gather(jnp.concatenate(fields), 'ep')
-        table = jnp.take(table, jnp.stack([me, me ^ 1, me ^ 2, me ^ 3]), axis=0)
         mine = e_loc * me + base
         mates = e_loc * (me ^ 1) + base
-        run_ids = jnp.stack([mine, mine + 1, mates, mates + 1]).astype(f32)
+        who = jnp.stack([me, me ^ 1, me ^ 2, me ^ 3, mine, mine + 1, mates, mates + 1]).astype(i32)
         base_arr = base.reshape(1).astype(i32)
-        tri = jnp.triu(jnp.ones((128, 128), bf16))
-
-        def routing(off):
-            ids = table[:, off:off + top_k]
-            gates = table[:, off + top_k:off + 2 * top_k]
-            match = ids[None] == run_ids[:, None, None, None]
-            hit = jnp.any(match, axis=2)
-            gate = jnp.sum(jnp.where(match, gates[None], 0.0), axis=2)
-            n2 = 2 * n_tok
-            hit = hit.reshape(E_RUN, 2, n2 // 128, 128)
-            within = jnp.dot(hit.astype(bf16), tri, preferred_element_type=f32)
-            tot = within[..., -1]
-            blk = jnp.arange(n2 // 128)
-            before = jnp.sum(jnp.where(blk[:, None] < blk[None, :], tot[..., :, None], 0.0), axis=2)
-            incl = (within + before[..., None]).astype(i32)
-            rank = jnp.where(hit, incl - 1, -1).reshape(E_RUN, 2, n2)
-            incl = incl.reshape(E_RUN, 2, n2)
-            cnt = incl[..., -1]
-            first = jnp.arange(n_sub, dtype=i32) * SUB
-            last = jnp.minimum(first + SUB, cnt[..., None]) - 1
-            start = jnp.sum((incl[:, :, None, :] <= first[None, None, :, None]).astype(i32), axis=-1)
-            end = jnp.sum((incl[:, :, None, :] <= last[..., None]).astype(i32), axis=-1) + 1
-            start = jnp.minimum(start, n2 - 1) // 128 * 128
-            nwin = jnp.maximum((end - start + WIN - 1) // WIN, 1)
-            rows = SUB * PER_TILE
-            ntile = jnp.maximum((cnt + rows - 1) // rows, 1)
-            gate = gate.reshape(E_RUN, 2, n2)
-            return [(start[:, i].reshape(-1), nwin[:, i].reshape(-1), ntile[:, i], base_arr,
-                     rank[:, i][:, None, :], gate[:, i][:, None, :]) for i in range(2)]
+        ranks, gates, starts, nwins, ntiles = run_routing(who, table, n_sub)
+        meta_f, meta_b = [(starts[m], nwins[m], ntiles[m], base_arr, ranks[m], gates[m]) for m in range(2)]
+
+        dy_send, w_send = lax.optimization_barrier((bwd_dy, w_own, table))[:2]
+        far_dy = to_cross(dy_send)
+        dy_near, dy_far = (bwd_dy, to_mate(dy_send)), (far_dy, to_mate(far_dy))
+        w_mate = tuple(to_mate(w) for w in w_send)
 
         def dense_fwd(x_tok):
             norm_in = rms_norm(x_tok)
@@ -386,8 +430,8 @@
             mid_res = (x_tok.astype(f32) + jnp.dot(dense_act(pre_act), stage_w_out, preferred_element_type=f32)).astype(bf16)
             return pre_act, mid_res
 
-        def combine_far(parts):
-            return to_cross(parts[0] + to_mate(parts[1]))
+        def combine(parts):
+            return parts[0] + to_mate(parts[1])
 
         _, mid_f = dense_fwd(fwd_x)
         norm_f = rms_norm(mid_f)
@@ -395,21 +439,19 @@
         pre_b, mid_b = dense_fwd(bwd_x)
         norm_b, norm_back = jax.vjp(rms_norm, mid_b)
         near_b, far_b = gather_pair(norm_b)
-        meta_near_f, meta_far_f = routing(0)
-        meta_near_b, meta_far_b = routing(2 * top_k)
-
-        pf_near = run_experts(meta_near_f, near_f, None, w_own, w_mate, None)
-        pf_far = run_experts(meta_far_f, far_f, None, w_own, w_mate, None)
-        ret_f = combine_far(pf_far)
-        pb_far = run_experts(meta_far_b, far_b, dy_far, w_own, w_mate, None)
-        ret_b = combine_far(pb_far[:2])
-        pb_near = run_experts(meta_near_b, near_b, dy_near, w_own, w_mate, pb_far[2:])
+
+        pf_near = run_experts(meta_f, False, near_f, None, w_own, w_mate, None)
+        pf_far = run_experts(meta_f, True, far_f, None, w_own, w_mate, None)
+        ret_f = to_cross(combine(pf_far))
+        pb_far = run_experts(meta_b, True, far_b, dy_far, w_own, w_mate, None)
+        ret_b = to_cross(combine(pb_far[:2]))
+        pb_near = run_experts(meta_b, False, near_b, dy_near, w_own, w_mate, pb_far[2:])
         dw_full, dw_mate = pb_near[2:5], pb_near[5:8]
 
-        y_val = (mid_f.astype(f32) + (pf_near[0] + to_mate(pf_near[1]) + ret_f)).astype(bf16)
+        y_val = (mid_f.astype(f32) + (combine(pf_near) + ret_f)).astype(bf16)
         y_next = lax.ppermute(y_val, 'pp', fwd_perm)
 
-        d_norm = (pb_near[0] + to_mate(pb_near[1]) + ret_b).astype(bf16)
+        d_norm = (combine(pb_near) + ret_b).astype(bf16)
         d_mid = bwd_dy + norm_back(d_norm)[0]
         d_hidden = jnp.einsum('th,fh->tf', d_mid, stage_w_out, preferred_element_type=f32).astype(bf16)
         _, dense_back = jax.vjp(dense_act, pre_b)
@@ -421,11 +463,12 @@
 
         back = [to_mate(v) for v in dw_mate]
         zero = jnp.zeros((), i32)
-        dw_gate, dw_up, dw_down_t = [lax.dynamic_update_slice(full, part, (2 - base, zero, zero)) for full, part in zip(dw_full, back)]
-        dw_down = jnp.swapaxes(dw_down_t, 1, 2)
+        dw_gate, dw_up, dw_down = [lax.dynamic_update_slice(full, part, (2 - base, zero, zero)) for full, part in zip(dw_full, back)]
         return y_next[None], dx_prev[None], dw_gate[None], dw_up[None], dw_down[None]
 
     spec_act = P('pp', 'ep', None)
     spec_dense = P('pp', None, None)
     spec_exp = P('pp', 'ep', None, None)
+
+
     return jax.shard_map(device_fn, mesh=mesh, in_specs=(spec_act,) * 7 + (spec_dense,) * 2 + (spec_exp,) * 3, out_specs=(spec_act, spec_act, spec_exp, spec_exp, spec_exp), check_vma=False)

time: 769 us -> 739 us (0.961)
  waiting for transfers between devices: 82.8 us -> 144 us
  local copies, waits for them, and re-layouts: 73.5 us -> 29.3 us
  blocking collectives: 84.9 us -> 52.2 us
  other arithmetic: 52.4 us -> 35.8 us
  starting transfers between devices: 173 us -> 182 us
    ppermute x5, waiting for transfers between devices: 64.1 us -> 113 us  [to_cross(): return lax.ppermute(v, 'ep', [(i, i ^ 2) for i in range(n_ep)])]
    all_gather x1, blocking collectives: 84.9 us -> 52.2 us  [device_fn(): table = lax.all_gather(jnp.concatenate(fields), 'ep')]
    slice x21 -> x0, local copies, waits for them, and re-layouts: 15.7 us -> none  [the longest x6 4.34 us: routing(): nwin[:, i].reshape(-1)]
    ppermute x1, waiting for transfers between devices: 18.6 us -> 30.9 us  [device_fn(): dx_prev = lax.ppermute(dx_val, 'pp', bwd_perm)]
    unnamed x59 -> x58, local copies, waits for them, and re-layouts: 19 us -> 6.99 us
    reshape x6 -> x0, local copies, waits for them, and re-layouts: 8.15 us -> none  [the longest x2 3.25 us: routing(): rank = jnp.where(hit, incl - 1, -1).reshape(E_RUN, 2, n2)]
    pallas_call x4 -> x5, Pallas kernels: 266 us -> 264 us  [the longest x4 260 us: run_experts(): pl.pallas_call(functools.partial(expert_kernel, bwd, carry, E_RUN if far...]
  transfers between devices with their start and end apart: 23 -> 23, of which waited for: 3 -> 4; matrix products, arithmetic and copies ran while one was open for 17% -> 10% of each run, Pallas kernels for 35% -> 36%
where the time goes in v2:
time: 739 us; the launch traced here: 735 us
  Pallas kernels  264 us (36%)
  starting transfers between devices  182 us (25%)
  waiting for transfers between devices  144 us (19%)
  blocking collectives  52.2 us (7%)
  other arithmetic  35.8 us (5%)
  local copies, waits for them, and re-layouts  29.3 us (4%)
  matrix products  25.7 us (3%)
    pallas_call x4, Pallas kernels, run_experts(): pl.pallas_call(functools.partial(expert_kernel, bwd, carry, E_RUN if far...  260 us
    ppermute x5, waiting for transfers between devices, to_cross(): return lax.ppermute(v, 'ep', [(i, i ^ 2) for i in range(n_ep)])  113 us
    ppermute x5, starting transfers between devices, to_cross(): return lax.ppermute(v, 'ep', [(i, i ^ 2) for i in range(n_ep)])  81 us
    all_gather x1, blocking collectives, device_fn(): table = lax.all_gather(jnp.concatenate(fields), 'ep')  52.2 us
    ppermute x1, starting transfers between devices, device_fn(): y_next = lax.ppermute(y_val, 'pp', fwd_perm)  48.8 us
    ppermute x1, starting transfers between devices, device_fn(): dx_prev = lax.ppermute(dx_val, 'pp', bwd_perm)  48.5 us
    ppermute x1, waiting for transfers between devices, device_fn(): dx_prev = lax.ppermute(dx_val, 'pp', bwd_perm)  30.9 us
  transfers between devices with their start and end apart: 23, of which 4 were waited for; matrix products, arithmetic and copies ran while one was open for 10% of the time, Pallas kernels for 36%

profile of v2, /device:TPU:0, one launch (start us, length us, event | category | flops | bytes accessed | tf_op | source)
XLA Modules:
  0.0 734.8 jit_solution(9026138131007222395)
XLA Ops:
  0.6 2.2 fusion.21
  2.8 8.6 %fusion.28 = (f32[2048]{0:T(1024)S(1)}, bf16[2048,512]{1,0:T(8,128)(2,1)S(1)}) fusion(bf16[1,1280,512]{2,1,0:T(8,128)(2,1)} %param.20, bf16[1,2048,512]{2,1,0:T(8,128)(2,1)} %param.12, f32[2048]{0:T(1024)S(1)} %add_rsqrt_fusion.1, bf16[1,512,1280]{2,1,0:T(8,128)(2,1)S(1)} %copy-done), kind=kOutput, calls=%fused_computation.54 | convolution fusion | flops 5396494336 | bytes 6832128 | tf_op jit(solution)/shard_map/dot_general | solution.py:430
  11.5 1.8 fusion.29.refs_6_
  13.3 3.3 collective-permute-start.5
  16.7 52.2 %all-gather = f32[64,2048]{1,0:T(8,128)} all-gather(f32[16,2048]{1,0:T(8,128)S(1)} %pad_maximum_fusion), channel_id=2, replica_groups=mesh['pp'=2,'ep'=4] {'ep'}, dimensions={0}, use_global_device_ids=true | all-gather | bytes 655360 | tf_op jit(solution)/shard_map/all_gather | solution.py:414
  71.2 3.7 convolution_convert_fusion.1
  74.9 3.6 fusion.33
  81.5 4.1 routing.1
  88.5 40.5 %collective-permute-done.12.refs_6_ = bf16[2048,512]{1,0:T(8,128)(2,1)} collective-permute-done((bf16[2048,512]{1,0:T(8,128)(2,1)S(1)}, bf16[2048,512]{1,0:T(8,128)(2,1)}, u32[]{:S(2)}, u32[]{:S(2)}) %collective-permute-start.12) | collective-permute-done | bytes 2097184 | tf_op jit(solution)/shard_map/ppermute | solution.py:393
  131.5 1.7 slice_bitcast_fusion.1
  134.9 38.5 %collective-permute-done.14.refs_8_ = bf16[2048,512]{1,0:T(8,128)(2,1)} collective-permute-done((bf16[2048,512]{1,0:T(8,128)(2,1)}, bf16[2048,512]{1,0:T(8,128)(2,1)}, u32[]{:S(2)}, u32[]{:S(2)}) %collective-permute-start.14) | collective-permute-done | bytes 2097184 | tf_op jit(solution)/shard_map/ppermute | solution.py:393
  174.5 58.7 %experts_fwd.3 = (f32[2048,512]{1,0:T(8,128)}, f32[2048,512]{1,0:T(8,128)}) custom-call(s32[8,128]{1,0:T(8,128)} %get-tuple-element.74.refs_0_, s32[8,128]{1,0:T(8,128)} %get-tuple-element.72.refs_1_, s32[8,128]{1,0:T(8,128)} %get-tuple-element.70.refs_2_, s32[1]{0:T(128)} %bitcast.24.refs_3_, s32[8,4096]{1,0:T(8,128)} %get-tuple-element.68.refs_4_, ...), custom_call_target="tpu_custom_call" | custom-call | flops 28185722880 | bytes 60000000 | tf_op jit(solution)/shard_map/experts_fwd/pallas_call | solution.py:371
  233.7 58.7 %experts_fwd.2 = (f32[2048,512]{1,0:T(8,128)}, f32[2048,512]{1,0:T(8,128)}) custom-call(s32[8,128]{1,0:T(8,128)} %get-tuple-element.74.refs_0_, s32[8,128]{1,0:T(8,128)} %get-tuple-element.72.refs_1_, s32[8,128]{1,0:T(8,128)} %get-tuple-element.70.refs_2_, s32[1]{0:T(128)} %bitcast.24.refs_3_, s32[8,4096]{1,0:T(8,128)} %get-tuple-element.68.refs_4_, ...), custom_call_target="tpu_custom_call" | custom-call | flops 28185722880 | bytes 60000000 | tf_op jit(solution)/shard_map/experts_fwd/pallas_call | solution.py:371
  292.5 62.2 %experts_bwd.2 = (f32[2048,512]{1,0:T(8,128)}, f32[2048,512]{1,0:T(8,128)}, f32[4,512,1280]{2,1,0:T(8,128)}, f32[4,512,1280]{2,1,0:T(8,128)}, f32[4,1280,512]{2,...) custom-call(s32[8,128]{1,0:T(8,128)} %get-tuple-element.73.refs_0_, ...), custom_call_target="tpu_custom_call" | custom-call | flops 75161927680 | bytes 60000000 | tf_op jit(solution)/shard_map/experts_bwd/pallas_call | solution.py:371
  355.2 6.5 add.106
  361.6 17.4 %collective-permute-start.8 = (f32[2048,512]{1,0:T(8,128)}, f32[2048,512]{1,0:T(8,128)}, u32[]{:S(2)}, u32[]{:S(2)}) collective-permute-start(f32[2048,512]{1,0:T(8,128)} %add.106), channel_id=1, source_target_pairs={{0,2},{1,3},{2,0},{3,1},{4,6},{5,7},{6,4},{7,5}} | collective-permute-start | bytes 12582920 | tf_op jit(solution)/shard_map/ppermute | solution.py:393
  379.1 80.7 %experts_bwd.3 = (f32[2048,512]{1,0:T(8,128)}, f32[2048,512]{1,0:T(8,128)}, f32[4,512,1280]{2,1,0:T(8,128)}, f32[4,512,1280]{2,1,0:T(8,128)}, f32[4,1280,512]{2,...) custom-call(s32[8,128]{1,0:T(8,128)} %get-tuple-element.73.refs_0_, ...), custom_call_target="tpu_custom_call" | custom-call | flops 75161927680 | bytes 60000000 | tf_op jit(solution)/shard_map/experts_bwd/pallas_call | solution.py:371
  459.8 6.6 add.114
  466.4 58.5 %collective-permute-start.18 = (f32[2048,512]{1,0:T(8,128)}, f32[2048,512]{1,0:T(8,128)}, u32[]{:S(2)}, u32[]{:S(2)}) collective-permute-start(f32[2048,512]{1,0:T(8,128)} %add.114), channel_id=1, source_target_pairs={{0,2},{1,3},{2,0},{3,1},{4,6},{5,7},{6,4},{7,5}} | collective-permute-start | bytes 12582920 | tf_op jit(solution)/shard_map/ppermute | solution.py:393
  525.6 8.0 %fusion.30 = bf16[2048,512]{1,0:T(8,128)(2,1)} fusion(bf16[2048,512]{1,0:T(8,128)(2,1)S(1)} %copy-done.6, f32[2048,512]{1,0:T(8,128)} %collective-permute-done.8, f32[2048,512]{1,0:T(8,128)} %get-tuple-element.42, f32[2048,512]{1,0:T(8,128)} %collective-permute-done.4), kind=kLoop, calls=%fused_computation.56 | loop fusion | flops 5242880 | bytes 16777216 | tf_op jit(solution)/shard_map/convert_element_type | solution.py:451
  533.6 48.8 %collective-permute-start.9 = (bf16[2048,512]{1,0:T(8,128)(2,1)}, bf16[2048,512]{1,0:T(8,128)(2,1)}, u32[]{:S(2)}, u32[]{:S(2)}) collective-permute-start(bf16[2048,512]{1,0:T(8,128)(2,1)} %fusion.30), channel_id=1, source_target_pairs={{0,4},{4,0},{1,5},{5,1},{2,6},{6,2},{3,7},{7,3}} | collective-permute-start | bytes 6291464 | tf_op jit(solution)/shard_map/ppermute | solution.py:452
  582.4 34.1 %collective-permute-done.18 = f32[2048,512]{1,0:T(8,128)} collective-permute-done((f32[2048,512]{1,0:T(8,128)}, f32[2048,512]{1,0:T(8,128)}, u32[]{:S(2)}, u32[]{:S(2)}) %collective-permute-start.18) | collective-permute-done | bytes 4194336 | tf_op jit(solution)/shard_map/ppermute | solution.py:393
  616.4 4.6 fusion.35
  621.1 2.3 fusion.41
  623.4 9.9 %fusion.26 = (f32[2048]{0:T(1024)S(1)}, bf16[2048,512]{1,0:T(8,128)(2,1)}) fusion(bf16[1,2048,512]{2,1,0:T(8,128)(2,1)S(1)} %copy-done.4, bf16[1,512,1280]{2,1,0:T(8,128)(2,1)S(1)} %copy-done, bf16[2048,1280]{1,0:T(8,128)(2,1)} %copy-done.24, bf16[2048,512]{1,0:T(8,128)(2,1)} %fusion.41, bf16[1,1280,512]{2,1,0:T(8,128)(2,1)} %param.20), kind=kOutput, calls=%fused_computation.52 | convolution fusion | flops 5408028672 | bytes 14163968 | tf_op jit(solution)/shard_map/tf,hf->th/dot_general | solution.py:459
  633.3 2.9 fusion.40
  636.2 48.5 %collective-permute-start.19 = (bf16[2048,512]{1,0:T(8,128)(2,1)S(1)}, bf16[2048,512]{1,0:T(8,128)(2,1)S(1)}, u32[]{:S(2)}, u32[]{:S(2)}) collective-permute-start(bf16[2048,512]{1,0:T(8,128)(2,1)S(1)} %fusion.40), channel_id=1, source_target_pairs={{0,4},{4,0},{1,5},{5,1},{2,6},{6,2},{3,7},{7,3}} | collective-permute-start | bytes 6291464 | tf_op jit(solution)/shard_map/ppermute | solution.py:462
  684.7 5.6 bitcast_dynamic-update-slice_fusion.2
  690.4 5.4 bitcast_dynamic-update-slice_fusion.1
  695.8 3.2 bitcast_dynamic-update-slice_fusion
  699.0 30.9 %collective-permute-done.19 = bf16[2048,512]{1,0:T(8,128)(2,1)S(1)} collective-permute-done((bf16[2048,512]{1,0:T(8,128)(2,1)S(1)}, bf16[2048,512]{1,0:T(8,128)(2,1)S(1)}, u32[]{:S(2)}, u32[]{:S(2)}) %collective-permute-start.19) | collective-permute-done | bytes 2097184 | tf_op jit(solution)/shard_map/ppermute | solution.py:462
  730.0 3.0 copy.28
  (111 shorter events, 16.6 us)
Async XLA Ops:
  11.4 63.4 %copy-start.5 = (bf16[2048,512]{1,0:T(8,128)(2,1)}, bf16[2048,512]{1,0:T(8,128)(2,1)S(1)}, u32[]{:S(2)}) copy-start(bf16[2048,512]{1,0:T(8,128)(2,1)S(1)} %get-tuple-element.76) | copy-start | bytes 6291460
  11.5 58.0 %copy-start.3 = (bf16[1,2048,512]{2,1,0:T(8,128)(2,1)S(1)}, bf16[1,2048,512]{2,1,0:T(8,128)(2,1)}, u32[]{:S(2)}) copy-start(bf16[1,2048,512]{2,1,0:T(8,128)(2,1)} %param.13) | copy-start | bytes 6291460
  13.3 73.7 %collective-permute-start.5 = (bf16[2048,512]{1,0:T(8,128)(2,1)}, bf16[2048,512]{1,0:T(8,128)(2,1)}, u32[]{:S(2)}, u32[]{:S(2)}) collective-permute-start(bf16[2048,512]{1,0:T(8,128)(2,1)} %fusion.29.refs_6_), channel_id=1, source_target_pairs={{0,2},{1,3},{2,0},{3,1},{4,6},{5,7},{6,4},{7,5}} | collective-permute-start | bytes 6291464 | tf_op jit(solution)/shard_map/ppermute | solution.py:393
  68.9 105.0 %collective-permute-start.1 = (bf16[4,512,1280]{2,1,0:T(8,128)(2,1)}, bf16[4,512,1280]{2,1,0:T(8,128)(2,1)}, u32[]{:S(2)}, u32[]{:S(2)}) collective-permute-start(bf16[4,512,1280]{2,1,0:T(8,128)(2,1)} %bitcast.142), channel_id=1, source_target_pairs={{0,1},{1,0},{2,3},{3,2},{4,5},{5,4},{6,7},{7,6}} | collective-permute-start | bytes 15728648 | tf_op jit(solution)/shard_map/ppermute | solution.py:390
  68.9 105.0 %collective-permute-start.2 = (bf16[4,512,1280]{2,1,0:T(8,128)(2,1)}, bf16[4,512,1280]{2,1,0:T(8,128)(2,1)}, u32[]{:S(2)}, u32[]{:S(2)}) collective-permute-start(bf16[4,512,1280]{2,1,0:T(8,128)(2,1)} %bitcast.147), channel_id=1, source_target_pairs={{0,1},{1,0},{2,3},{3,2},{4,5},{5,4},{6,7},{7,6}} | collective-permute-start | bytes 15728648 | tf_op jit(solution)/shard_map/ppermute | solution.py:390
  69.4 105.0 %collective-permute-start.3 = (bf16[4,1280,512]{2,1,0:T(8,128)(2,1)}, bf16[4,1280,512]{2,1,0:T(8,128)(2,1)}, u32[]{:S(2)}, u32[]{:S(2)}) collective-permute-start(bf16[4,1280,512]{2,1,0:T(8,128)(2,1)} %bitcast.152), channel_id=1, source_target_pairs={{0,1},{1,0},{2,3},{3,2},{4,5},{5,4},{6,7},{7,6}} | collective-permute-start | bytes 15728648 | tf_op jit(solution)/shard_map/ppermute | solution.py:390
  80.3 152.9 %copy-start.8 = (bf16[2048,512]{1,0:T(8,128)(2,1)}, bf16[2048,512]{1,0:T(8,128)(2,1)S(1)}, u32[]{:S(2)}) copy-start(bf16[2048,512]{1,0:T(8,128)(2,1)S(1)} %fusion.34.refs_6_) | copy-start | bytes 6291460
  80.4 48.6 %collective-permute-start.12 = (bf16[2048,512]{1,0:T(8,128)(2,1)S(1)}, bf16[2048,512]{1,0:T(8,128)(2,1)}, u32[]{:S(2)}, u32[]{:S(2)}) collective-permute-start(bf16[2048,512]{1,0:T(8,128)(2,1)S(1)} %fusion.34.refs_6_), channel_id=1, source_target_pairs={{0,2},{1,3},{2,0},{3,1},{4,6},{5,7},{6,4},{7,5}} | collective-permute-start | bytes 6291464 | tf_op jit(solution)/shard_map/ppermute | solution.py:393
  87.0 86.5 %collective-permute-start.14 = (bf16[2048,512]{1,0:T(8,128)(2,1)}, bf16[2048,512]{1,0:T(8,128)(2,1)}, u32[]{:S(2)}, u32[]{:S(2)}) collective-permute-start(bf16[2048,512]{1,0:T(8,128)(2,1)} %bitcast.134), channel_id=1, source_target_pairs={{0,2},{1,3},{2,0},{3,1},{4,6},{5,7},{6,4},{7,5}} | collective-permute-start | bytes 6291464 | tf_op jit(solution)/shard_map/ppermute | solution.py:393
  129.0 44.5 %collective-permute-start.6 = (bf16[2048,512]{1,0:T(8,128)(2,1)}, bf16[2048,512]{1,0:T(8,128)(2,1)}, u32[]{:S(2)}, u32[]{:S(2)}) collective-permute-start(bf16[2048,512]{1,0:T(8,128)(2,1)} %collective-permute-done.5.refs_6_), channel_id=1, source_target_pairs={{0,1},{1,0},{2,3},{3,2},{4,5},{5,4},{6,7},{7,6}} | collective-permute-start | bytes 6291464 | tf_op jit(solution)/shard_map/ppermute | solution.py:390
  173.4 59.8 %collective-permute-start = (bf16[2048,512]{1,0:T(8,128)(2,1)}, bf16[2048,512]{1,0:T(8,128)(2,1)}, u32[]{:S(2)}, u32[]{:S(2)}) collective-permute-start(bf16[2048,512]{1,0:T(8,128)(2,1)} %fusion.29.refs_6_), channel_id=1, source_target_pairs={{0,1},{1,0},{2,3},{3,2},{4,5},{5,4},{6,7},{7,6}} | collective-permute-start | bytes 6291464 | tf_op jit(solution)/shard_map/ppermute | solution.py:390
  173.4 205.6 %collective-permute-start.10 = (bf16[2048,512]{1,0:T(8,128)(2,1)S(1)}, bf16[2048,512]{1,0:T(8,128)(2,1)}, u32[]{:S(2)}, u32[]{:S(2)}) collective-permute-start(bf16[2048,512]{1,0:T(8,128)(2,1)S(1)} %fusion.34.refs_6_), channel_id=1, source_target_pairs={{0,1},{1,0},{2,3},{3,2},{4,5},{5,4},{6,7},{7,6}} | collective-permute-start | bytes 6291464 | tf_op jit(solution)/shard_map/ppermute | solution.py:390
  174.0 205.1 %collective-permute-start.11 = (bf16[2048,512]{1,0:T(8,128)(2,1)}, bf16[2048,512]{1,0:T(8,128)(2,1)}, u32[]{:S(2)}, u32[]{:S(2)}) collective-permute-start(bf16[2048,512]{1,0:T(8,128)(2,1)} %bitcast.135), channel_id=1, source_target_pairs={{0,1},{1,0},{2,3},{3,2},{4,5},{5,4},{6,7},{7,6}} | collective-permute-start | bytes 6291464 | tf_op jit(solution)/shard_map/ppermute | solution.py:390
  174.0 118.4 %collective-permute-start.13 = (bf16[2048,512]{1,0:T(8,128)(2,1)}, bf16[2048,512]{1,0:T(8,128)(2,1)}, u32[]{:S(2)}, u32[]{:S(2)}) collective-permute-start(bf16[2048,512]{1,0:T(8,128)(2,1)} %collective-permute-done.12.refs_6_), channel_id=1, source_target_pairs={{0,1},{1,0},{2,3},{3,2},{4,5},{5,4},{6,7},{7,6}} | collective-permute-start | bytes 6291464 | tf_op jit(solution)/shard_map/ppermute | solution.py:390
  174.5 118.0 %collective-permute-start.15 = (bf16[2048,512]{1,0:T(8,128)(2,1)}, bf16[2048,512]{1,0:T(8,128)(2,1)}, u32[]{:S(2)}, u32[]{:S(2)}) collective-permute-start(bf16[2048,512]{1,0:T(8,128)(2,1)} %collective-permute-done.14.refs_8_), channel_id=1, source_target_pairs={{0,1},{1,0},{2,3},{3,2},{4,5},{5,4},{6,7},{7,6}} | collective-permute-start | bytes 6291464 | tf_op jit(solution)/shard_map/ppermute | solution.py:390
  233.2 121.9 %collective-permute-start.7 = (f32[2048,512]{1,0:T(8,128)}, f32[2048,512]{1,0:T(8,128)}, u32[]{:S(2)}, u32[]{:S(2)}) collective-permute-start(f32[2048,512]{1,0:T(8,128)} %get-tuple-element.45), channel_id=1, source_target_pairs={{0,1},{1,0},{2,3},{3,2},{4,5},{5,4},{6,7},{7,6}} | collective-permute-start | bytes 12582920 | tf_op jit(solution)/shard_map/ppermute | solution.py:390
  292.4 232.7 %collective-permute-start.4 = (f32[2048,512]{1,0:T(8,128)}, f32[2048,512]{1,0:T(8,128)}, u32[]{:S(2)}, u32[]{:S(2)}) collective-permute-start(f32[2048,512]{1,0:T(8,128)} %get-tuple-element.43), channel_id=1, source_target_pairs={{0,1},{1,0},{2,3},{3,2},{4,5},{5,4},{6,7},{7,6}} | collective-permute-start | bytes 12582920 | tf_op jit(solution)/shard_map/ppermute | solution.py:390
  354.7 105.1 %collective-permute-start.17 = (f32[2048,512]{1,0:T(8,128)}, f32[2048,512]{1,0:T(8,128)}, u32[]{:S(2)}, u32[]{:S(2)}) collective-permute-start(f32[2048,512]{1,0:T(8,128)} %get-tuple-element.56), channel_id=1, source_target_pairs={{0,1},{1,0},{2,3},{3,2},{4,5},{5,4},{6,7},{7,6}} | collective-permute-start | bytes 12582920 | tf_op jit(solution)/shard_map/ppermute | solution.py:390
  361.6 163.8 %collective-permute-start.8 = (f32[2048,512]{1,0:T(8,128)}, f32[2048,512]{1,0:T(8,128)}, u32[]{:S(2)}, u32[]{:S(2)}) collective-permute-start(f32[2048,512]{1,0:T(8,128)} %add.106), channel_id=1, source_target_pairs={{0,2},{1,3},{2,0},{3,1},{4,6},{5,7},{6,4},{7,5}} | collective-permute-start | bytes 12582920 | tf_op jit(solution)/shard_map/ppermute | solution.py:393
  459.7 73.8 %collective-permute-start.16 = (f32[2048,512]{1,0:T(8,128)}, f32[2048,512]{1,0:T(8,128)}, u32[]{:S(2)}, u32[]{:S(2)}) collective-permute-start(f32[2048,512]{1,0:T(8,128)} %get-tuple-element.54), channel_id=1, source_target_pairs={{0,1},{1,0},{2,3},{3,2},{4,5},{5,4},{6,7},{7,6}} | collective-permute-start | bytes 12582920 | tf_op jit(solution)/shard_map/ppermute | solution.py:390
  459.8 65.8 %copy-start.6 = (bf16[2048,512]{1,0:T(8,128)(2,1)S(1)}, bf16[2048,512]{1,0:T(8,128)(2,1)}, u32[]{:S(2)}) copy-start(bf16[2048,512]{1,0:T(8,128)(2,1)} %copy-done.5) | copy-start | bytes 6291460
  466.4 150.0 %collective-permute-start.18 = (f32[2048,512]{1,0:T(8,128)}, f32[2048,512]{1,0:T(8,128)}, u32[]{:S(2)}, u32[]{:S(2)}) collective-permute-start(f32[2048,512]{1,0:T(8,128)} %add.114), channel_id=1, source_target_pairs={{0,2},{1,3},{2,0},{3,1},{4,6},{5,7},{6,4},{7,5}} | collective-permute-start | bytes 12582920 | tf_op jit(solution)/shard_map/ppermute | solution.py:393
  524.9 159.8 %collective-permute-start.20 = (f32[2,512,1280]{2,1,0:T(8,128)}, f32[2,512,1280]{2,1,0:T(8,128)}, u32[]{:S(2)}, u32[]{:S(2)}) collective-permute-start(f32[2,512,1280]{2,1,0:T(8,128)} %get-tuple-element.58), channel_id=1, source_target_pairs={{0,1},{1,0},{2,3},{3,2},{4,5},{5,4},{6,7},{7,6}} | collective-permute-start | bytes 15728648 | tf_op jit(solution)/shard_map/ppermute | solution.py:390
  525.1 165.3 %collective-permute-start.21 = (f32[2,512,1280]{2,1,0:T(8,128)}, f32[2,512,1280]{2,1,0:T(8,128)}, u32[]{:S(2)}, u32[]{:S(2)}) collective-permute-start(f32[2,512,1280]{2,1,0:T(8,128)} %get-tuple-element.60), channel_id=1, source_target_pairs={{0,1},{1,0},{2,3},{3,2},{4,5},{5,4},{6,7},{7,6}} | collective-permute-start | bytes 15728648 | tf_op jit(solution)/shard_map/ppermute | solution.py:390
  525.4 170.4 %collective-permute-start.22 = (f32[2,1280,512]{2,1,0:T(8,128)}, f32[2,1280,512]{2,1,0:T(8,128)}, u32[]{:S(2)}, u32[]{:S(2)}) collective-permute-start(f32[2,1280,512]{2,1,0:T(8,128)} %get-tuple-element.62), channel_id=1, source_target_pairs={{0,1},{1,0},{2,3},{3,2},{4,5},{5,4},{6,7},{7,6}} | collective-permute-start | bytes 15728648 | tf_op jit(solution)/shard_map/ppermute | solution.py:390
  525.6 90.8 %copy-start.2 = (bf16[2048,512]{1,0:T(8,128)(2,1)S(1)}, bf16[2048,512]{1,0:T(8,128)(2,1)}, u32[]{:S(2)}) copy-start(bf16[2048,512]{1,0:T(8,128)(2,1)} %copy-done.1) | copy-start | bytes 6291460
  525.6 90.8 %copy-start.7 = (f32[2048,512]{1,0:T(8,128)S(1)}, f32[2048,512]{1,0:T(8,128)}, u32[]{:S(2)}) copy-start(f32[2048,512]{1,0:T(8,128)} %get-tuple-element.53) | copy-start | bytes 12582916
  533.6 165.4 %collective-permute-start.9 = (bf16[2048,512]{1,0:T(8,128)(2,1)}, bf16[2048,512]{1,0:T(8,128)(2,1)}, u32[]{:S(2)}, u32[]{:S(2)}) collective-permute-start(bf16[2048,512]{1,0:T(8,128)(2,1)} %fusion.30), channel_id=1, source_target_pairs={{0,4},{4,0},{1,5},{5,1},{2,6},{6,2},{3,7},{7,3}} | collective-permute-start | bytes 6291464 | tf_op jit(solution)/shard_map/ppermute | solution.py:452
  636.2 93.8 %collective-permute-start.19 = (bf16[2048,512]{1,0:T(8,128)(2,1)S(1)}, bf16[2048,512]{1,0:T(8,128)(2,1)S(1)}, u32[]{:S(2)}, u32[]{:S(2)}) collective-permute-start(bf16[2048,512]{1,0:T(8,128)(2,1)S(1)} %fusion.40), channel_id=1, source_target_pairs={{0,4},{4,0},{1,5},{5,1},{2,6},{6,2},{3,7},{7,3}} | collective-permute-start | bytes 6291464 | tf_op jit(solution)/shard_map/ppermute | solution.py:462
  684.7 11.1 %slice-start = ((s8[10485760]{0:T(1024)(128)(4,1)}), s8[4194304]{0:T(1024)(128)(4,1)S(1)}, s32[]{:S(2)}) async-start(s8[10485760]{0:T(1024)(128)(4,1)} %bitcast.137), calls=%async_computation | async-start | bytes 8388608
  684.7 11.1 %slice-start.1 = ((s8[10485760]{0:T(1024)(128)(4,1)}), s8[4194304]{0:T(1024)(128)(4,1)S(1)}, s32[]{:S(2)}) async-start(s8[10485760]{0:T(1024)(128)(4,1)} %bitcast.137), calls=%async_computation.1 | async-start | bytes 8388608
  699.0 35.3 %copy-start.22 = (f32[1,4,1280,512]{3,2,1,0:T(8,128)}, f32[1,4,1280,512]{3,2,1,0:T(8,128)S(1)}, u32[]{:S(2)}) copy-start(f32[1,4,1280,512]{3,2,1,0:T(8,128)S(1)} %bitcast_dynamic-update-slice_fusion) | copy-start | bytes 31457284
  (19 other events, 78.2 us)

commit v3 on v2

--- a/solution.py
+++ b/solution.py
@@ -9,25 +9,20 @@
 
 
 EPS_NORM = 1e-6
-SUB = 256
-PER_TILE = 2
-WIN = 512
-WIN_MORE = 1024
+SUB = 128
+TILE_SUBS = (3, 4)
+WIN = 256
+WIN_MORE = 768
+ALIGN = 64
 CHUNK = 256
+DW_SLOTS = 3
+TAIL = 4
+DENSE_ROWS = 512
 E_RUN = 4
 
 f32 = jnp.float32
 bf16 = jnp.bfloat16
 i32 = jnp.int32
-
-
-def rms_norm(rows_in):
-    rows_f32 = rows_in.astype(f32)
-    return (rows_f32 * lax.rsqrt(jnp.mean(rows_f32 * rows_f32, axis=-1, keepdims=True) + EPS_NORM)).astype(bf16)
-
-
-def dense_act(pre_act):
-    return jax.nn.silu(pre_act.astype(f32)).astype(bf16)
 
 
 def dot_nn(a, b):
@@ -53,12 +48,14 @@
     starts, nwins, ntiles, base_ref, rank_ref, gate_ref = take(6)
     tok_in = take(2)
     dy_in = take(2) if bwd else []
+    mb = int(bwd)
+    per_tile = TILE_SUBS[mb]
     w_own = take(3)
     w_mate = take(3)
     dw_in = take(6) if carry else []
     p_out = take(2)
     dw_out = take(6) if bwd else []
-    tok, acc, wg_buf, wu_buf, wd_buf, x_acc = take(6)
+    tok, acc, wg_buf, wu_buf, wd_buf, x_acc, out_all = take(7)
     if bwd:
         dyt, d_acc, xt, dg_all, du_all, dwg_buf, dwu_buf, dwd_buf = take(8)
         tok_sem, w_sem, in_sem, out_sem = take(4)
@@ -124,21 +121,19 @@
 
     def window(e, st, k):
         size = WIN_MORE if k is not None else WIN
-        so = starts[row0 + e, st]
+        so = starts[mb, row0 + e, st]
         if k is not None:
             so += WIN + (k - 1) * WIN_MORE
-        s = pl.multiple_of(jnp.minimum(so, n_tok - size), 128)
-        rk = rank_ref[pl.ds(row0 + e, 1), pl.ds(s, size)]
+        s = jnp.minimum(so, n_tok - size)
+        shift = lax.rem(s // ALIGN, 2)
+        lanes = pl.ds(pl.multiple_of(s - shift * ALIGN, 128), size)
+        rk = rank_ref[mb, shift, pl.ds(row0 + e, 1), lanes]
         lane = lax.broadcasted_iota(i32, (1, size), 1) + s
         rk = jnp.where(lane >= so, rk, -1) - st * SUB
         mask = lax.broadcasted_iota(i32, (SUB, size), 0) == rk
-        return pl.ds(s, size), mask
-
-    def ones(mask):
-        return jnp.where(mask, 1.0, 0.0).astype(bf16)
-
-    def gated(mask, e, win):
-        return jnp.where(mask, gate_ref[pl.ds(row0 + e, 1), win], 0.0).astype(bf16)
+        toks = pl.ds(pl.multiple_of(s, ALIGN), size)
+        return toks, lambda: jnp.where(mask, 1.0, 0.0).astype(bf16), \
+            lambda: jnp.where(mask, gate_ref[mb, shift, pl.ds(row0 + e, 1), lanes], 0.0).astype(bf16)
 
     def expert(e, _):
         slot = lax.rem(e, 2)
@@ -151,31 +146,43 @@
 
         wg, wu, wd = wg_buf.at[slot], wu_buf.at[slot], wd_buf.at[slot]
         if bwd:
+            d_slot = lax.rem(e, DW_SLOTS)
+
+            @pl.when(e >= 2)
+            def _():
+                old = e - 2
+                dw_copies(dw_out, old, lax.rem(old, DW_SLOTS), out_sem, False)[1]()
+
             if carry:
-                dw_copies(dw_in, e, slot, in_sem, True)[1]()
+                @pl.when(e < E_RUN - 1)
+                def _():
+                    dw_copies(dw_in, e + 1, lax.rem(e + 1, DW_SLOTS), in_sem, True)[0]()
+
+                dw_copies(dw_in, e, d_slot, in_sem, True)[1]()
             else:
                 for b in (dwg_buf, dwu_buf, dwd_buf):
-                    b[slot] = jnp.zeros(b.shape[1:], f32)
-            dwg, dwu, dwd = dwg_buf.at[slot], dwu_buf.at[slot], dwd_buf.at[slot]
+                    b[d_slot] = jnp.zeros(b.shape[1:], f32)
+            dwg, dwu, dwd = dwg_buf.at[d_slot], dwu_buf.at[d_slot], dwd_buf.at[d_slot]
 
         def tile(t, _):
-            for h in range(PER_TILE):
-                st = t * PER_TILE + h
+            for h in range(per_tile):
                 rows = pl.ds(h * SUB, SUB)
-                win, mask = window(e, st, None)
-                x_acc[rows, :] = dot_nn(ones(mask), tok[win, :])
+                toks, ones, gated = window(e, t * per_tile + h, None)
+                x_acc[rows, :] = dot_nn(ones(), tok[toks, :])
                 if bwd:
-                    d_acc[rows, :] = dot_nn(gated(mask, e, win), dyt[win, :])
-            for h in range(PER_TILE):
-                st = t * PER_TILE + h
-                rows = pl.ds(h * SUB, SUB)
-
-                @pl.loop(1, nwins[row0 + e, st])
+                    d_acc[rows, :] = dot_nn(gated(), dyt[toks, :])
+
+            @pl.loop(0, per_tile)
+            def _(h):
+                st = t * per_tile + h
+                rows = pl.ds(pl.multiple_of(h * SUB, SUB), SUB)
+
+                @pl.loop(1, nwins[mb, row0 + e, st])
                 def _(k):
-                    win, mask = window(e, st, k)
-                    x_acc[rows, :] += dot_nn(ones(mask), tok[win, :])
+                    toks, ones, gated = window(e, st, k)
+                    x_acc[rows, :] += dot_nn(ones(), tok[toks, :])
                     if bwd:
-                        d_acc[rows, :] += dot_nn(gated(mask, e, win), dyt[win, :])
+                        d_acc[rows, :] += dot_nn(gated(), dyt[toks, :])
 
             x = x_acc[...].astype(bf16)
             if bwd:
@@ -205,36 +212,26 @@
                 out = dot_nn(act_all[...], wd[...]).astype(bf16)
 
             def put(st, k, part):
-                win, mask = window(e, st, k)
-                sel = ones(mask) if bwd else gated(mask, e, win)
-                acc[win, :] += dot_tn(sel, part)
-
-            for h in range(PER_TILE):
-                put(t * PER_TILE + h, None, out[h * SUB:(h + 1) * SUB, :])
-            x_acc[...] = out.astype(f32)
-            for h in range(PER_TILE):
-                st = t * PER_TILE + h
-
-                @pl.loop(1, nwins[row0 + e, st])
+                toks, ones, gated = window(e, st, k)
+                acc[toks, :] += dot_tn(ones() if bwd else gated(), part)
+
+            out_all[...] = out
+            for h in range(per_tile):
+                put(t * per_tile + h, None, out[h * SUB:(h + 1) * SUB, :])
+
+            @pl.loop(0, per_tile)
+            def _(h):
+                st = t * per_tile + h
+
+                @pl.loop(1, nwins[mb, row0 + e, st])
                 def _(k):
-                    put(st, k, x_acc[h * SUB:(h + 1) * SUB, :].astype(bf16))
-
-            if bwd:
-                @pl.when(t == 0)
-                def _():
-                    @pl.when(e >= 1)
-                    def _():
-                        dw_copies(dw_out, e - 1, 1 - slot, out_sem, False)[1]()
-
-                    if carry:
-                        @pl.when(e < E_RUN - 1)
-                        def _():
-                            dw_copies(dw_in, e + 1, 1 - slot, in_sem, True)[0]()
+                    put(st, k, out_all[pl.ds(pl.multiple_of(h * SUB, SUB), SUB), :])
+
             return 0
 
-        lax.fori_loop(0, ntiles[row0 + e, 0], tile, 0)
+        lax.fori_loop(0, ntiles[mb, row0 + e, 0], tile, 0)
         if bwd:
-            dw_copies(dw_out, e, slot, out_sem, False)[0]()
+            dw_copies(dw_out, e, d_slot, out_sem, False)[0]()
         return 0
 
     lax.fori_loop(0, E_RUN, expert, 0)
@@ -242,13 +239,14 @@
     for c in outs:
         c.start()
     if bwd:
-        dw_copies(dw_out, E_RUN - 1, (E_RUN - 1) % 2, out_sem, False)[1]()
+        for e in (E_RUN - 2, E_RUN - 1):
+            dw_copies(dw_out, e, e % DW_SLOTS, out_sem, False)[1]()
     for c in outs:
         c.wait()
 
 
-def routing_kernel(n_sub, who_ref, tab_ref, rank_ref, gate_ref, start_ref, nwin_ref, ntile_ref, hit_ref):
-    _, fields, n_tok = tab_ref.shape
+def routing_kernel(n_sub, who_ref, tab0, tab1, tab2, tab3, rank_ref, gate_ref, start_ref, nwin_ref, ntile_ref, hit_ref):
+    fields, n_tok = tab0.shape
     top_k = fields // 4
     n2 = 2 * n_tok
     n_blk = n2 // 128
@@ -258,15 +256,15 @@
     full = jnp.ones((128, 128), bf16)
     lane = lax.broadcasted_iota(i32, (2 * E_RUN, 128), 1)
     for mb in range(2):
-        for q in range(4):
-            part = tab_ref[who_ref[q], pl.ds(mb * 2 * top_k, 2 * top_k), :]
+        for q, tab in enumerate((tab0, tab1, tab2, tab3)):
+            part = tab[mb * 2 * top_k:(mb + 1) * 2 * top_k, :]
             ids, gates = part[:top_k], part[top_k:]
             cols = pl.ds((q % 2) * n_tok, n_tok)
             for e in range(E_RUN):
-                match = ids == who_ref[4 + e].astype(f32)
+                match = ids == who_ref[e].astype(f32)
                 row = (q // 2) * E_RUN + e
                 hit_ref[row:row + 1, cols] = jnp.sum(jnp.where(match, 1.0, 0.0), axis=0, keepdims=True)
-                gate_ref[mb, row:row + 1, cols] = jnp.sum(jnp.where(match, gates, 0.0), axis=0, keepdims=True)
+                gate_ref[mb, 0, row:row + 1, cols] = jnp.sum(jnp.where(match, gates, 0.0), axis=0, keepdims=True)
         hits = [hit_ref[:, b * 128:(b + 1) * 128] for b in range(n_blk)]
         stacked = jnp.concatenate(hits, axis=0).astype(bf16)
         within = dot_nn(stacked, tri)
@@ -276,9 +274,13 @@
         for b in range(n_blk):
             rows = slice(b * 2 * E_RUN, (b + 1) * 2 * E_RUN)
             v = (within[rows] + carry).astype(i32)
-            rank_ref[mb, :, b * 128:(b + 1) * 128] = jnp.where(hits[b] > 0.5, v - 1, -1)
+            rank_ref[mb, 0, :, b * 128:(b + 1) * 128] = jnp.where(hits[b] > 0.5, v - 1, -1)
             incl.append(v)
             carry = carry + totals[rows]
+        for ref, fill in ((rank_ref, -1), (gate_ref, 0.0)):
+            ref[mb, 1, :, :n2 - 128] = ref[mb, 0, :, ALIGN:n2 - 128 + ALIGN]
+            tail = jnp.concatenate([ref[mb, 0, :, n2 - 128:], jnp.full((2 * E_RUN, 128), fill, ref.dtype)], axis=1)
+            ref[mb, 1, :, n2 - 128:] = tail[:, ALIGN:128 + ALIGN]
         cnt = carry.astype(i32)
 
         def tokens_upto(limit):
@@ -290,31 +292,108 @@
         start = jnp.zeros((2 * E_RUN, 128), i32)
         nwin = jnp.ones((2 * E_RUN, 128), i32)
         for j in range(n_sub):
-            lo = jnp.minimum(tokens_upto(j * SUB), n2 - 1) // 128 * 128
+            lo = jnp.minimum(tokens_upto(j * SUB), n2 - 1) // ALIGN * ALIGN
             hi = tokens_upto(jnp.minimum((j + 1) * SUB, cnt) - 1) + 1
             n = jnp.maximum((hi - lo - WIN + WIN_MORE - 1) // WIN_MORE, 0) + 1
             start = jnp.where(lane == j, lo, start)
             nwin = jnp.where(lane == j, n, nwin)
         start_ref[mb] = start
         nwin_ref[mb] = nwin
-        tile_rows = SUB * PER_TILE
+        tile_rows = SUB * TILE_SUBS[mb]
         ntile_ref[mb] = jnp.maximum((cnt + tile_rows - 1) // tile_rows, 1)
 
 
-def run_routing(who, table, n_sub):
-    _, _, n_tok = table.shape
+def run_routing(who, tables, n_sub):
+    n_tok = tables[0].shape[1]
     rows = 2 * E_RUN
-    wide = (2, rows, 2 * n_tok)
+    wide = (2, 2, rows, 2 * n_tok)
     small = jax.ShapeDtypeStruct((2, rows, 128), i32)
     vmem = pl.BlockSpec(memory_space=pltpu.VMEM)
     return pl.pallas_call(
         functools.partial(routing_kernel, n_sub),
         out_shape=[jax.ShapeDtypeStruct(wide, i32), jax.ShapeDtypeStruct(wide, f32), small, small, small],
-        in_specs=[pl.BlockSpec(memory_space=pltpu.SMEM), vmem],
+        in_specs=[pl.BlockSpec(memory_space=pltpu.SMEM)] + [vmem] * 4,
         out_specs=[vmem] * 5,
         scratch_shapes=[pltpu.VMEM((rows, 2 * n_tok), f32)],
         name='routing',
-    )(who, table)
+    )(who, *tables)
+
+
+def sigmoid(v):
+    return 1.0 / (1.0 + jnp.exp(-v))
+
+
+def rms_scale(rows_f32):
+    return lax.rsqrt(jnp.mean(rows_f32 * rows_f32, axis=-1, keepdims=True) + EPS_NORM)
+
+
+def rms_back(rows_f32, cot):
+    cot = cot.astype(f32)
+    scale = rms_scale(rows_f32)
+    proj = jnp.mean(cot * rows_f32, axis=-1, keepdims=True)
+    return (scale * cot - rows_f32 * (scale * scale * scale * proj)).astype(bf16)
+
+
+def dense_kernel(x_ref, w_in, w_out, norm_ref, mid_ref, *pre_ref):
+    x = x_ref[...].astype(f32)
+    norm_in = (x * rms_scale(x)).astype(bf16)
+    pre = dot_nn(norm_in, w_in[...]).astype(bf16)
+    if pre_ref:
+        pre_ref[0][...] = pre
+    pre = pre.astype(f32)
+    hid = (pre * sigmoid(pre)).astype(bf16)
+    mid = (x + dot_nn(hid, w_out[...])).astype(bf16)
+    mid_ref[...] = mid
+    mid = mid.astype(f32)
+    norm_ref[...] = (mid * rms_scale(mid)).astype(bf16)
+
+
+def run_dense(x, w_in, w_out, keep_pre):
+    n_tok, width = x.shape
+    ff = w_in.shape[1]
+    row = pl.BlockSpec((DENSE_ROWS, width), lambda i: (i, 0))
+    out_shape = [jax.ShapeDtypeStruct(x.shape, bf16)] * 2
+    out_specs = [row, row]
+    if keep_pre:
+        out_shape += [jax.ShapeDtypeStruct((n_tok, ff), bf16)]
+        out_specs += [pl.BlockSpec((DENSE_ROWS, ff), lambda i: (i, 0))]
+    return pl.pallas_call(
+        dense_kernel,
+        grid=(n_tok // DENSE_ROWS,),
+        out_shape=out_shape,
+        in_specs=[row, pl.BlockSpec((width, ff), lambda i: (0, 0)), pl.BlockSpec((ff, width), lambda i: (0, 0))],
+        out_specs=out_specs,
+        cost_estimate=pl.CostEstimate(flops=4 * n_tok * width * ff, bytes_accessed=12_000_000, transcendentals=0),
+        name='dense_fwd',
+    )(x, w_in, w_out)
+
+
+def tail_kernel(p_own, p_mate, p_far, mid_ref, dy_ref, x_ref, pre_ref, w_in, w_out, dx_ref):
+    d_norm = (p_own[...] + p_mate[...] + p_far[...]).astype(bf16)
+    d_mid = (dy_ref[...].astype(f32) + rms_back(mid_ref[...].astype(f32), d_norm).astype(f32)).astype(bf16)
+    d_hid = dot_nt(d_mid, w_out[...]).astype(bf16).astype(f32)
+    pre = pre_ref[...].astype(f32)
+    sig = sigmoid(pre)
+    d_pre = (d_hid * (sig + pre * sig * (1.0 - sig))).astype(bf16)
+    d_in = dot_nt(d_pre, w_in[...]).astype(bf16)
+    dx_ref[...] = (d_mid.astype(f32) + rms_back(x_ref[...].astype(f32), d_in).astype(f32)).astype(bf16)
+
+
+def run_tail(chunk, p_own, p_mate, p_far, mid, dy, x, pre, w_in, w_out):
+    n_tok, width = x.shape
+    ff = w_in.shape[1]
+    steps = 2
+    rows = n_tok // TAIL // steps
+    row = pl.BlockSpec((rows, width), lambda i: (chunk * steps + i, 0))
+    return pl.pallas_call(
+        tail_kernel,
+        grid=(steps,),
+        out_shape=jax.ShapeDtypeStruct((n_tok // TAIL, width), bf16),
+        in_specs=[row] * 6 + [pl.BlockSpec((rows, ff), lambda i: (chunk * steps + i, 0)),
+                              pl.BlockSpec((width, ff), lambda i: (0, 0)), pl.BlockSpec((ff, width), lambda i: (0, 0))],
+        out_specs=pl.BlockSpec((rows, width), lambda i: (i, 0)),
+        cost_estimate=pl.CostEstimate(flops=4 * rows * steps * width * ff, bytes_accessed=6_000_000, transcendentals=0),
+    )(p_own, p_mate, p_far, mid, dy, x, pre, w_in, w_out)
 
 
 def run_experts(meta, far, toks, dys, w_own, w_mate, dw_prev):
@@ -337,7 +416,7 @@
     if bwd:
         for n in (e_loc, 2):
             out_shape += [jax.ShapeDtypeStruct((n, *w.shape[1:]), f32) for w in w_own]
-    rows = SUB * PER_TILE
+    rows = SUB * TILE_SUBS[int(bwd)]
     scratch = [
         pltpu.VMEM((2 * half, width), bf16),
         pltpu.VMEM((2 * half, width), f32),
@@ -345,6 +424,7 @@
         pltpu.VMEM((2, width, ff), bf16),
         pltpu.VMEM((2, ff, width), bf16),
         pltpu.VMEM((rows, width), f32),
+        pltpu.VMEM((rows, width), bf16),
     ]
     if bwd:
         scratch += [
@@ -353,13 +433,13 @@
             pltpu.VMEM((width, rows), bf16),
             pltpu.VMEM((rows, ff), bf16),
             pltpu.VMEM((rows, ff), bf16),
-            pltpu.VMEM((2, width, ff), f32),
-            pltpu.VMEM((2, width, ff), f32),
-            pltpu.VMEM((2, ff, width), f32),
+            pltpu.VMEM((DW_SLOTS, width, ff), f32),
+            pltpu.VMEM((DW_SLOTS, width, ff), f32),
+            pltpu.VMEM((DW_SLOTS, ff, width), f32),
             pltpu.SemaphoreType.DMA((2, 2)),
             pltpu.SemaphoreType.DMA((2, 3)),
-            pltpu.SemaphoreType.DMA((2, 3)),
-            pltpu.SemaphoreType.DMA((2, 3)),
+            pltpu.SemaphoreType.DMA((DW_SLOTS, 3)),
+            pltpu.SemaphoreType.DMA((DW_SLOTS, 3)),
         ]
     else:
         scratch += [
@@ -404,62 +484,53 @@
         me = lax.axis_index('ep')
         core = lax.rem(me, 2)
         base = 2 * core
-        n_sub = 2 * cap // SUB
+        n_sub = -(-2 * cap // SUB)
 
         def gather_pair(v):
             far = to_cross(v)
             return (v, to_mate(v)), (far, to_mate(far))
 
         fields = [ids_fwd[0].astype(f32).T, gate_fwd[0].astype(f32).T, ids_bwd[0].astype(f32).T, gate_bwd[0].astype(f32).T]
-        table = lax.all_gather(jnp.concatenate(fields), 'ep')
+        table = jnp.concatenate(fields)
+        tables = [table, to_mate(table), to_cross(table)]
+        tables.append(lax.ppermute(table, 'ep', [(i, i ^ 3) for i in range(n_ep)]))
         mine = e_loc * me + base
         mates = e_loc * (me ^ 1) + base
-        who = jnp.stack([me, me ^ 1, me ^ 2, me ^ 3, mine, mine + 1, mates, mates + 1]).astype(i32)
+        who = jnp.stack([mine, mine + 1, mates, mates + 1]).astype(i32)
         base_arr = base.reshape(1).astype(i32)
-        ranks, gates, starts, nwins, ntiles = run_routing(who, table, n_sub)
-        meta_f, meta_b = [(starts[m], nwins[m], ntiles[m], base_arr, ranks[m], gates[m]) for m in range(2)]
-
-        dy_send, w_send = lax.optimization_barrier((bwd_dy, w_own, table))[:2]
-        far_dy = to_cross(dy_send)
-        dy_near, dy_far = (bwd_dy, to_mate(dy_send)), (far_dy, to_mate(far_dy))
-        w_mate = tuple(to_mate(w) for w in w_send)
-
-        def dense_fwd(x_tok):
-            norm_in = rms_norm(x_tok)
-            pre_act = jnp.dot(norm_in, stage_w_in, preferred_element_type=f32).astype(bf16)
-            mid_res = (x_tok.astype(f32) + jnp.dot(dense_act(pre_act), stage_w_out, preferred_element_type=f32)).astype(bf16)
-            return pre_act, mid_res
+        ranks, gates, starts, nwins, ntiles = run_routing(who, tables, n_sub)
+        meta = (starts, nwins, ntiles, base_arr, ranks, gates)
+
+        far_dy = to_cross(bwd_dy)
+        dy_near, dy_far = (bwd_dy, to_mate(bwd_dy)), (far_dy, to_mate(far_dy))
+        w_mate = tuple(to_mate(w) for w in w_own)
 
         def combine(parts):
             return parts[0] + to_mate(parts[1])
 
-        _, mid_f = dense_fwd(fwd_x)
-        norm_f = rms_norm(mid_f)
+        norm_f, mid_f = run_dense(fwd_x, stage_w_in, stage_w_out, False)
         near_f, far_f = gather_pair(norm_f)
-        pre_b, mid_b = dense_fwd(bwd_x)
-        norm_b, norm_back = jax.vjp(rms_norm, mid_b)
+        norm_b, mid_b, pre_b = run_dense(bwd_x, stage_w_in, stage_w_out, True)
         near_b, far_b = gather_pair(norm_b)
 
-        pf_near = run_experts(meta_f, False, near_f, None, w_own, w_mate, None)
-        pf_far = run_experts(meta_f, True, far_f, None, w_own, w_mate, None)
+        pf_near = run_experts(meta, False, near_f, None, w_own, w_mate, None)
+        pf_far = run_experts(meta, True, far_f, None, w_own, w_mate, None)
         ret_f = to_cross(combine(pf_far))
-        pb_far = run_experts(meta_b, True, far_b, dy_far, w_own, w_mate, None)
+        pb_far = run_experts(meta, True, far_b, dy_far, w_own, w_mate, None)
         ret_b = to_cross(combine(pb_far[:2]))
-        pb_near = run_experts(meta_b, False, near_b, dy_near, w_own, w_mate, pb_far[2:])
+        pb_near = run_experts(meta, False, near_b, dy_near, w_own, w_mate, pb_far[2:])
         dw_full, dw_mate = pb_near[2:5], pb_near[5:8]
 
-        y_val = (mid_f.astype(f32) + (combine(pf_near) + ret_f)).astype(bf16)
+        near_f_mate = to_mate(pf_near[1])
+        y_val = (mid_f.astype(f32) + (pf_near[0] + near_f_mate + ret_f)).astype(bf16)
         y_next = lax.ppermute(y_val, 'pp', fwd_perm)
 
-        d_norm = (combine(pb_near) + ret_b).astype(bf16)
-        d_mid = bwd_dy + norm_back(d_norm)[0]
-        d_hidden = jnp.einsum('th,fh->tf', d_mid, stage_w_out, preferred_element_type=f32).astype(bf16)
-        _, dense_back = jax.vjp(dense_act, pre_b)
-        d_pre = dense_back(d_hidden)[0]
-        d_norm_in = jnp.einsum('tf,hf->th', d_pre, stage_w_in, preferred_element_type=f32).astype(bf16)
-        _, norm_in_back = jax.vjp(rms_norm, bwd_x)
-        dx_val = d_mid + norm_in_back(d_norm_in)[0]
-        dx_prev = lax.ppermute(dx_val, 'pp', bwd_perm)
+        dx_parts = []
+        from_mate = to_mate(pb_near[1])
+        for c in range(TAIL):
+            dx_val = run_tail(c, pb_near[0], from_mate, ret_b, mid_b, bwd_dy, bwd_x, pre_b, stage_w_in, stage_w_out)
+            dx_parts.append(lax.ppermute(dx_val, 'pp', bwd_perm))
+        dx_prev = jnp.concatenate(dx_parts)
 
         back = [to_mate(v) for v in dw_mate]
         zero = jnp.zeros((), i32)

time: 739 us -> 796 us (1.077)
  waiting for transfers between devices: 144 us -> 261 us
  blocking collectives: 52.2 us -> 0 us
  Pallas kernels: 264 us -> 291 us
  matrix products: 25.7 us -> 0 us
  starting transfers between devices: 182 us -> 197 us
  other arithmetic: 35.8 us -> 21.7 us
  local copies, waits for them, and re-layouts: 29.3 us -> 17.3 us
    ppermute x5 -> x6, waiting for transfers between devices: 113 us -> 220 us  [to_cross(): return lax.ppermute(v, 'ep', [(i, i ^ 2) for i in range(n_ep)])]
    all_gather x1 -> x0, blocking collectives: 52.2 us -> none  [device_fn(): table = lax.all_gather(jnp.concatenate(fields), 'ep')]
    pallas_call x0 -> x6, Pallas kernels: none -> 48.3 us  [the longest x4 27.1 us: run_tail(): pl.pallas_call(tail_kernel, grid=(steps,), out_shape=jax.ShapeDtypeStruct...]
    dot_general x4 -> x0, matrix products: 25.7 us -> none  [the longest x2 12.2 us: dense_fwd(): jnp.dot(dense_act(pre_act), stage_w_out, preferred_element_type=f32)]
    ppermute x16 -> x17, waiting for transfers between devices: 0.04 us -> 22.9 us  [to_mate(): return lax.ppermute(v, 'ep', [(i, i ^ 1) for i in range(n_ep)])]
    pallas_call x4, Pallas kernels: 260 us -> 238 us  [run_experts(): pl.pallas_call(functools.partial(expert_kernel, bwd, carry, E_RUN if far...]
    ppermute x1 -> x5, waiting for transfers between devices: 30.9 us -> 18.3 us  [the longest x4 18.2 us: device_fn(): dx_parts.append(lax.ppermute(dx_val, 'pp', bwd_perm))]
    ppermute x1 -> x5, starting transfers between devices: 48.5 us -> 54.8 us  [the longest x4 54.5 us: device_fn(): dx_parts.append(lax.ppermute(dx_val, 'pp', bwd_perm))]
  transfers between devices with their start and end apart: 23 -> 29, of which waited for: 4 -> 8; matrix products, arithmetic and copies ran while one was open for 10% -> 5% of each run, Pallas kernels for 36% -> 36%
where the time goes in v3:
time: 796 us; the launch traced here: 789 us
  Pallas kernels  291 us (37%)
  waiting for transfers between devices  261 us (33%)
  starting transfers between devices  197 us (25%)
  other arithmetic  21.7 us (3%)
  local copies, waits for them, and re-layouts  17.3 us (2%)
    pallas_call x4, Pallas kernels, run_experts(): pl.pallas_call(functools.partial(expert_kernel, bwd, carry, E_RUN if far...  238 us
    ppermute x6, waiting for transfers between devices, to_cross(): return lax.ppermute(v, 'ep', [(i, i ^ 2) for i in range(n_ep)])  220 us
    ppermute x6, starting transfers between devices, to_cross(): return lax.ppermute(v, 'ep', [(i, i ^ 2) for i in range(n_ep)])  82.6 us
    ppermute x4, starting transfers between devices, device_fn(): dx_parts.append(lax.ppermute(dx_val, 'pp', bwd_perm))  54.5 us
    ppermute x1, starting transfers between devices, device_fn(): y_next = lax.ppermute(y_val, 'pp', fwd_perm)  52 us
    pallas_call x4, Pallas kernels, run_tail(): pl.pallas_call(tail_kernel, grid=(steps,), out_shape=jax.ShapeDtypeStruct...  27.1 us
    ppermute x17, waiting for transfers between devices, to_mate(): return lax.ppermute(v, 'ep', [(i, i ^ 1) for i in range(n_ep)])  22.9 us
    pallas_call x2, Pallas kernels, run_dense(): pl.pallas_call(dense_kernel, grid=(n_tok // DENSE_ROWS,), out_shape=out_s...  21.2 us
  transfers between devices with their start and end apart: 29, of which 8 were waited for; matrix products, arithmetic and copies ran while one was open for 5% of the time, Pallas kernels for 36%

profile of v3, /device:TPU:0, one launch (start us, length us, event | category | flops | bytes accessed | tf_op | source)
XLA Modules:
  0.0 789.0 jit_solution(4331667042644149046)
XLA Ops:
  0.7 10.8 %dense_fwd.3 = (bf16[2048,512]{1,0:T(8,128)(2,1)}, bf16[2048,512]{1,0:T(8,128)(2,1)}, bf16[2048,1280]{1,0:T(8,128)(2,1)}) custom-call(bf16[2048,512]{1,0:T(8,128)(2,1)} %bitcast.43, bf16[512,1280]{1,0:T(8,128)(2,1)} %bitcast.55, bf16[1280,512]{1,0:T(8,128)(2,1)} %bitcast.61), custom_call_target="tpu_custom_call" | custom-call | flops 5368709120 | bytes 12000000 | tf_op jit(solution)/shard_map/dense_fwd/pallas_call | solution.py:360
  11.5 3.3 collective-permute-start.15
  15.9 22.9 %collective-permute-done.tab1 = f32[16,2048]{1,0:T(8,128)S(1)} collective-permute-done((f32[16,2048]{1,0:T(8,128)S(1)}, f32[16,2048]{1,0:T(8,128)S(1)}, u32[]{:S(2)}, u32[]{:S(2)}) %collective-permute-start) | collective-permute-done | bytes 131104 | tf_op jit(solution)/shard_map/ppermute | solution.py:470
  38.9 24.6 %collective-permute-done.1.tab2 = f32[16,2048]{1,0:T(8,128)S(1)} collective-permute-done((f32[16,2048]{1,0:T(8,128)S(1)}, f32[16,2048]{1,0:T(8,128)S(1)}, u32[]{:S(2)}, u32[]{:S(2)}) %collective-permute-start.1) | collective-permute-done | bytes 131104 | tf_op jit(solution)/shard_map/ppermute | solution.py:473
  63.7 10.4 %dense_fwd.2 = (bf16[2048,512]{1,0:T(8,128)(2,1)}, bf16[2048,512]{1,0:T(8,128)(2,1)}) custom-call(bf16[2048,512]{1,0:T(8,128)(2,1)} %bitcast.86, bf16[512,1280]{1,0:T(8,128)(2,1)} %bitcast.56, bf16[1280,512]{1,0:T(8,128)(2,1)} %bitcast.62), custom_call_target="tpu_custom_call" | custom-call | flops 5368709120 | bytes 12000000 | tf_op jit(solution)/shard_map/dense_fwd/pallas_call | solution.py:360
  76.3 46.0 %collective-permute-done.17.refs_8_ = bf16[2048,512]{1,0:T(8,128)(2,1)} collective-permute-done((bf16[2048,512]{1,0:T(8,128)(2,1)S(1)}, bf16[2048,512]{1,0:T(8,128)(2,1)}, u32[]{:S(2)}, u32[]{:S(2)}) %collective-permute-start.17) | collective-permute-done | bytes 2097184 | tf_op jit(solution)/shard_map/ppermute | solution.py:473
  123.6 43.6 %collective-permute-done.8.refs_6_ = bf16[2048,512]{1,0:T(8,128)(2,1)} collective-permute-done((bf16[2048,512]{1,0:T(8,128)(2,1)}, bf16[2048,512]{1,0:T(8,128)(2,1)}, u32[]{:S(2)}, u32[]{:S(2)}) %collective-permute-start.8) | collective-permute-done | bytes 2097184 | tf_op jit(solution)/shard_map/ppermute | solution.py:473
  168.3 5.3 routing.1
  174.6 59.5 %experts_bwd.2 = (f32[2048,512]{1,0:T(8,128)}, f32[2048,512]{1,0:T(8,128)}, f32[4,512,1280]{2,1,0:T(8,128)}, f32[4,512,1280]{2,1,0:T(8,128)}, f32[4,1280,512]{2,...) custom-call(s32[2,8,128]{2,1,0:T(8,128)} %get-tuple-element.36.refs_0_, ...), custom_call_target="tpu_custom_call" | custom-call | flops 75161927680 | bytes 60000000 | tf_op jit(solution)/shard_map/experts_bwd/pallas_call | solution.py:451
  234.1 59.7 %experts_bwd.3 = (f32[2048,512]{1,0:T(8,128)}, f32[2048,512]{1,0:T(8,128)}, f32[4,512,1280]{2,1,0:T(8,128)}, f32[4,512,1280]{2,1,0:T(8,128)}, f32[4,1280,512]{2,...) custom-call(s32[2,8,128]{2,1,0:T(8,128)} %get-tuple-element.36.refs_0_, ...), custom_call_target="tpu_custom_call" | custom-call | flops 75161927680 | bytes 60000000 | tf_op jit(solution)/shard_map/experts_bwd/pallas_call | solution.py:451
  293.8 1.8 collective-permute-start.28
  295.7 58.7 %experts_fwd.3 = (f32[2048,512]{1,0:T(8,128)}, f32[2048,512]{1,0:T(8,128)}) custom-call(s32[2,8,128]{2,1,0:T(8,128)} %get-tuple-element.36.refs_0_, s32[2,8,128]{2,1,0:T(8,128)} %get-tuple-element.37.refs_1_, s32[2,8,128]{2,1,0:T(8,128)} %get-tuple-element.38.refs_2_, s32[1]{0:T(128)} %bitcast.15.refs_3_, s32[2,2,8,4096]{3,2,1,0:T(8,128)} %get-tuple-element.39.refs_4_, ...), custom_call_target="tpu_custom_call" | custom-call | flops 28185722880 | bytes 60000000 | tf_op jit(solution)/shard_map/experts_fwd/pallas_call | solution.py:451
  354.9 59.7 %experts_fwd.2 = (f32[2048,512]{1,0:T(8,128)}, f32[2048,512]{1,0:T(8,128)}) custom-call(s32[2,8,128]{2,1,0:T(8,128)} %get-tuple-element.36.refs_0_, s32[2,8,128]{2,1,0:T(8,128)} %get-tuple-element.37.refs_1_, s32[2,8,128]{2,1,0:T(8,128)} %get-tuple-element.38.refs_2_, s32[1]{0:T(128)} %bitcast.15.refs_3_, s32[2,2,8,4096]{3,2,1,0:T(8,128)} %get-tuple-element.39.refs_4_, ...), custom_call_target="tpu_custom_call" | custom-call | flops 28185722880 | bytes 60000000 | tf_op jit(solution)/shard_map/experts_fwd/pallas_call | solution.py:451
  415.1 6.7 add.38
  421.8 77.2 %collective-permute-start.11 = (f32[2048,512]{1,0:T(8,128)}, f32[2048,512]{1,0:T(8,128)}, u32[]{:S(2)}, u32[]{:S(2)}) collective-permute-start(f32[2048,512]{1,0:T(8,128)} %add.38), channel_id=1, source_target_pairs={{0,2},{1,3},{2,0},{3,1},{4,6},{5,7},{6,4},{7,5}} | collective-permute-start | bytes 12582920 | tf_op jit(solution)/shard_map/ppermute | solution.py:473
  499.0 5.2 add.41
  504.7 5.6 bitcast_dynamic-update-slice_fusion
  510.3 80.4 %collective-permute-done.11 = f32[2048,512]{1,0:T(8,128)} collective-permute-done((f32[2048,512]{1,0:T(8,128)}, f32[2048,512]{1,0:T(8,128)}, u32[]{:S(2)}, u32[]{:S(2)}) %collective-permute-start.11) | collective-permute-done | bytes 4194336 | tf_op jit(solution)/shard_map/ppermute | solution.py:473
  590.7 6.6 add_convert_fusion
  597.3 52.0 %collective-permute-start.12 = (bf16[2048,512]{1,0:T(8,128)(2,1)}, bf16[2048,512]{1,0:T(8,128)(2,1)S(1)}, u32[]{:S(2)}, u32[]{:S(2)}) collective-permute-start(bf16[2048,512]{1,0:T(8,128)(2,1)} %add_convert_fusion), channel_id=1, source_target_pairs={{0,4},{4,0},{1,5},{5,1},{2,6},{6,2},{3,7},{7,3}} | collective-permute-start | bytes 6291464 | tf_op jit(solution)/shard_map/ppermute | solution.py:526
  649.4 5.2 bitcast_dynamic-update-slice_fusion.1
  654.5 25.4 %collective-permute-done.21.p_far = f32[2048,512]{1,0:T(8,128)} collective-permute-done((f32[2048,512]{1,0:T(8,128)}, f32[2048,512]{1,0:T(8,128)}, u32[]{:S(2)}, u32[]{:S(2)}) %collective-permute-start.21) | collective-permute-done | bytes 4194336 | tf_op jit(solution)/shard_map/ppermute | solution.py:473
  679.9 6.7 shard_map.155
  686.6 52.4 %collective-permute-start.22 = (bf16[512,512]{1,0:T(8,128)(2,1)}, bf16[512,512]{1,0:T(8,128)(2,1)S(1)}, u32[]{:S(2)}, u32[]{:S(2)}) collective-permute-start(bf16[512,512]{1,0:T(8,128)(2,1)} %shard_map.155), channel_id=1, source_target_pairs={{0,4},{4,0},{1,5},{5,1},{2,6},{6,2},{3,7},{7,3}} | collective-permute-start | bytes 1572872 | tf_op jit(solution)/shard_map/ppermute | solution.py:532
  739.1 6.7 shard_map.156
  745.8 7.0 shard_map.157
  752.8 2.0 collective-permute-start.24
  754.7 6.7 shard_map.158
  761.5 5.2 bitcast_dynamic-update-slice_fusion.2
  766.7 7.9 %collective-permute-done.24 = bf16[512,512]{1,0:T(8,128)(2,1)} collective-permute-done((bf16[512,512]{1,0:T(8,128)(2,1)}, bf16[512,512]{1,0:T(8,128)(2,1)}, u32[]{:S(2)}, u32[]{:S(2)}) %collective-permute-start.24) | collective-permute-done | bytes 524320 | tf_op jit(solution)/shard_map/ppermute | solution.py:532
  774.6 10.3 %collective-permute-done.25 = bf16[512,512]{1,0:T(8,128)(2,1)S(1)} collective-permute-done((bf16[512,512]{1,0:T(8,128)(2,1)}, bf16[512,512]{1,0:T(8,128)(2,1)S(1)}, u32[]{:S(2)}, u32[]{:S(2)}) %collective-permute-start.25) | collective-permute-done | bytes 524320 | tf_op jit(solution)/shard_map/ppermute | solution.py:532
  785.0 2.5 maximum_bitcast_fusion
  (73 shorter events, 10.0 us)
Async XLA Ops:
  11.5 64.2 %collective-permute-start.15 = (bf16[2048,512]{1,0:T(8,128)(2,1)}, bf16[2048,512]{1,0:T(8,128)(2,1)}, u32[]{:S(2)}, u32[]{:S(2)}) collective-permute-start(bf16[2048,512]{1,0:T(8,128)(2,1)} %get-tuple-element.46.refs_6_), channel_id=1, source_target_pairs={{0,2},{1,3},{2,0},{3,1},{4,6},{5,7},{6,4},{7,5}} | collective-permute-start | bytes 6291464 | tf_op jit(solution)/shard_map/ppermute | solution.py:473
  14.8 159.3 %collective-permute-start.4 = (bf16[4,512,1280]{2,1,0:T(8,128)(2,1)}, bf16[4,512,1280]{2,1,0:T(8,128)(2,1)}, u32[]{:S(2)}, u32[]{:S(2)}) collective-permute-start(bf16[4,512,1280]{2,1,0:T(8,128)(2,1)} %bitcast.71), channel_id=1, source_target_pairs={{0,1},{1,0},{2,3},{3,2},{4,5},{5,4},{6,7},{7,6}} | collective-permute-start | bytes 15728648 | tf_op jit(solution)/shard_map/ppermute | solution.py:470
  14.8 159.4 %collective-permute-start.5 = (bf16[4,512,1280]{2,1,0:T(8,128)(2,1)}, bf16[4,512,1280]{2,1,0:T(8,128)(2,1)}, u32[]{:S(2)}, u32[]{:S(2)}) collective-permute-start(bf16[4,512,1280]{2,1,0:T(8,128)(2,1)} %bitcast.76), channel_id=1, source_target_pairs={{0,1},{1,0},{2,3},{3,2},{4,5},{5,4},{6,7},{7,6}} | collective-permute-start | bytes 15728648 | tf_op jit(solution)/shard_map/ppermute | solution.py:470
  15.3 159.3 %collective-permute-start.6 = (bf16[4,1280,512]{2,1,0:T(8,128)(2,1)}, bf16[4,1280,512]{2,1,0:T(8,128)(2,1)}, u32[]{:S(2)}, u32[]{:S(2)}) collective-permute-start(bf16[4,1280,512]{2,1,0:T(8,128)(2,1)} %bitcast.81), channel_id=1, source_target_pairs={{0,1},{1,0},{2,3},{3,2},{4,5},{5,4},{6,7},{7,6}} | collective-permute-start | bytes 15728648 | tf_op jit(solution)/shard_map/ppermute | solution.py:470
  15.4 23.4 %collective-permute-start = (f32[16,2048]{1,0:T(8,128)S(1)}, f32[16,2048]{1,0:T(8,128)S(1)}, u32[]{:S(2)}, u32[]{:S(2)}) collective-permute-start(f32[16,2048]{1,0:T(8,128)S(1)} %pad_maximum_fusion.tab0), channel_id=1, source_target_pairs={{0,1},{1,0},{2,3},{3,2},{4,5},{5,4},{6,7},{7,6}} | collective-permute-start | bytes 393224 | tf_op jit(solution)/shard_map/ppermute | solution.py:470
  38.8 24.6 %collective-permute-start.1 = (f32[16,2048]{1,0:T(8,128)S(1)}, f32[16,2048]{1,0:T(8,128)S(1)}, u32[]{:S(2)}, u32[]{:S(2)}) collective-permute-start(f32[16,2048]{1,0:T(8,128)S(1)} %pad_maximum_fusion.tab0), channel_id=1, source_target_pairs={{0,2},{1,3},{2,0},{3,1},{4,6},{5,7},{6,4},{7,5}} | collective-permute-start | bytes 393224 | tf_op jit(solution)/shard_map/ppermute | solution.py:473
  63.4 10.8 %collective-permute-start.2 = (f32[16,2048]{1,0:T(8,128)S(1)}, f32[16,2048]{1,0:T(8,128)S(1)}, u32[]{:S(2)}, u32[]{:S(2)}) collective-permute-start(f32[16,2048]{1,0:T(8,128)S(1)} %pad_maximum_fusion.tab0), channel_id=1, source_target_pairs={{0,3},{1,2},{2,1},{3,0},{4,7},{5,6},{6,5},{7,4}} | collective-permute-start | bytes 393224 | tf_op jit(solution)/shard_map/ppermute | solution.py:496
  74.2 94.1 %copy-start.7 = (f32[16,2048]{1,0:T(8,128)}, f32[16,2048]{1,0:T(8,128)S(1)}, u32[]{:S(2)}) copy-start(f32[16,2048]{1,0:T(8,128)S(1)} %collective-permute-done.2.tab3) | copy-start | bytes 393220
  74.2 48.0 %collective-permute-start.17 = (bf16[2048,512]{1,0:T(8,128)(2,1)S(1)}, bf16[2048,512]{1,0:T(8,128)(2,1)}, u32[]{:S(2)}, u32[]{:S(2)}) collective-permute-start(bf16[2048,512]{1,0:T(8,128)(2,1)S(1)} %bitcast.53), channel_id=1, source_target_pairs={{0,2},{1,3},{2,0},{3,1},{4,6},{5,7},{6,4},{7,5}} | collective-permute-start | bytes 6291464 | tf_op jit(solution)/shard_map/ppermute | solution.py:473
  75.7 91.5 %collective-permute-start.8 = (bf16[2048,512]{1,0:T(8,128)(2,1)}, bf16[2048,512]{1,0:T(8,128)(2,1)}, u32[]{:S(2)}, u32[]{:S(2)}) collective-permute-start(bf16[2048,512]{1,0:T(8,128)(2,1)} %get-tuple-element.41.refs_6_), channel_id=1, source_target_pairs={{0,2},{1,3},{2,0},{3,1},{4,6},{5,7},{6,4},{7,5}} | collective-permute-start | bytes 6291464 | tf_op jit(solution)/shard_map/ppermute | solution.py:473
  122.3 51.3 %collective-permute-start.16 = (bf16[2048,512]{1,0:T(8,128)(2,1)}, bf16[2048,512]{1,0:T(8,128)(2,1)}, u32[]{:S(2)}, u32[]{:S(2)}) collective-permute-start(bf16[2048,512]{1,0:T(8,128)(2,1)} %collective-permute-done.15.refs_6_), channel_id=1, source_target_pairs={{0,1},{1,0},{2,3},{3,2},{4,5},{5,4},{6,7},{7,6}} | collective-permute-start | bytes 6291464 | tf_op jit(solution)/shard_map/ppermute | solution.py:470
  167.2 6.5 collective-permute-start.18
  173.6 60.5 %collective-permute-start.13 = (bf16[2048,512]{1,0:T(8,128)(2,1)}, bf16[2048,512]{1,0:T(8,128)(2,1)}, u32[]{:S(2)}, u32[]{:S(2)}) collective-permute-start(bf16[2048,512]{1,0:T(8,128)(2,1)} %get-tuple-element.46.refs_6_), channel_id=1, source_target_pairs={{0,1},{1,0},{2,3},{3,2},{4,5},{5,4},{6,7},{7,6}} | collective-permute-start | bytes 6291464 | tf_op jit(solution)/shard_map/ppermute | solution.py:470
  173.7 60.4 %collective-permute-start.14 = (bf16[2048,512]{1,0:T(8,128)(2,1)S(1)}, bf16[2048,512]{1,0:T(8,128)(2,1)}, u32[]{:S(2)}, u32[]{:S(2)}) collective-permute-start(bf16[2048,512]{1,0:T(8,128)(2,1)S(1)} %bitcast.54), channel_id=1, source_target_pairs={{0,1},{1,0},{2,3},{3,2},{4,5},{5,4},{6,7},{7,6}} | collective-permute-start | bytes 6291464 | tf_op jit(solution)/shard_map/ppermute | solution.py:470
  174.1 180.8 %collective-permute-start.3 = (bf16[2048,512]{1,0:T(8,128)(2,1)}, bf16[2048,512]{1,0:T(8,128)(2,1)}, u32[]{:S(2)}, u32[]{:S(2)}) collective-permute-start(bf16[2048,512]{1,0:T(8,128)(2,1)} %get-tuple-element.41.refs_6_), channel_id=1, source_target_pairs={{0,1},{1,0},{2,3},{3,2},{4,5},{5,4},{6,7},{7,6}} | collective-permute-start | bytes 6291464 | tf_op jit(solution)/shard_map/ppermute | solution.py:470
  174.2 121.5 %collective-permute-start.9 = (bf16[2048,512]{1,0:T(8,128)(2,1)}, bf16[2048,512]{1,0:T(8,128)(2,1)}, u32[]{:S(2)}, u32[]{:S(2)}) collective-permute-start(bf16[2048,512]{1,0:T(8,128)(2,1)} %collective-permute-done.8.refs_6_), channel_id=1, source_target_pairs={{0,1},{1,0},{2,3},{3,2},{4,5},{5,4},{6,7},{7,6}} | collective-permute-start | bytes 6291464 | tf_op jit(solution)/shard_map/ppermute | solution.py:470
  293.8 210.9 %collective-permute-start.28 = (f32[2,1280,512]{2,1,0:T(8,128)}, f32[2,1280,512]{2,1,0:T(8,128)}, u32[]{:S(2)}, u32[]{:S(2)}) collective-permute-start(f32[2,1280,512]{2,1,0:T(8,128)} %get-tuple-element.64), channel_id=1, source_target_pairs={{0,1},{1,0},{2,3},{3,2},{4,5},{5,4},{6,7},{7,6}} | collective-permute-start | bytes 15728648 | tf_op jit(solution)/shard_map/ppermute | solution.py:470
  295.6 203.4 %collective-permute-start.20 = (f32[2048,512]{1,0:T(8,128)}, f32[2048,512]{1,0:T(8,128)}, u32[]{:S(2)}, u32[]{:S(2)}) collective-permute-start(f32[2048,512]{1,0:T(8,128)} %get-tuple-element.56), channel_id=1, source_target_pairs={{0,1},{1,0},{2,3},{3,2},{4,5},{5,4},{6,7},{7,6}} | collective-permute-start | bytes 12582920 | tf_op jit(solution)/shard_map/ppermute | solution.py:470
  354.4 60.7 %collective-permute-start.10 = (f32[2048,512]{1,0:T(8,128)}, f32[2048,512]{1,0:T(8,128)}, u32[]{:S(2)}, u32[]{:S(2)}) collective-permute-start(f32[2048,512]{1,0:T(8,128)} %get-tuple-element.45), channel_id=1, source_target_pairs={{0,1},{1,0},{2,3},{3,2},{4,5},{5,4},{6,7},{7,6}} | collective-permute-start | bytes 12582920 | tf_op jit(solution)/shard_map/ppermute | solution.py:470
  414.6 89.6 %collective-permute-start.7 = (f32[2048,512]{1,0:T(8,128)}, f32[2048,512]{1,0:T(8,128)}, u32[]{:S(2)}, u32[]{:S(2)}) collective-permute-start(f32[2048,512]{1,0:T(8,128)} %get-tuple-element.43), channel_id=1, source_target_pairs={{0,1},{1,0},{2,3},{3,2},{4,5},{5,4},{6,7},{7,6}} | collective-permute-start | bytes 12582920 | tf_op jit(solution)/shard_map/ppermute | solution.py:470
  414.6 234.8 %collective-permute-start.27 = (f32[2,512,1280]{2,1,0:T(8,128)}, f32[2,512,1280]{2,1,0:T(8,128)}, u32[]{:S(2)}, u32[]{:S(2)}) collective-permute-start(f32[2,512,1280]{2,1,0:T(8,128)} %get-tuple-element.62), channel_id=1, source_target_pairs={{0,1},{1,0},{2,3},{3,2},{4,5},{5,4},{6,7},{7,6}} | collective-permute-start | bytes 15728648 | tf_op jit(solution)/shard_map/ppermute | solution.py:470
  421.8 168.9 %collective-permute-start.11 = (f32[2048,512]{1,0:T(8,128)}, f32[2048,512]{1,0:T(8,128)}, u32[]{:S(2)}, u32[]{:S(2)}) collective-permute-start(f32[2048,512]{1,0:T(8,128)} %add.38), channel_id=1, source_target_pairs={{0,2},{1,3},{2,0},{3,1},{4,6},{5,7},{6,4},{7,5}} | collective-permute-start | bytes 12582920 | tf_op jit(solution)/shard_map/ppermute | solution.py:473
  499.0 262.5 %collective-permute-start.26 = (f32[2,512,1280]{2,1,0:T(8,128)}, f32[2,512,1280]{2,1,0:T(8,128)}, u32[]{:S(2)}, u32[]{:S(2)}) collective-permute-start(f32[2,512,1280]{2,1,0:T(8,128)} %get-tuple-element.60), channel_id=1, source_target_pairs={{0,1},{1,0},{2,3},{3,2},{4,5},{5,4},{6,7},{7,6}} | collective-permute-start | bytes 15728648 | tf_op jit(solution)/shard_map/ppermute | solution.py:470
  504.2 150.4 %collective-permute-start.19 = (f32[2048,512]{1,0:T(8,128)}, f32[2048,512]{1,0:T(8,128)}, u32[]{:S(2)}, u32[]{:S(2)}) collective-permute-start(f32[2048,512]{1,0:T(8,128)} %get-tuple-element.54), channel_id=1, source_target_pairs={{0,1},{1,0},{2,3},{3,2},{4,5},{5,4},{6,7},{7,6}} | collective-permute-start | bytes 12582920 | tf_op jit(solution)/shard_map/ppermute | solution.py:470
  504.7 175.3 %collective-permute-start.21 = (f32[2048,512]{1,0:T(8,128)}, f32[2048,512]{1,0:T(8,128)}, u32[]{:S(2)}, u32[]{:S(2)}) collective-permute-start(f32[2048,512]{1,0:T(8,128)} %add.41), channel_id=1, source_target_pairs={{0,2},{1,3},{2,0},{3,1},{4,6},{5,7},{6,4},{7,5}} | collective-permute-start | bytes 12582920 | tf_op jit(solution)/shard_map/ppermute | solution.py:473
  504.7 86.0 %copy-start.2 = (f32[2048,512]{1,0:T(8,128)S(1)}, f32[2048,512]{1,0:T(8,128)}, u32[]{:S(2)}) copy-start(f32[2048,512]{1,0:T(8,128)} %get-tuple-element.42) | copy-start | bytes 12582916
  504.7 86.0 %copy-start.3 = (bf16[2048,512]{1,0:T(8,128)(2,1)S(1)}, bf16[2048,512]{1,0:T(8,128)(2,1)}, u32[]{:S(2)}) copy-start(bf16[2048,512]{1,0:T(8,128)(2,1)} %get-tuple-element.35) | copy-start | bytes 6291460
  597.3 190.1 %collective-permute-start.12 = (bf16[2048,512]{1,0:T(8,128)(2,1)}, bf16[2048,512]{1,0:T(8,128)(2,1)S(1)}, u32[]{:S(2)}, u32[]{:S(2)}) collective-permute-start(bf16[2048,512]{1,0:T(8,128)(2,1)} %add_convert_fusion), channel_id=1, source_target_pairs={{0,4},{4,0},{1,5},{5,1},{2,6},{6,2},{3,7},{7,3}} | collective-permute-start | bytes 6291464 | tf_op jit(solution)/shard_map/ppermute | solution.py:526
  686.6 80.1 %collective-permute-start.22 = (bf16[512,512]{1,0:T(8,128)(2,1)}, bf16[512,512]{1,0:T(8,128)(2,1)S(1)}, u32[]{:S(2)}, u32[]{:S(2)}) collective-permute-start(bf16[512,512]{1,0:T(8,128)(2,1)} %shard_map.155), channel_id=1, source_target_pairs={{0,4},{4,0},{1,5},{5,1},{2,6},{6,2},{3,7},{7,3}} | collective-permute-start | bytes 1572872 | tf_op jit(solution)/shard_map/ppermute | solution.py:532
  745.8 20.9 %collective-permute-start.23 = (bf16[512,512]{1,0:T(8,128)(2,1)}, bf16[512,512]{1,0:T(8,128)(2,1)S(1)}, u32[]{:S(2)}, u32[]{:S(2)}) collective-permute-start(bf16[512,512]{1,0:T(8,128)(2,1)} %shard_map.156), channel_id=1, source_target_pairs={{0,4},{4,0},{1,5},{5,1},{2,6},{6,2},{3,7},{7,3}} | collective-permute-start | bytes 1572872 | tf_op jit(solution)/shard_map/ppermute | solution.py:532
  752.8 21.9 %collective-permute-start.24 = (bf16[512,512]{1,0:T(8,128)(2,1)}, bf16[512,512]{1,0:T(8,128)(2,1)}, u32[]{:S(2)}, u32[]{:S(2)}) collective-permute-start(bf16[512,512]{1,0:T(8,128)(2,1)} %shard_map.157), channel_id=1, source_target_pairs={{0,4},{4,0},{1,5},{5,1},{2,6},{6,2},{3,7},{7,3}} | collective-permute-start | bytes 1572872 | tf_op jit(solution)/shard_map/ppermute | solution.py:532
  761.4 23.5 %collective-permute-start.25 = (bf16[512,512]{1,0:T(8,128)(2,1)}, bf16[512,512]{1,0:T(8,128)(2,1)S(1)}, u32[]{:S(2)}, u32[]{:S(2)}) collective-permute-start(bf16[512,512]{1,0:T(8,128)(2,1)} %shard_map.158), channel_id=1, source_target_pairs={{0,4},{4,0},{1,5},{5,1},{2,6},{6,2},{3,7},{7,3}} | collective-permute-start | bytes 1572872 | tf_op jit(solution)/shard_map/ppermute | solution.py:532
  (9 other events, 257.9 us)

commit v4 on v3

--- a/solution.py
+++ b/solution.py
@@ -12,9 +12,10 @@
 SUB = 128
 TILE_SUBS = (3, 4)
 WIN = 256
-WIN_MORE = 768
+WIN_MORE = 1536
 ALIGN = 64
 CHUNK = 256
+OUT_ROWS = 512
 DW_SLOTS = 3
 TAIL = 4
 DENSE_ROWS = 512
@@ -55,7 +56,7 @@
     dw_in = take(6) if carry else []
     p_out = take(2)
     dw_out = take(6) if bwd else []
-    tok, acc, wg_buf, wu_buf, wd_buf, x_acc, out_all = take(7)
+    order, tok, acc, wg_buf, wu_buf, wd_buf, x_acc, out_all = take(8)
     if bwd:
         dyt, d_acc, xt, dg_all, du_all, dwg_buf, dwu_buf, dwd_buf = take(8)
         tok_sem, w_sem, in_sem, out_sem = take(4)
@@ -112,10 +113,27 @@
 
         return start, wait
 
-    w_start(0, 0)
+    tiles_of = [ntiles[mb, row0 + e, 0] for e in range(E_RUN)]
+    for e in range(E_RUN):
+        rank = 0
+        for o in range(E_RUN):
+            if o != e:
+                ahead = tiles_of[o] >= tiles_of[e] if o < e else tiles_of[o] > tiles_of[e]
+                rank = rank + ahead.astype(i32)
+        place = jnp.where(rank == 0, 0, jnp.where(rank == 1, E_RUN - 1, rank - 1))
+        order[place] = e
+
+    def clear(ref):
+        rows = 64
+
+        @pl.loop(0, ref.shape[0] // rows)
+        def _(k):
+            ref[pl.ds(pl.multiple_of(k * rows, rows), rows), :] = jnp.zeros((rows, ref.shape[1]), ref.dtype)
+
+    w_start(order[0], 0)
     if carry:
-        dw_copies(dw_in, 0, 0, in_sem, True)[0]()
-    acc[...] = jnp.zeros_like(acc)
+        dw_copies(dw_in, order[0], 0, in_sem, True)[0]()
+    clear(acc)
     for c in loads:
         c.wait()
 
@@ -135,33 +153,41 @@
         return toks, lambda: jnp.where(mask, 1.0, 0.0).astype(bf16), \
             lambda: jnp.where(mask, gate_ref[mb, shift, pl.ds(row0 + e, 1), lanes], 0.0).astype(bf16)
 
-    def expert(e, _):
-        slot = lax.rem(e, 2)
+    def p_copy(q):
+        per = half // OUT_ROWS
+        for j in range(2):
+            @pl.when(q // per == j)
+            def _():
+                dst = p_out[j].at[pl.ds(pl.multiple_of((q - j * per) * OUT_ROWS, OUT_ROWS), OUT_ROWS), :]
+                pltpu.make_async_copy(acc.at[pl.ds(pl.multiple_of(q * OUT_ROWS, OUT_ROWS), OUT_ROWS), :], dst, tok_sem.at[0, j]).start()
+
+    def expert(i, _):
+        e = order[i]
+        slot = lax.rem(i, 2)
         for c in w_copies(w_own, 0, slot):
             c.wait()
 
-        @pl.when(e < E_RUN - 1)
+        @pl.when(i < E_RUN - 1)
         def _():
-            w_start(e + 1, 1 - slot)
+            w_start(order[i + 1], 1 - slot)
 
         wg, wu, wd = wg_buf.at[slot], wu_buf.at[slot], wd_buf.at[slot]
         if bwd:
-            d_slot = lax.rem(e, DW_SLOTS)
-
-            @pl.when(e >= 2)
-            def _():
-                old = e - 2
-                dw_copies(dw_out, old, lax.rem(old, DW_SLOTS), out_sem, False)[1]()
+            d_slot = lax.rem(i, DW_SLOTS)
+
+            @pl.when(i >= 2)
+            def _():
+                dw_copies(dw_out, 0, lax.rem(i - 2, DW_SLOTS), out_sem, False)[1]()
 
             if carry:
-                @pl.when(e < E_RUN - 1)
+                @pl.when(i < E_RUN - 1)
                 def _():
-                    dw_copies(dw_in, e + 1, lax.rem(e + 1, DW_SLOTS), in_sem, True)[0]()
+                    dw_copies(dw_in, order[i + 1], lax.rem(i + 1, DW_SLOTS), in_sem, True)[0]()
 
                 dw_copies(dw_in, e, d_slot, in_sem, True)[1]()
             else:
                 for b in (dwg_buf, dwu_buf, dwd_buf):
-                    b[d_slot] = jnp.zeros(b.shape[1:], f32)
+                    clear(b.at[d_slot])
             dwg, dwu, dwd = dwg_buf.at[d_slot], dwu_buf.at[d_slot], dwd_buf.at[d_slot]
 
         def tile(t, _):
@@ -172,17 +198,23 @@
                 if bwd:
                     d_acc[rows, :] = dot_nn(gated(), dyt[toks, :])
 
-            @pl.loop(0, per_tile)
-            def _(h):
-                st = t * per_tile + h
-                rows = pl.ds(pl.multiple_of(h * SUB, SUB), SUB)
-
-                @pl.loop(1, nwins[mb, row0 + e, st])
-                def _(k):
-                    toks, ones, gated = window(e, st, k)
-                    x_acc[rows, :] += dot_nn(ones(), tok[toks, :])
-                    if bwd:
-                        d_acc[rows, :] += dot_nn(gated(), dyt[toks, :])
+            n_win = nwins[mb, row0 + e, t * per_tile]
+            for h in range(1, per_tile):
+                n_win = jnp.maximum(n_win, nwins[mb, row0 + e, t * per_tile + h])
+
+            @pl.when(n_win > 1)
+            def _():
+                @pl.loop(0, per_tile)
+                def _(h):
+                    st = t * per_tile + h
+                    rows = pl.ds(pl.multiple_of(h * SUB, SUB), SUB)
+
+                    @pl.loop(1, nwins[mb, row0 + e, st])
+                    def _(k):
+                        toks, ones, gated = window(e, st, k)
+                        x_acc[rows, :] += dot_nn(ones(), tok[toks, :])
+                        if bwd:
+                            d_acc[rows, :] += dot_nn(gated(), dyt[toks, :])
 
             x = x_acc[...].astype(bf16)
             if bwd:
@@ -219,13 +251,27 @@
             for h in range(per_tile):
                 put(t * per_tile + h, None, out[h * SUB:(h + 1) * SUB, :])
 
-            @pl.loop(0, per_tile)
-            def _(h):
-                st = t * per_tile + h
-
-                @pl.loop(1, nwins[mb, row0 + e, st])
-                def _(k):
-                    put(st, k, out_all[pl.ds(pl.multiple_of(h * SUB, SUB), SUB), :])
+            @pl.when(n_win > 1)
+            def _():
+                @pl.loop(0, per_tile)
+                def _(h):
+                    st = t * per_tile + h
+
+                    @pl.loop(1, nwins[mb, row0 + e, st])
+                    def _(k):
+                        put(st, k, out_all[pl.ds(pl.multiple_of(h * SUB, SUB), SUB), :])
+
+            @pl.when(i == E_RUN - 1)
+            def _():
+                def final(tile_idx):
+                    return jnp.minimum(starts[mb, row0 + e, tile_idx * per_tile], n_tok - WIN_MORE) // OUT_ROWS
+
+                lo = jnp.where(t == 0, 0, final(t))
+                hi = jnp.where(t == ntiles[mb, row0 + e, 0] - 1, n_tok // OUT_ROWS, final(t + 1))
+
+                @pl.loop(lo, hi)
+                def _(q):
+                    p_copy(q)
 
             return 0
 
@@ -236,8 +282,6 @@
 
     lax.fori_loop(0, E_RUN, expert, 0)
     outs = [pltpu.make_async_copy(acc.at[pl.ds(j * half, half), :], p_out[j], tok_sem.at[0, j]) for j in range(2)]
-    for c in outs:
-        c.start()
     if bwd:
         for e in (E_RUN - 2, E_RUN - 1):
             dw_copies(dw_out, e, e % DW_SLOTS, out_sem, False)[1]()
@@ -334,15 +378,18 @@
     return (scale * cot - rows_f32 * (scale * scale * scale * proj)).astype(bf16)
 
 
-def dense_kernel(x_ref, w_in, w_out, norm_ref, mid_ref, *pre_ref):
+def dense_kernel(x_ref, w_in, w_out, norm_ref, mid_ref, *rest):
+    *pre_ref, hid = rest
     x = x_ref[...].astype(f32)
     norm_in = (x * rms_scale(x)).astype(bf16)
-    pre = dot_nn(norm_in, w_in[...]).astype(bf16)
-    if pre_ref:
-        pre_ref[0][...] = pre
-    pre = pre.astype(f32)
-    hid = (pre * sigmoid(pre)).astype(bf16)
-    mid = (x + dot_nn(hid, w_out[...])).astype(bf16)
+    for c in range(0, w_in.shape[1], CHUNK):
+        cols = pl.ds(c, CHUNK)
+        pre = dot_nn(norm_in, w_in[:, cols]).astype(bf16)
+        if pre_ref:
+            pre_ref[0][:, cols] = pre
+        pre = pre.astype(f32)
+        hid[:, cols] = (pre * sigmoid(pre)).astype(bf16)
+    mid = (x_ref[...].astype(f32) + dot_nn(hid[...], w_out[...])).astype(bf16)
     mid_ref[...] = mid
     mid = mid.astype(f32)
     norm_ref[...] = (mid * rms_scale(mid)).astype(bf16)
@@ -363,19 +410,22 @@
         out_shape=out_shape,
         in_specs=[row, pl.BlockSpec((width, ff), lambda i: (0, 0)), pl.BlockSpec((ff, width), lambda i: (0, 0))],
         out_specs=out_specs,
+        scratch_shapes=[pltpu.VMEM((DENSE_ROWS, ff), bf16)],
         cost_estimate=pl.CostEstimate(flops=4 * n_tok * width * ff, bytes_accessed=12_000_000, transcendentals=0),
         name='dense_fwd',
     )(x, w_in, w_out)
 
 
-def tail_kernel(p_own, p_mate, p_far, mid_ref, dy_ref, x_ref, pre_ref, w_in, w_out, dx_ref):
+def tail_kernel(p_own, p_mate, p_far, mid_ref, dy_ref, x_ref, pre_ref, w_in, w_out, dx_ref, d_all):
     d_norm = (p_own[...] + p_mate[...] + p_far[...]).astype(bf16)
     d_mid = (dy_ref[...].astype(f32) + rms_back(mid_ref[...].astype(f32), d_norm).astype(f32)).astype(bf16)
-    d_hid = dot_nt(d_mid, w_out[...]).astype(bf16).astype(f32)
-    pre = pre_ref[...].astype(f32)
-    sig = sigmoid(pre)
-    d_pre = (d_hid * (sig + pre * sig * (1.0 - sig))).astype(bf16)
-    d_in = dot_nt(d_pre, w_in[...]).astype(bf16)
+    for c in range(0, w_in.shape[1], CHUNK):
+        cols = pl.ds(c, CHUNK)
+        d_hid = dot_nt(d_mid, w_out[cols, :]).astype(bf16).astype(f32)
+        pre = pre_ref[:, cols].astype(f32)
+        sig = sigmoid(pre)
+        d_all[:, cols] = (d_hid * (sig + pre * sig * (1.0 - sig))).astype(bf16)
+    d_in = dot_nt(d_all[...], w_in[...]).astype(bf16)
     dx_ref[...] = (d_mid.astype(f32) + rms_back(x_ref[...].astype(f32), d_in).astype(f32)).astype(bf16)
 
 
@@ -392,6 +442,7 @@
         in_specs=[row] * 6 + [pl.BlockSpec((rows, ff), lambda i: (chunk * steps + i, 0)),
                               pl.BlockSpec((width, ff), lambda i: (0, 0)), pl.BlockSpec((ff, width), lambda i: (0, 0))],
         out_specs=pl.BlockSpec((rows, width), lambda i: (i, 0)),
+        scratch_shapes=[pltpu.VMEM((rows, ff), bf16)],
         cost_estimate=pl.CostEstimate(flops=4 * rows * steps * width * ff, bytes_accessed=6_000_000, transcendentals=0),
     )(p_own, p_mate, p_far, mid, dy, x, pre, w_in, w_out)
 
@@ -418,6 +469,7 @@
             out_shape += [jax.ShapeDtypeStruct((n, *w.shape[1:]), f32) for w in w_own]
     rows = SUB * TILE_SUBS[int(bwd)]
     scratch = [
+        pltpu.SMEM((E_RUN,), i32),
         pltpu.VMEM((2 * half, width), bf16),
         pltpu.VMEM((2 * half, width), f32),
         pltpu.VMEM((2, width, ff), bf16),

time: 796 us -> 779 us (0.979)
  Pallas kernels: 291 us -> 279 us
    pallas_call x4, Pallas kernels: 238 us -> 225 us  [run_experts(): pl.pallas_call(functools.partial(expert_kernel, bwd, carry, E_RUN if far...]
  transfers between devices with their start and end apart: 29 -> 29, of which waited for: 8 -> 8; matrix products, arithmetic and copies ran while one was open for 5% -> 5% of each run, Pallas kernels for 36% -> 35%
where the time goes in v4:
time: 779 us; the launch traced here: 773 us
  Pallas kernels  279 us (36%)
  waiting for transfers between devices  263 us (34%)
  starting transfers between devices  191 us (25%)
  other arithmetic  21.7 us (3%)
  local copies, waits for them, and re-layouts  17.3 us (2%)
    pallas_call x4, Pallas kernels, run_experts(): pl.pallas_call(functools.partial(expert_kernel, bwd, carry, E_RUN if far...  225 us
    ppermute x6, waiting for transfers between devices, to_cross(): return lax.ppermute(v, 'ep', [(i, i ^ 2) for i in range(n_ep)])  222 us
    ppermute x6, starting transfers between devices, to_cross(): return lax.ppermute(v, 'ep', [(i, i ^ 2) for i in range(n_ep)])  82.1 us
    ppermute x4, starting transfers between devices, device_fn(): dx_parts.append(lax.ppermute(dx_val, 'pp', bwd_perm))  52.8 us
    ppermute x1, starting transfers between devices, device_fn(): y_next = lax.ppermute(y_val, 'pp', fwd_perm)  50.3 us
    pallas_call x4, Pallas kernels, run_tail(): pl.pallas_call(tail_kernel, grid=(steps,), out_shape=jax.ShapeDtypeStruct...  27.1 us
    ppermute x17, waiting for transfers between devices, to_mate(): return lax.ppermute(v, 'ep', [(i, i ^ 1) for i in range(n_ep)])  22.9 us
    pallas_call x2, Pallas kernels, run_dense(): pl.pallas_call(dense_kernel, grid=(n_tok // DENSE_ROWS,), out_shape=out_s...  21.3 us
  transfers between devices with their start and end apart: 29, of which 8 were waited for; matrix products, arithmetic and copies ran while one was open for 5% of the time, Pallas kernels for 35%

profile of v4, /device:TPU:0, one launch (start us, length us, event | category | flops | bytes accessed | tf_op | source)
XLA Modules:
  0.0 772.7 jit_solution(839838981192828899)
XLA Ops:
  0.7 10.8 %dense_fwd.3 = (bf16[2048,512]{1,0:T(8,128)(2,1)}, bf16[2048,512]{1,0:T(8,128)(2,1)}, bf16[2048,1280]{1,0:T(8,128)(2,1)}) custom-call(bf16[2048,512]{1,0:T(8,128)(2,1)} %bitcast.43, bf16[512,1280]{1,0:T(8,128)(2,1)} %bitcast.55, bf16[1280,512]{1,0:T(8,128)(2,1)} %bitcast.61), custom_call_target="tpu_custom_call" | custom-call | flops 5368709120 | bytes 12000000 | tf_op jit(solution)/shard_map/dense_fwd/pallas_call | solution.py:407
  11.5 3.3 collective-permute-start.15
  16.0 22.9 %collective-permute-done.tab1 = f32[16,2048]{1,0:T(8,128)S(1)} collective-permute-done((f32[16,2048]{1,0:T(8,128)S(1)}, f32[16,2048]{1,0:T(8,128)S(1)}, u32[]{:S(2)}, u32[]{:S(2)}) %collective-permute-start) | collective-permute-done | bytes 131104 | tf_op jit(solution)/shard_map/ppermute | solution.py:522
  38.9 24.6 %collective-permute-done.1.tab2 = f32[16,2048]{1,0:T(8,128)S(1)} collective-permute-done((f32[16,2048]{1,0:T(8,128)S(1)}, f32[16,2048]{1,0:T(8,128)S(1)}, u32[]{:S(2)}, u32[]{:S(2)}) %collective-permute-start.1) | collective-permute-done | bytes 131104 | tf_op jit(solution)/shard_map/ppermute | solution.py:525
  63.8 10.5 %dense_fwd.2 = (bf16[2048,512]{1,0:T(8,128)(2,1)}, bf16[2048,512]{1,0:T(8,128)(2,1)}) custom-call(bf16[2048,512]{1,0:T(8,128)(2,1)} %bitcast.86, bf16[512,1280]{1,0:T(8,128)(2,1)} %bitcast.56, bf16[1280,512]{1,0:T(8,128)(2,1)} %bitcast.62), custom_call_target="tpu_custom_call" | custom-call | flops 5368709120 | bytes 12000000 | tf_op jit(solution)/shard_map/dense_fwd/pallas_call | solution.py:407
  74.3 1.4 collective-permute-start.17
  76.3 46.0 %collective-permute-done.17.refs_8_ = bf16[2048,512]{1,0:T(8,128)(2,1)} collective-permute-done((bf16[2048,512]{1,0:T(8,128)(2,1)S(1)}, bf16[2048,512]{1,0:T(8,128)(2,1)}, u32[]{:S(2)}, u32[]{:S(2)}) %collective-permute-start.17) | collective-permute-done | bytes 2097184 | tf_op jit(solution)/shard_map/ppermute | solution.py:525
  123.6 43.7 %collective-permute-done.8.refs_6_ = bf16[2048,512]{1,0:T(8,128)(2,1)} collective-permute-done((bf16[2048,512]{1,0:T(8,128)(2,1)}, bf16[2048,512]{1,0:T(8,128)(2,1)}, u32[]{:S(2)}, u32[]{:S(2)}) %collective-permute-start.8) | collective-permute-done | bytes 2097184 | tf_op jit(solution)/shard_map/ppermute | solution.py:525
  168.4 5.3 routing.1
  174.7 57.9 %experts_bwd.2 = (f32[2048,512]{1,0:T(8,128)}, f32[2048,512]{1,0:T(8,128)}, f32[4,512,1280]{2,1,0:T(8,128)}, f32[4,512,1280]{2,1,0:T(8,128)}, f32[4,1280,512]{2,...) custom-call(s32[2,8,128]{2,1,0:T(8,128)} %get-tuple-element.36.refs_0_, ...), custom_call_target="tpu_custom_call" | custom-call | flops 75161927680 | bytes 60000000 | tf_op jit(solution)/shard_map/experts_bwd/pallas_call | solution.py:503
  232.6 57.9 %experts_bwd.3 = (f32[2048,512]{1,0:T(8,128)}, f32[2048,512]{1,0:T(8,128)}, f32[4,512,1280]{2,1,0:T(8,128)}, f32[4,512,1280]{2,1,0:T(8,128)}, f32[4,1280,512]{2,...) custom-call(s32[2,8,128]{2,1,0:T(8,128)} %get-tuple-element.36.refs_0_, ...), custom_call_target="tpu_custom_call" | custom-call | flops 75161927680 | bytes 60000000 | tf_op jit(solution)/shard_map/experts_bwd/pallas_call | solution.py:503
  291.1 54.5 %experts_fwd.3 = (f32[2048,512]{1,0:T(8,128)}, f32[2048,512]{1,0:T(8,128)}) custom-call(s32[2,8,128]{2,1,0:T(8,128)} %get-tuple-element.36.refs_0_, s32[2,8,128]{2,1,0:T(8,128)} %get-tuple-element.37.refs_1_, s32[2,8,128]{2,1,0:T(8,128)} %get-tuple-element.38.refs_2_, s32[1]{0:T(128)} %bitcast.15.refs_3_, s32[2,2,8,4096]{3,2,1,0:T(8,128)} %get-tuple-element.39.refs_4_, ...), custom_call_target="tpu_custom_call" | custom-call | flops 28185722880 | bytes 60000000 | tf_op jit(solution)/shard_map/experts_fwd/pallas_call | solution.py:503
  345.6 54.7 %experts_fwd.2 = (f32[2048,512]{1,0:T(8,128)}, f32[2048,512]{1,0:T(8,128)}) custom-call(s32[2,8,128]{2,1,0:T(8,128)} %get-tuple-element.36.refs_0_, s32[2,8,128]{2,1,0:T(8,128)} %get-tuple-element.37.refs_1_, s32[2,8,128]{2,1,0:T(8,128)} %get-tuple-element.38.refs_2_, s32[1]{0:T(128)} %bitcast.15.refs_3_, s32[2,2,8,4096]{3,2,1,0:T(8,128)} %get-tuple-element.39.refs_4_, ...), custom_call_target="tpu_custom_call" | custom-call | flops 28185722880 | bytes 60000000 | tf_op jit(solution)/shard_map/experts_fwd/pallas_call | solution.py:503
  400.9 6.7 add.38
  407.6 76.7 %collective-permute-start.11 = (f32[2048,512]{1,0:T(8,128)}, f32[2048,512]{1,0:T(8,128)}, u32[]{:S(2)}, u32[]{:S(2)}) collective-permute-start(f32[2048,512]{1,0:T(8,128)} %add.38), channel_id=1, source_target_pairs={{0,2},{1,3},{2,0},{3,1},{4,6},{5,7},{6,4},{7,5}} | collective-permute-start | bytes 12582920 | tf_op jit(solution)/shard_map/ppermute | solution.py:525
  484.4 5.2 add.41
  490.1 5.6 bitcast_dynamic-update-slice_fusion
  495.7 80.4 %collective-permute-done.11 = f32[2048,512]{1,0:T(8,128)} collective-permute-done((f32[2048,512]{1,0:T(8,128)}, f32[2048,512]{1,0:T(8,128)}, u32[]{:S(2)}, u32[]{:S(2)}) %collective-permute-start.11) | collective-permute-done | bytes 4194336 | tf_op jit(solution)/shard_map/ppermute | solution.py:525
  576.1 6.6 add_convert_fusion
  582.7 50.3 %collective-permute-start.12 = (bf16[2048,512]{1,0:T(8,128)(2,1)}, bf16[2048,512]{1,0:T(8,128)(2,1)S(1)}, u32[]{:S(2)}, u32[]{:S(2)}) collective-permute-start(bf16[2048,512]{1,0:T(8,128)(2,1)} %add_convert_fusion), channel_id=1, source_target_pairs={{0,4},{4,0},{1,5},{5,1},{2,6},{6,2},{3,7},{7,3}} | collective-permute-start | bytes 6291464 | tf_op jit(solution)/shard_map/ppermute | solution.py:578
  633.0 5.2 bitcast_dynamic-update-slice_fusion.1
  638.2 27.1 %collective-permute-done.21.p_far = f32[2048,512]{1,0:T(8,128)} collective-permute-done((f32[2048,512]{1,0:T(8,128)}, f32[2048,512]{1,0:T(8,128)}, u32[]{:S(2)}, u32[]{:S(2)}) %collective-permute-start.21) | collective-permute-done | bytes 4194336 | tf_op jit(solution)/shard_map/ppermute | solution.py:525
  665.3 6.7 shard_map.155
  672.0 50.7 %collective-permute-start.22 = (bf16[512,512]{1,0:T(8,128)(2,1)}, bf16[512,512]{1,0:T(8,128)(2,1)S(1)}, u32[]{:S(2)}, u32[]{:S(2)}) collective-permute-start(bf16[512,512]{1,0:T(8,128)(2,1)} %shard_map.155), channel_id=1, source_target_pairs={{0,4},{4,0},{1,5},{5,1},{2,6},{6,2},{3,7},{7,3}} | collective-permute-start | bytes 1572872 | tf_op jit(solution)/shard_map/ppermute | solution.py:584
  722.7 6.7 shard_map.156
  729.5 7.0 shard_map.157
  736.4 2.0 collective-permute-start.24
  738.4 6.7 shard_map.158
  745.2 5.2 bitcast_dynamic-update-slice_fusion.2
  750.4 7.9 %collective-permute-done.24 = bf16[512,512]{1,0:T(8,128)(2,1)} collective-permute-done((bf16[512,512]{1,0:T(8,128)(2,1)}, bf16[512,512]{1,0:T(8,128)(2,1)}, u32[]{:S(2)}, u32[]{:S(2)}) %collective-permute-start.24) | collective-permute-done | bytes 524320 | tf_op jit(solution)/shard_map/ppermute | solution.py:584
  758.3 10.3 %collective-permute-done.25 = bf16[512,512]{1,0:T(8,128)(2,1)S(1)} collective-permute-done((bf16[512,512]{1,0:T(8,128)(2,1)}, bf16[512,512]{1,0:T(8,128)(2,1)S(1)}, u32[]{:S(2)}, u32[]{:S(2)}) %collective-permute-start.25) | collective-permute-done | bytes 524320 | tf_op jit(solution)/shard_map/ppermute | solution.py:584
  768.6 2.5 maximum_bitcast_fusion
  (73 shorter events, 8.5 us)
Async XLA Ops:
  11.5 64.2 %collective-permute-start.15 = (bf16[2048,512]{1,0:T(8,128)(2,1)}, bf16[2048,512]{1,0:T(8,128)(2,1)}, u32[]{:S(2)}, u32[]{:S(2)}) collective-permute-start(bf16[2048,512]{1,0:T(8,128)(2,1)} %get-tuple-element.46.refs_6_), channel_id=1, source_target_pairs={{0,2},{1,3},{2,0},{3,1},{4,6},{5,7},{6,4},{7,5}} | collective-permute-start | bytes 6291464 | tf_op jit(solution)/shard_map/ppermute | solution.py:525
  14.8 159.3 %collective-permute-start.4 = (bf16[4,512,1280]{2,1,0:T(8,128)(2,1)}, bf16[4,512,1280]{2,1,0:T(8,128)(2,1)}, u32[]{:S(2)}, u32[]{:S(2)}) collective-permute-start(bf16[4,512,1280]{2,1,0:T(8,128)(2,1)} %bitcast.71), channel_id=1, source_target_pairs={{0,1},{1,0},{2,3},{3,2},{4,5},{5,4},{6,7},{7,6}} | collective-permute-start | bytes 15728648 | tf_op jit(solution)/shard_map/ppermute | solution.py:522
  14.8 159.5 %collective-permute-start.5 = (bf16[4,512,1280]{2,1,0:T(8,128)(2,1)}, bf16[4,512,1280]{2,1,0:T(8,128)(2,1)}, u32[]{:S(2)}, u32[]{:S(2)}) collective-permute-start(bf16[4,512,1280]{2,1,0:T(8,128)(2,1)} %bitcast.76), channel_id=1, source_target_pairs={{0,1},{1,0},{2,3},{3,2},{4,5},{5,4},{6,7},{7,6}} | collective-permute-start | bytes 15728648 | tf_op jit(solution)/shard_map/ppermute | solution.py:522
  15.3 159.4 %collective-permute-start.6 = (bf16[4,1280,512]{2,1,0:T(8,128)(2,1)}, bf16[4,1280,512]{2,1,0:T(8,128)(2,1)}, u32[]{:S(2)}, u32[]{:S(2)}) collective-permute-start(bf16[4,1280,512]{2,1,0:T(8,128)(2,1)} %bitcast.81), channel_id=1, source_target_pairs={{0,1},{1,0},{2,3},{3,2},{4,5},{5,4},{6,7},{7,6}} | collective-permute-start | bytes 15728648 | tf_op jit(solution)/shard_map/ppermute | solution.py:522
  15.4 23.4 %collective-permute-start = (f32[16,2048]{1,0:T(8,128)S(1)}, f32[16,2048]{1,0:T(8,128)S(1)}, u32[]{:S(2)}, u32[]{:S(2)}) collective-permute-start(f32[16,2048]{1,0:T(8,128)S(1)} %pad_maximum_fusion.tab0), channel_id=1, source_target_pairs={{0,1},{1,0},{2,3},{3,2},{4,5},{5,4},{6,7},{7,6}} | collective-permute-start | bytes 393224 | tf_op jit(solution)/shard_map/ppermute | solution.py:522
  38.9 24.6 %collective-permute-start.1 = (f32[16,2048]{1,0:T(8,128)S(1)}, f32[16,2048]{1,0:T(8,128)S(1)}, u32[]{:S(2)}, u32[]{:S(2)}) collective-permute-start(f32[16,2048]{1,0:T(8,128)S(1)} %pad_maximum_fusion.tab0), channel_id=1, source_target_pairs={{0,2},{1,3},{2,0},{3,1},{4,6},{5,7},{6,4},{7,5}} | collective-permute-start | bytes 393224 | tf_op jit(solution)/shard_map/ppermute | solution.py:525
  63.5 10.8 %collective-permute-start.2 = (f32[16,2048]{1,0:T(8,128)S(1)}, f32[16,2048]{1,0:T(8,128)S(1)}, u32[]{:S(2)}, u32[]{:S(2)}) collective-permute-start(f32[16,2048]{1,0:T(8,128)S(1)} %pad_maximum_fusion.tab0), channel_id=1, source_target_pairs={{0,3},{1,2},{2,1},{3,0},{4,7},{5,6},{6,5},{7,4}} | collective-permute-start | bytes 393224 | tf_op jit(solution)/shard_map/ppermute | solution.py:548
  74.3 94.1 %copy-start.7 = (f32[16,2048]{1,0:T(8,128)}, f32[16,2048]{1,0:T(8,128)S(1)}, u32[]{:S(2)}) copy-start(f32[16,2048]{1,0:T(8,128)S(1)} %collective-permute-done.2.tab3) | copy-start | bytes 393220
  74.3 48.1 %collective-permute-start.17 = (bf16[2048,512]{1,0:T(8,128)(2,1)S(1)}, bf16[2048,512]{1,0:T(8,128)(2,1)}, u32[]{:S(2)}, u32[]{:S(2)}) collective-permute-start(bf16[2048,512]{1,0:T(8,128)(2,1)S(1)} %bitcast.53), channel_id=1, source_target_pairs={{0,2},{1,3},{2,0},{3,1},{4,6},{5,7},{6,4},{7,5}} | collective-permute-start | bytes 6291464 | tf_op jit(solution)/shard_map/ppermute | solution.py:525
  75.7 91.6 %collective-permute-start.8 = (bf16[2048,512]{1,0:T(8,128)(2,1)}, bf16[2048,512]{1,0:T(8,128)(2,1)}, u32[]{:S(2)}, u32[]{:S(2)}) collective-permute-start(bf16[2048,512]{1,0:T(8,128)(2,1)} %get-tuple-element.41.refs_6_), channel_id=1, source_target_pairs={{0,2},{1,3},{2,0},{3,1},{4,6},{5,7},{6,4},{7,5}} | collective-permute-start | bytes 6291464 | tf_op jit(solution)/shard_map/ppermute | solution.py:525
  122.4 51.3 %collective-permute-start.16 = (bf16[2048,512]{1,0:T(8,128)(2,1)}, bf16[2048,512]{1,0:T(8,128)(2,1)}, u32[]{:S(2)}, u32[]{:S(2)}) collective-permute-start(bf16[2048,512]{1,0:T(8,128)(2,1)} %collective-permute-done.15.refs_6_), channel_id=1, source_target_pairs={{0,1},{1,0},{2,3},{3,2},{4,5},{5,4},{6,7},{7,6}} | collective-permute-start | bytes 6291464 | tf_op jit(solution)/shard_map/ppermute | solution.py:522
  167.3 6.5 collective-permute-start.18
  173.6 58.9 %collective-permute-start.13 = (bf16[2048,512]{1,0:T(8,128)(2,1)}, bf16[2048,512]{1,0:T(8,128)(2,1)}, u32[]{:S(2)}, u32[]{:S(2)}) collective-permute-start(bf16[2048,512]{1,0:T(8,128)(2,1)} %get-tuple-element.46.refs_6_), channel_id=1, source_target_pairs={{0,1},{1,0},{2,3},{3,2},{4,5},{5,4},{6,7},{7,6}} | collective-permute-start | bytes 6291464 | tf_op jit(solution)/shard_map/ppermute | solution.py:522
  173.8 58.8 %collective-permute-start.14 = (bf16[2048,512]{1,0:T(8,128)(2,1)S(1)}, bf16[2048,512]{1,0:T(8,128)(2,1)}, u32[]{:S(2)}, u32[]{:S(2)}) collective-permute-start(bf16[2048,512]{1,0:T(8,128)(2,1)S(1)} %bitcast.54), channel_id=1, source_target_pairs={{0,1},{1,0},{2,3},{3,2},{4,5},{5,4},{6,7},{7,6}} | collective-permute-start | bytes 6291464 | tf_op jit(solution)/shard_map/ppermute | solution.py:522
  174.2 171.5 %collective-permute-start.3 = (bf16[2048,512]{1,0:T(8,128)(2,1)}, bf16[2048,512]{1,0:T(8,128)(2,1)}, u32[]{:S(2)}, u32[]{:S(2)}) collective-permute-start(bf16[2048,512]{1,0:T(8,128)(2,1)} %get-tuple-element.41.refs_6_), channel_id=1, source_target_pairs={{0,1},{1,0},{2,3},{3,2},{4,5},{5,4},{6,7},{7,6}} | collective-permute-start | bytes 6291464 | tf_op jit(solution)/shard_map/ppermute | solution.py:522
  174.3 116.8 %collective-permute-start.9 = (bf16[2048,512]{1,0:T(8,128)(2,1)}, bf16[2048,512]{1,0:T(8,128)(2,1)}, u32[]{:S(2)}, u32[]{:S(2)}) collective-permute-start(bf16[2048,512]{1,0:T(8,128)(2,1)} %collective-permute-done.8.refs_6_), channel_id=1, source_target_pairs={{0,1},{1,0},{2,3},{3,2},{4,5},{5,4},{6,7},{7,6}} | collective-permute-start | bytes 6291464 | tf_op jit(solution)/shard_map/ppermute | solution.py:522
  290.5 199.5 %collective-permute-start.28 = (f32[2,1280,512]{2,1,0:T(8,128)}, f32[2,1280,512]{2,1,0:T(8,128)}, u32[]{:S(2)}, u32[]{:S(2)}) collective-permute-start(f32[2,1280,512]{2,1,0:T(8,128)} %get-tuple-element.64), channel_id=1, source_target_pairs={{0,1},{1,0},{2,3},{3,2},{4,5},{5,4},{6,7},{7,6}} | collective-permute-start | bytes 15728648 | tf_op jit(solution)/shard_map/ppermute | solution.py:522
  290.6 193.8 %collective-permute-start.20 = (f32[2048,512]{1,0:T(8,128)}, f32[2048,512]{1,0:T(8,128)}, u32[]{:S(2)}, u32[]{:S(2)}) collective-permute-start(f32[2048,512]{1,0:T(8,128)} %get-tuple-element.56), channel_id=1, source_target_pairs={{0,1},{1,0},{2,3},{3,2},{4,5},{5,4},{6,7},{7,6}} | collective-permute-start | bytes 12582920 | tf_op jit(solution)/shard_map/ppermute | solution.py:522
  345.6 55.3 %collective-permute-start.10 = (f32[2048,512]{1,0:T(8,128)}, f32[2048,512]{1,0:T(8,128)}, u32[]{:S(2)}, u32[]{:S(2)}) collective-permute-start(f32[2048,512]{1,0:T(8,128)} %get-tuple-element.45), channel_id=1, source_target_pairs={{0,1},{1,0},{2,3},{3,2},{4,5},{5,4},{6,7},{7,6}} | collective-permute-start | bytes 12582920 | tf_op jit(solution)/shard_map/ppermute | solution.py:522
  400.4 89.2 %collective-permute-start.7 = (f32[2048,512]{1,0:T(8,128)}, f32[2048,512]{1,0:T(8,128)}, u32[]{:S(2)}, u32[]{:S(2)}) collective-permute-start(f32[2048,512]{1,0:T(8,128)} %get-tuple-element.43), channel_id=1, source_target_pairs={{0,1},{1,0},{2,3},{3,2},{4,5},{5,4},{6,7},{7,6}} | collective-permute-start | bytes 12582920 | tf_op jit(solution)/shard_map/ppermute | solution.py:522
  400.8 232.2 %collective-permute-start.27 = (f32[2,512,1280]{2,1,0:T(8,128)}, f32[2,512,1280]{2,1,0:T(8,128)}, u32[]{:S(2)}, u32[]{:S(2)}) collective-permute-start(f32[2,512,1280]{2,1,0:T(8,128)} %get-tuple-element.62), channel_id=1, source_target_pairs={{0,1},{1,0},{2,3},{3,2},{4,5},{5,4},{6,7},{7,6}} | collective-permute-start | bytes 15728648 | tf_op jit(solution)/shard_map/ppermute | solution.py:522
  407.6 168.4 %collective-permute-start.11 = (f32[2048,512]{1,0:T(8,128)}, f32[2048,512]{1,0:T(8,128)}, u32[]{:S(2)}, u32[]{:S(2)}) collective-permute-start(f32[2048,512]{1,0:T(8,128)} %add.38), channel_id=1, source_target_pairs={{0,2},{1,3},{2,0},{3,1},{4,6},{5,7},{6,4},{7,5}} | collective-permute-start | bytes 12582920 | tf_op jit(solution)/shard_map/ppermute | solution.py:525
  484.3 260.8 %collective-permute-start.26 = (f32[2,512,1280]{2,1,0:T(8,128)}, f32[2,512,1280]{2,1,0:T(8,128)}, u32[]{:S(2)}, u32[]{:S(2)}) collective-permute-start(f32[2,512,1280]{2,1,0:T(8,128)} %get-tuple-element.60), channel_id=1, source_target_pairs={{0,1},{1,0},{2,3},{3,2},{4,5},{5,4},{6,7},{7,6}} | collective-permute-start | bytes 15728648 | tf_op jit(solution)/shard_map/ppermute | solution.py:522
  489.5 148.7 %collective-permute-start.19 = (f32[2048,512]{1,0:T(8,128)}, f32[2048,512]{1,0:T(8,128)}, u32[]{:S(2)}, u32[]{:S(2)}) collective-permute-start(f32[2048,512]{1,0:T(8,128)} %get-tuple-element.54), channel_id=1, source_target_pairs={{0,1},{1,0},{2,3},{3,2},{4,5},{5,4},{6,7},{7,6}} | collective-permute-start | bytes 12582920 | tf_op jit(solution)/shard_map/ppermute | solution.py:522
  490.0 175.3 %collective-permute-start.21 = (f32[2048,512]{1,0:T(8,128)}, f32[2048,512]{1,0:T(8,128)}, u32[]{:S(2)}, u32[]{:S(2)}) collective-permute-start(f32[2048,512]{1,0:T(8,128)} %add.41), channel_id=1, source_target_pairs={{0,2},{1,3},{2,0},{3,1},{4,6},{5,7},{6,4},{7,5}} | collective-permute-start | bytes 12582920 | tf_op jit(solution)/shard_map/ppermute | solution.py:525
  490.1 86.0 %copy-start.2 = (f32[2048,512]{1,0:T(8,128)S(1)}, f32[2048,512]{1,0:T(8,128)}, u32[]{:S(2)}) copy-start(f32[2048,512]{1,0:T(8,128)} %get-tuple-element.42) | copy-start | bytes 12582916
  490.1 86.0 %copy-start.3 = (bf16[2048,512]{1,0:T(8,128)(2,1)S(1)}, bf16[2048,512]{1,0:T(8,128)(2,1)}, u32[]{:S(2)}) copy-start(bf16[2048,512]{1,0:T(8,128)(2,1)} %get-tuple-element.35) | copy-start | bytes 6291460
  582.7 188.4 %collective-permute-start.12 = (bf16[2048,512]{1,0:T(8,128)(2,1)}, bf16[2048,512]{1,0:T(8,128)(2,1)S(1)}, u32[]{:S(2)}, u32[]{:S(2)}) collective-permute-start(bf16[2048,512]{1,0:T(8,128)(2,1)} %add_convert_fusion), channel_id=1, source_target_pairs={{0,4},{4,0},{1,5},{5,1},{2,6},{6,2},{3,7},{7,3}} | collective-permute-start | bytes 6291464 | tf_op jit(solution)/shard_map/ppermute | solution.py:578
  672.0 78.4 %collective-permute-start.22 = (bf16[512,512]{1,0:T(8,128)(2,1)}, bf16[512,512]{1,0:T(8,128)(2,1)S(1)}, u32[]{:S(2)}, u32[]{:S(2)}) collective-permute-start(bf16[512,512]{1,0:T(8,128)(2,1)} %shard_map.155), channel_id=1, source_target_pairs={{0,4},{4,0},{1,5},{5,1},{2,6},{6,2},{3,7},{7,3}} | collective-permute-start | bytes 1572872 | tf_op jit(solution)/shard_map/ppermute | solution.py:584
  729.4 20.9 %collective-permute-start.23 = (bf16[512,512]{1,0:T(8,128)(2,1)}, bf16[512,512]{1,0:T(8,128)(2,1)S(1)}, u32[]{:S(2)}, u32[]{:S(2)}) collective-permute-start(bf16[512,512]{1,0:T(8,128)(2,1)} %shard_map.156), channel_id=1, source_target_pairs={{0,4},{4,0},{1,5},{5,1},{2,6},{6,2},{3,7},{7,3}} | collective-permute-start | bytes 1572872 | tf_op jit(solution)/shard_map/ppermute | solution.py:584
  736.4 21.9 %collective-permute-start.24 = (bf16[512,512]{1,0:T(8,128)(2,1)}, bf16[512,512]{1,0:T(8,128)(2,1)}, u32[]{:S(2)}, u32[]{:S(2)}) collective-permute-start(bf16[512,512]{1,0:T(8,128)(2,1)} %shard_map.157), channel_id=1, source_target_pairs={{0,4},{4,0},{1,5},{5,1},{2,6},{6,2},{3,7},{7,3}} | collective-permute-start | bytes 1572872 | tf_op jit(solution)/shard_map/ppermute | solution.py:584
  745.1 23.5 %collective-permute-start.25 = (bf16[512,512]{1,0:T(8,128)(2,1)}, bf16[512,512]{1,0:T(8,128)(2,1)S(1)}, u32[]{:S(2)}, u32[]{:S(2)}) collective-permute-start(bf16[512,512]{1,0:T(8,128)(2,1)} %shard_map.158), channel_id=1, source_target_pairs={{0,4},{4,0},{1,5},{5,1},{2,6},{6,2},{3,7},{7,3}} | collective-permute-start | bytes 1572872 | tf_op jit(solution)/shard_map/ppermute | solution.py:584
  (9 other events, 257.7 us)

commit v5 on v4

--- a/solution.py
+++ b/solution.py
@@ -17,7 +17,7 @@
 CHUNK = 256
 OUT_ROWS = 512
 DW_SLOTS = 3
-TAIL = 4
+TAIL = (0, 1, 3, 5, 8)
 DENSE_ROWS = 512
 E_RUN = 4
 
@@ -432,14 +432,14 @@
 def run_tail(chunk, p_own, p_mate, p_far, mid, dy, x, pre, w_in, w_out):
     n_tok, width = x.shape
     ff = w_in.shape[1]
-    steps = 2
-    rows = n_tok // TAIL // steps
-    row = pl.BlockSpec((rows, width), lambda i: (chunk * steps + i, 0))
+    first, steps = TAIL[chunk], TAIL[chunk + 1] - TAIL[chunk]
+    rows = n_tok // TAIL[-1]
+    row = pl.BlockSpec((rows, width), lambda i: (first + i, 0))
     return pl.pallas_call(
         tail_kernel,
         grid=(steps,),
-        out_shape=jax.ShapeDtypeStruct((n_tok // TAIL, width), bf16),
-        in_specs=[row] * 6 + [pl.BlockSpec((rows, ff), lambda i: (chunk * steps + i, 0)),
+        out_shape=jax.ShapeDtypeStruct((rows * steps, width), bf16),
+        in_specs=[row] * 6 + [pl.BlockSpec((rows, ff), lambda i: (first + i, 0)),
                               pl.BlockSpec((width, ff), lambda i: (0, 0)), pl.BlockSpec((ff, width), lambda i: (0, 0))],
         out_specs=pl.BlockSpec((rows, width), lambda i: (i, 0)),
         scratch_shapes=[pltpu.VMEM((rows, ff), bf16)],
@@ -515,6 +515,7 @@
 def solution(mesh):
     n_ep = mesh.shape['ep']
     n_pp = mesh.shape['pp']
+    n_tail = len(TAIL) - 1
     fwd_perm = [(i, (i + 1) % n_pp) for i in range(n_pp)]
     bwd_perm = [(i, (i - 1) % n_pp) for i in range(n_pp)]
 
@@ -579,7 +580,7 @@
 
         dx_parts = []
         from_mate = to_mate(pb_near[1])
-        for c in range(TAIL):
+        for c in range(n_tail):
             dx_val = run_tail(c, pb_near[0], from_mate, ret_b, mid_b, bwd_dy, bwd_x, pre_b, stage_w_in, stage_w_out)
             dx_parts.append(lax.ppermute(dx_val, 'pp', bwd_perm))
         dx_prev = jnp.concatenate(dx_parts)

time: 779 us -> 779 us (level)
  no operation moved by 1% of the time
where the time goes in v5:
time: 779 us; the launch traced here: 772 us
  Pallas kernels  279 us (36%)
  waiting for transfers between devices  264 us (34%)
  starting transfers between devices  191 us (25%)
  other arithmetic  20.7 us (3%)
  local copies, waits for them, and re-layouts  17.3 us (2%)
    pallas_call x4, Pallas kernels, run_experts(): pl.pallas_call(functools.partial(expert_kernel, bwd, carry, E_RUN if far...  225 us
    ppermute x6, waiting for transfers between devices, to_cross(): return lax.ppermute(v, 'ep', [(i, i ^ 2) for i in range(n_ep)])  222 us
    ppermute x6, starting transfers between devices, to_cross(): return lax.ppermute(v, 'ep', [(i, i ^ 2) for i in range(n_ep)])  82.1 us
    ppermute x4, starting transfers between devices, device_fn(): dx_parts.append(lax.ppermute(dx_val, 'pp', bwd_perm))  52.8 us
    ppermute x1, starting transfers between devices, device_fn(): y_next = lax.ppermute(y_val, 'pp', fwd_perm)  50.3 us
    pallas_call x4, Pallas kernels, run_tail(): pl.pallas_call(tail_kernel, grid=(steps,), out_shape=jax.ShapeDtypeStruct...  27 us
    ppermute x17, waiting for transfers between devices, to_mate(): return lax.ppermute(v, 'ep', [(i, i ^ 1) for i in range(n_ep)])  22.9 us
    pallas_call x2, Pallas kernels, run_dense(): pl.pallas_call(dense_kernel, grid=(n_tok // DENSE_ROWS,), out_shape=out_s...  21.3 us
  transfers between devices with their start and end apart: 29, of which 8 were waited for; matrix products, arithmetic and copies ran while one was open for 5% of the time, Pallas kernels for 35%

profile of v5, /device:TPU:0, one launch (start us, length us, event | category | flops | bytes accessed | tf_op | source)
XLA Modules:
  0.0 772.4 jit_solution(5148426606137289082)
XLA Ops:
  0.7 10.8 %dense_fwd.3 = (bf16[2048,512]{1,0:T(8,128)(2,1)}, bf16[2048,512]{1,0:T(8,128)(2,1)}, bf16[2048,1280]{1,0:T(8,128)(2,1)}) custom-call(bf16[2048,512]{1,0:T(8,128)(2,1)} %bitcast.43, bf16[512,1280]{1,0:T(8,128)(2,1)} %bitcast.55, bf16[1280,512]{1,0:T(8,128)(2,1)} %bitcast.61), custom_call_target="tpu_custom_call" | custom-call | flops 5368709120 | bytes 12000000 | tf_op jit(solution)/shard_map/dense_fwd/pallas_call | solution.py:407
  11.5 3.3 collective-permute-start.15
  16.0 22.9 %collective-permute-done.tab1 = f32[16,2048]{1,0:T(8,128)S(1)} collective-permute-done((f32[16,2048]{1,0:T(8,128)S(1)}, f32[16,2048]{1,0:T(8,128)S(1)}, u32[]{:S(2)}, u32[]{:S(2)}) %collective-permute-start) | collective-permute-done | bytes 131104 | tf_op jit(solution)/shard_map/ppermute | solution.py:523
  38.9 24.6 %collective-permute-done.1.tab2 = f32[16,2048]{1,0:T(8,128)S(1)} collective-permute-done((f32[16,2048]{1,0:T(8,128)S(1)}, f32[16,2048]{1,0:T(8,128)S(1)}, u32[]{:S(2)}, u32[]{:S(2)}) %collective-permute-start.1) | collective-permute-done | bytes 131104 | tf_op jit(solution)/shard_map/ppermute | solution.py:526
  63.8 10.5 %dense_fwd.2 = (bf16[2048,512]{1,0:T(8,128)(2,1)}, bf16[2048,512]{1,0:T(8,128)(2,1)}) custom-call(bf16[2048,512]{1,0:T(8,128)(2,1)} %bitcast.86, bf16[512,1280]{1,0:T(8,128)(2,1)} %bitcast.56, bf16[1280,512]{1,0:T(8,128)(2,1)} %bitcast.62), custom_call_target="tpu_custom_call" | custom-call | flops 5368709120 | bytes 12000000 | tf_op jit(solution)/shard_map/dense_fwd/pallas_call | solution.py:407
  74.3 1.4 collective-permute-start.17
  76.3 46.0 %collective-permute-done.17.refs_8_ = bf16[2048,512]{1,0:T(8,128)(2,1)} collective-permute-done((bf16[2048,512]{1,0:T(8,128)(2,1)S(1)}, bf16[2048,512]{1,0:T(8,128)(2,1)}, u32[]{:S(2)}, u32[]{:S(2)}) %collective-permute-start.17) | collective-permute-done | bytes 2097184 | tf_op jit(solution)/shard_map/ppermute | solution.py:526
  123.6 43.7 %collective-permute-done.8.refs_6_ = bf16[2048,512]{1,0:T(8,128)(2,1)} collective-permute-done((bf16[2048,512]{1,0:T(8,128)(2,1)}, bf16[2048,512]{1,0:T(8,128)(2,1)}, u32[]{:S(2)}, u32[]{:S(2)}) %collective-permute-start.8) | collective-permute-done | bytes 2097184 | tf_op jit(solution)/shard_map/ppermute | solution.py:526
  168.4 5.3 routing.1
  174.7 57.9 %experts_bwd.2 = (f32[2048,512]{1,0:T(8,128)}, f32[2048,512]{1,0:T(8,128)}, f32[4,512,1280]{2,1,0:T(8,128)}, f32[4,512,1280]{2,1,0:T(8,128)}, f32[4,1280,512]{2,...) custom-call(s32[2,8,128]{2,1,0:T(8,128)} %get-tuple-element.36.refs_0_, ...), custom_call_target="tpu_custom_call" | custom-call | flops 75161927680 | bytes 60000000 | tf_op jit(solution)/shard_map/experts_bwd/pallas_call | solution.py:503
  232.6 57.9 %experts_bwd.3 = (f32[2048,512]{1,0:T(8,128)}, f32[2048,512]{1,0:T(8,128)}, f32[4,512,1280]{2,1,0:T(8,128)}, f32[4,512,1280]{2,1,0:T(8,128)}, f32[4,1280,512]{2,...) custom-call(s32[2,8,128]{2,1,0:T(8,128)} %get-tuple-element.36.refs_0_, ...), custom_call_target="tpu_custom_call" | custom-call | flops 75161927680 | bytes 60000000 | tf_op jit(solution)/shard_map/experts_bwd/pallas_call | solution.py:503
  291.1 54.5 %experts_fwd.3 = (f32[2048,512]{1,0:T(8,128)}, f32[2048,512]{1,0:T(8,128)}) custom-call(s32[2,8,128]{2,1,0:T(8,128)} %get-tuple-element.36.refs_0_, s32[2,8,128]{2,1,0:T(8,128)} %get-tuple-element.37.refs_1_, s32[2,8,128]{2,1,0:T(8,128)} %get-tuple-element.38.refs_2_, s32[1]{0:T(128)} %bitcast.15.refs_3_, s32[2,2,8,4096]{3,2,1,0:T(8,128)} %get-tuple-element.39.refs_4_, ...), custom_call_target="tpu_custom_call" | custom-call | flops 28185722880 | bytes 60000000 | tf_op jit(solution)/shard_map/experts_fwd/pallas_call | solution.py:503
  345.6 54.7 %experts_fwd.2 = (f32[2048,512]{1,0:T(8,128)}, f32[2048,512]{1,0:T(8,128)}) custom-call(s32[2,8,128]{2,1,0:T(8,128)} %get-tuple-element.36.refs_0_, s32[2,8,128]{2,1,0:T(8,128)} %get-tuple-element.37.refs_1_, s32[2,8,128]{2,1,0:T(8,128)} %get-tuple-element.38.refs_2_, s32[1]{0:T(128)} %bitcast.15.refs_3_, s32[2,2,8,4096]{3,2,1,0:T(8,128)} %get-tuple-element.39.refs_4_, ...), custom_call_target="tpu_custom_call" | custom-call | flops 28185722880 | bytes 60000000 | tf_op jit(solution)/shard_map/experts_fwd/pallas_call | solution.py:503
  400.9 6.7 add.38
  407.6 76.7 %collective-permute-start.11 = (f32[2048,512]{1,0:T(8,128)}, f32[2048,512]{1,0:T(8,128)}, u32[]{:S(2)}, u32[]{:S(2)}) collective-permute-start(f32[2048,512]{1,0:T(8,128)} %add.38), channel_id=1, source_target_pairs={{0,2},{1,3},{2,0},{3,1},{4,6},{5,7},{6,4},{7,5}} | collective-permute-start | bytes 12582920 | tf_op jit(solution)/shard_map/ppermute | solution.py:526
  484.4 5.2 add.41
  490.1 5.6 bitcast_dynamic-update-slice_fusion
  495.7 80.4 %collective-permute-done.11 = f32[2048,512]{1,0:T(8,128)} collective-permute-done((f32[2048,512]{1,0:T(8,128)}, f32[2048,512]{1,0:T(8,128)}, u32[]{:S(2)}, u32[]{:S(2)}) %collective-permute-start.11) | collective-permute-done | bytes 4194336 | tf_op jit(solution)/shard_map/ppermute | solution.py:526
  576.1 6.6 add_convert_fusion
  582.7 50.3 %collective-permute-start.12 = (bf16[2048,512]{1,0:T(8,128)(2,1)}, bf16[2048,512]{1,0:T(8,128)(2,1)S(1)}, u32[]{:S(2)}, u32[]{:S(2)}) collective-permute-start(bf16[2048,512]{1,0:T(8,128)(2,1)} %add_convert_fusion), channel_id=1, source_target_pairs={{0,4},{4,0},{1,5},{5,1},{2,6},{6,2},{3,7},{7,3}} | collective-permute-start | bytes 6291464 | tf_op jit(solution)/shard_map/ppermute | solution.py:579
  633.0 5.2 bitcast_dynamic-update-slice_fusion.1
  638.2 27.1 %collective-permute-done.21.p_far = f32[2048,512]{1,0:T(8,128)} collective-permute-done((f32[2048,512]{1,0:T(8,128)}, f32[2048,512]{1,0:T(8,128)}, u32[]{:S(2)}, u32[]{:S(2)}) %collective-permute-start.21) | collective-permute-done | bytes 4194336 | tf_op jit(solution)/shard_map/ppermute | solution.py:526
  665.3 4.8 shard_map.155
  670.1 50.8 %collective-permute-start.22 = (bf16[256,512]{1,0:T(8,128)(2,1)}, bf16[256,512]{1,0:T(8,128)(2,1)S(1)}, u32[]{:S(2)}, u32[]{:S(2)}) collective-permute-start(bf16[256,512]{1,0:T(8,128)(2,1)} %shard_map.155), channel_id=1, source_target_pairs={{0,4},{4,0},{1,5},{5,1},{2,6},{6,2},{3,7},{7,3}} | collective-permute-start | bytes 786440 | tf_op jit(solution)/shard_map/ppermute | solution.py:585
  720.9 6.7 shard_map.156
  727.6 7.0 shard_map.157
  734.6 2.0 collective-permute-start.24
  736.6 8.6 %shard_map.158 = bf16[768,512]{1,0:T(8,128)(2,1)} custom-call(f32[2048,512]{1,0:T(8,128)} %get-tuple-element.53.p_own, f32[2048,512]{1,0:T(8,128)} %collective-permute-done.19.p_mate, f32[2048,512]{1,0:T(8,128)} %collective-permute-done.21.p_far, bf16[2048,512]{1,0:T(8,128)(2,1)} %get-tuple-element.57.mid_ref, bf16[2048,512]{1,0:T(8,128)(2,1)} %bitcast.52, ...), custom_call_target="tpu_custom_call" | custom-call | flops 2013265920 | bytes 6000000 | tf_op jit(solution)/shard_map/pallas_call | solution.py:438
  745.2 5.2 bitcast_dynamic-update-slice_fusion.2
  750.4 3.4 collective-permute-done.24
  753.8 15.5 %collective-permute-done.25 = bf16[768,512]{1,0:T(8,128)(2,1)S(1)} collective-permute-done((bf16[768,512]{1,0:T(8,128)(2,1)}, bf16[768,512]{1,0:T(8,128)(2,1)S(1)}, u32[]{:S(2)}, u32[]{:S(2)}) %collective-permute-start.25) | collective-permute-done | bytes 786464 | tf_op jit(solution)/shard_map/ppermute | solution.py:585
  769.3 1.5 maximum_bitcast_fusion
  (73 shorter events, 8.5 us)
Async XLA Ops:
  11.5 64.2 %collective-permute-start.15 = (bf16[2048,512]{1,0:T(8,128)(2,1)}, bf16[2048,512]{1,0:T(8,128)(2,1)}, u32[]{:S(2)}, u32[]{:S(2)}) collective-permute-start(bf16[2048,512]{1,0:T(8,128)(2,1)} %get-tuple-element.46.refs_6_), channel_id=1, source_target_pairs={{0,2},{1,3},{2,0},{3,1},{4,6},{5,7},{6,4},{7,5}} | collective-permute-start | bytes 6291464 | tf_op jit(solution)/shard_map/ppermute | solution.py:526
  14.8 159.3 %collective-permute-start.4 = (bf16[4,512,1280]{2,1,0:T(8,128)(2,1)}, bf16[4,512,1280]{2,1,0:T(8,128)(2,1)}, u32[]{:S(2)}, u32[]{:S(2)}) collective-permute-start(bf16[4,512,1280]{2,1,0:T(8,128)(2,1)} %bitcast.71), channel_id=1, source_target_pairs={{0,1},{1,0},{2,3},{3,2},{4,5},{5,4},{6,7},{7,6}} | collective-permute-start | bytes 15728648 | tf_op jit(solution)/shard_map/ppermute | solution.py:523
  14.8 159.5 %collective-permute-start.5 = (bf16[4,512,1280]{2,1,0:T(8,128)(2,1)}, bf16[4,512,1280]{2,1,0:T(8,128)(2,1)}, u32[]{:S(2)}, u32[]{:S(2)}) collective-permute-start(bf16[4,512,1280]{2,1,0:T(8,128)(2,1)} %bitcast.76), channel_id=1, source_target_pairs={{0,1},{1,0},{2,3},{3,2},{4,5},{5,4},{6,7},{7,6}} | collective-permute-start | bytes 15728648 | tf_op jit(solution)/shard_map/ppermute | solution.py:523
  15.3 159.4 %collective-permute-start.6 = (bf16[4,1280,512]{2,1,0:T(8,128)(2,1)}, bf16[4,1280,512]{2,1,0:T(8,128)(2,1)}, u32[]{:S(2)}, u32[]{:S(2)}) collective-permute-start(bf16[4,1280,512]{2,1,0:T(8,128)(2,1)} %bitcast.81), channel_id=1, source_target_pairs={{0,1},{1,0},{2,3},{3,2},{4,5},{5,4},{6,7},{7,6}} | collective-permute-start | bytes 15728648 | tf_op jit(solution)/shard_map/ppermute | solution.py:523
  15.4 23.4 %collective-permute-start = (f32[16,2048]{1,0:T(8,128)S(1)}, f32[16,2048]{1,0:T(8,128)S(1)}, u32[]{:S(2)}, u32[]{:S(2)}) collective-permute-start(f32[16,2048]{1,0:T(8,128)S(1)} %pad_maximum_fusion.tab0), channel_id=1, source_target_pairs={{0,1},{1,0},{2,3},{3,2},{4,5},{5,4},{6,7},{7,6}} | collective-permute-start | bytes 393224 | tf_op jit(solution)/shard_map/ppermute | solution.py:523
  38.9 24.6 %collective-permute-start.1 = (f32[16,2048]{1,0:T(8,128)S(1)}, f32[16,2048]{1,0:T(8,128)S(1)}, u32[]{:S(2)}, u32[]{:S(2)}) collective-permute-start(f32[16,2048]{1,0:T(8,128)S(1)} %pad_maximum_fusion.tab0), channel_id=1, source_target_pairs={{0,2},{1,3},{2,0},{3,1},{4,6},{5,7},{6,4},{7,5}} | collective-permute-start | bytes 393224 | tf_op jit(solution)/shard_map/ppermute | solution.py:526
  63.5 10.8 %collective-permute-start.2 = (f32[16,2048]{1,0:T(8,128)S(1)}, f32[16,2048]{1,0:T(8,128)S(1)}, u32[]{:S(2)}, u32[]{:S(2)}) collective-permute-start(f32[16,2048]{1,0:T(8,128)S(1)} %pad_maximum_fusion.tab0), channel_id=1, source_target_pairs={{0,3},{1,2},{2,1},{3,0},{4,7},{5,6},{6,5},{7,4}} | collective-permute-start | bytes 393224 | tf_op jit(solution)/shard_map/ppermute | solution.py:549
  74.3 94.1 %copy-start.7 = (f32[16,2048]{1,0:T(8,128)}, f32[16,2048]{1,0:T(8,128)S(1)}, u32[]{:S(2)}) copy-start(f32[16,2048]{1,0:T(8,128)S(1)} %collective-permute-done.2.tab3) | copy-start | bytes 393220
  74.3 48.1 %collective-permute-start.17 = (bf16[2048,512]{1,0:T(8,128)(2,1)S(1)}, bf16[2048,512]{1,0:T(8,128)(2,1)}, u32[]{:S(2)}, u32[]{:S(2)}) collective-permute-start(bf16[2048,512]{1,0:T(8,128)(2,1)S(1)} %bitcast.53), channel_id=1, source_target_pairs={{0,2},{1,3},{2,0},{3,1},{4,6},{5,7},{6,4},{7,5}} | collective-permute-start | bytes 6291464 | tf_op jit(solution)/shard_map/ppermute | solution.py:526
  75.7 91.6 %collective-permute-start.8 = (bf16[2048,512]{1,0:T(8,128)(2,1)}, bf16[2048,512]{1,0:T(8,128)(2,1)}, u32[]{:S(2)}, u32[]{:S(2)}) collective-permute-start(bf16[2048,512]{1,0:T(8,128)(2,1)} %get-tuple-element.41.refs_6_), channel_id=1, source_target_pairs={{0,2},{1,3},{2,0},{3,1},{4,6},{5,7},{6,4},{7,5}} | collective-permute-start | bytes 6291464 | tf_op jit(solution)/shard_map/ppermute | solution.py:526
  122.4 51.3 %collective-permute-start.16 = (bf16[2048,512]{1,0:T(8,128)(2,1)}, bf16[2048,512]{1,0:T(8,128)(2,1)}, u32[]{:S(2)}, u32[]{:S(2)}) collective-permute-start(bf16[2048,512]{1,0:T(8,128)(2,1)} %collective-permute-done.15.refs_6_), channel_id=1, source_target_pairs={{0,1},{1,0},{2,3},{3,2},{4,5},{5,4},{6,7},{7,6}} | collective-permute-start | bytes 6291464 | tf_op jit(solution)/shard_map/ppermute | solution.py:523
  167.3 6.5 collective-permute-start.18
  173.6 58.9 %collective-permute-start.13 = (bf16[2048,512]{1,0:T(8,128)(2,1)}, bf16[2048,512]{1,0:T(8,128)(2,1)}, u32[]{:S(2)}, u32[]{:S(2)}) collective-permute-start(bf16[2048,512]{1,0:T(8,128)(2,1)} %get-tuple-element.46.refs_6_), channel_id=1, source_target_pairs={{0,1},{1,0},{2,3},{3,2},{4,5},{5,4},{6,7},{7,6}} | collective-permute-start | bytes 6291464 | tf_op jit(solution)/shard_map/ppermute | solution.py:523
  173.8 58.8 %collective-permute-start.14 = (bf16[2048,512]{1,0:T(8,128)(2,1)S(1)}, bf16[2048,512]{1,0:T(8,128)(2,1)}, u32[]{:S(2)}, u32[]{:S(2)}) collective-permute-start(bf16[2048,512]{1,0:T(8,128)(2,1)S(1)} %bitcast.54), channel_id=1, source_target_pairs={{0,1},{1,0},{2,3},{3,2},{4,5},{5,4},{6,7},{7,6}} | collective-permute-start | bytes 6291464 | tf_op jit(solution)/shard_map/ppermute | solution.py:523
  174.2 171.5 %collective-permute-start.3 = (bf16[2048,512]{1,0:T(8,128)(2,1)}, bf16[2048,512]{1,0:T(8,128)(2,1)}, u32[]{:S(2)}, u32[]{:S(2)}) collective-permute-start(bf16[2048,512]{1,0:T(8,128)(2,1)} %get-tuple-element.41.refs_6_), channel_id=1, source_target_pairs={{0,1},{1,0},{2,3},{3,2},{4,5},{5,4},{6,7},{7,6}} | collective-permute-start | bytes 6291464 | tf_op jit(solution)/shard_map/ppermute | solution.py:523
  174.3 116.8 %collective-permute-start.9 = (bf16[2048,512]{1,0:T(8,128)(2,1)}, bf16[2048,512]{1,0:T(8,128)(2,1)}, u32[]{:S(2)}, u32[]{:S(2)}) collective-permute-start(bf16[2048,512]{1,0:T(8,128)(2,1)} %collective-permute-done.8.refs_6_), channel_id=1, source_target_pairs={{0,1},{1,0},{2,3},{3,2},{4,5},{5,4},{6,7},{7,6}} | collective-permute-start | bytes 6291464 | tf_op jit(solution)/shard_map/ppermute | solution.py:523
  290.5 199.5 %collective-permute-start.28 = (f32[2,1280,512]{2,1,0:T(8,128)}, f32[2,1280,512]{2,1,0:T(8,128)}, u32[]{:S(2)}, u32[]{:S(2)}) collective-permute-start(f32[2,1280,512]{2,1,0:T(8,128)} %get-tuple-element.64), channel_id=1, source_target_pairs={{0,1},{1,0},{2,3},{3,2},{4,5},{5,4},{6,7},{7,6}} | collective-permute-start | bytes 15728648 | tf_op jit(solution)/shard_map/ppermute | solution.py:523
  290.6 193.8 %collective-permute-start.20 = (f32[2048,512]{1,0:T(8,128)}, f32[2048,512]{1,0:T(8,128)}, u32[]{:S(2)}, u32[]{:S(2)}) collective-permute-start(f32[2048,512]{1,0:T(8,128)} %get-tuple-element.56), channel_id=1, source_target_pairs={{0,1},{1,0},{2,3},{3,2},{4,5},{5,4},{6,7},{7,6}} | collective-permute-start | bytes 12582920 | tf_op jit(solution)/shard_map/ppermute | solution.py:523
  345.6 55.3 %collective-permute-start.10 = (f32[2048,512]{1,0:T(8,128)}, f32[2048,512]{1,0:T(8,128)}, u32[]{:S(2)}, u32[]{:S(2)}) collective-permute-start(f32[2048,512]{1,0:T(8,128)} %get-tuple-element.45), channel_id=1, source_target_pairs={{0,1},{1,0},{2,3},{3,2},{4,5},{5,4},{6,7},{7,6}} | collective-permute-start | bytes 12582920 | tf_op jit(solution)/shard_map/ppermute | solution.py:523
  400.4 89.2 %collective-permute-start.7 = (f32[2048,512]{1,0:T(8,128)}, f32[2048,512]{1,0:T(8,128)}, u32[]{:S(2)}, u32[]{:S(2)}) collective-permute-start(f32[2048,512]{1,0:T(8,128)} %get-tuple-element.43), channel_id=1, source_target_pairs={{0,1},{1,0},{2,3},{3,2},{4,5},{5,4},{6,7},{7,6}} | collective-permute-start | bytes 12582920 | tf_op jit(solution)/shard_map/ppermute | solution.py:523
  400.8 232.2 %collective-permute-start.27 = (f32[2,512,1280]{2,1,0:T(8,128)}, f32[2,512,1280]{2,1,0:T(8,128)}, u32[]{:S(2)}, u32[]{:S(2)}) collective-permute-start(f32[2,512,1280]{2,1,0:T(8,128)} %get-tuple-element.62), channel_id=1, source_target_pairs={{0,1},{1,0},{2,3},{3,2},{4,5},{5,4},{6,7},{7,6}} | collective-permute-start | bytes 15728648 | tf_op jit(solution)/shard_map/ppermute | solution.py:523
  407.6 168.4 %collective-permute-start.11 = (f32[2048,512]{1,0:T(8,128)}, f32[2048,512]{1,0:T(8,128)}, u32[]{:S(2)}, u32[]{:S(2)}) collective-permute-start(f32[2048,512]{1,0:T(8,128)} %add.38), channel_id=1, source_target_pairs={{0,2},{1,3},{2,0},{3,1},{4,6},{5,7},{6,4},{7,5}} | collective-permute-start | bytes 12582920 | tf_op jit(solution)/shard_map/ppermute | solution.py:526
  484.3 260.8 %collective-permute-start.26 = (f32[2,512,1280]{2,1,0:T(8,128)}, f32[2,512,1280]{2,1,0:T(8,128)}, u32[]{:S(2)}, u32[]{:S(2)}) collective-permute-start(f32[2,512,1280]{2,1,0:T(8,128)} %get-tuple-element.60), channel_id=1, source_target_pairs={{0,1},{1,0},{2,3},{3,2},{4,5},{5,4},{6,7},{7,6}} | collective-permute-start | bytes 15728648 | tf_op jit(solution)/shard_map/ppermute | solution.py:523
  489.5 148.7 %collective-permute-start.19 = (f32[2048,512]{1,0:T(8,128)}, f32[2048,512]{1,0:T(8,128)}, u32[]{:S(2)}, u32[]{:S(2)}) collective-permute-start(f32[2048,512]{1,0:T(8,128)} %get-tuple-element.54), channel_id=1, source_target_pairs={{0,1},{1,0},{2,3},{3,2},{4,5},{5,4},{6,7},{7,6}} | collective-permute-start | bytes 12582920 | tf_op jit(solution)/shard_map/ppermute | solution.py:523
  490.0 175.3 %collective-permute-start.21 = (f32[2048,512]{1,0:T(8,128)}, f32[2048,512]{1,0:T(8,128)}, u32[]{:S(2)}, u32[]{:S(2)}) collective-permute-start(f32[2048,512]{1,0:T(8,128)} %add.41), channel_id=1, source_target_pairs={{0,2},{1,3},{2,0},{3,1},{4,6},{5,7},{6,4},{7,5}} | collective-permute-start | bytes 12582920 | tf_op jit(solution)/shard_map/ppermute | solution.py:526
  490.1 86.0 %copy-start.2 = (f32[2048,512]{1,0:T(8,128)S(1)}, f32[2048,512]{1,0:T(8,128)}, u32[]{:S(2)}) copy-start(f32[2048,512]{1,0:T(8,128)} %get-tuple-element.42) | copy-start | bytes 12582916
  490.1 86.0 %copy-start.3 = (bf16[2048,512]{1,0:T(8,128)(2,1)S(1)}, bf16[2048,512]{1,0:T(8,128)(2,1)}, u32[]{:S(2)}) copy-start(bf16[2048,512]{1,0:T(8,128)(2,1)} %get-tuple-element.35) | copy-start | bytes 6291460
  582.7 188.1 %collective-permute-start.12 = (bf16[2048,512]{1,0:T(8,128)(2,1)}, bf16[2048,512]{1,0:T(8,128)(2,1)S(1)}, u32[]{:S(2)}, u32[]{:S(2)}) collective-permute-start(bf16[2048,512]{1,0:T(8,128)(2,1)} %add_convert_fusion), channel_id=1, source_target_pairs={{0,4},{4,0},{1,5},{5,1},{2,6},{6,2},{3,7},{7,3}} | collective-permute-start | bytes 6291464 | tf_op jit(solution)/shard_map/ppermute | solution.py:579
  670.1 80.2 %collective-permute-start.22 = (bf16[256,512]{1,0:T(8,128)(2,1)}, bf16[256,512]{1,0:T(8,128)(2,1)S(1)}, u32[]{:S(2)}, u32[]{:S(2)}) collective-permute-start(bf16[256,512]{1,0:T(8,128)(2,1)} %shard_map.155), channel_id=1, source_target_pairs={{0,4},{4,0},{1,5},{5,1},{2,6},{6,2},{3,7},{7,3}} | collective-permute-start | bytes 786440 | tf_op jit(solution)/shard_map/ppermute | solution.py:585
  727.6 22.8 %collective-permute-start.23 = (bf16[512,512]{1,0:T(8,128)(2,1)}, bf16[512,512]{1,0:T(8,128)(2,1)S(1)}, u32[]{:S(2)}, u32[]{:S(2)}) collective-permute-start(bf16[512,512]{1,0:T(8,128)(2,1)} %shard_map.156), channel_id=1, source_target_pairs={{0,4},{4,0},{1,5},{5,1},{2,6},{6,2},{3,7},{7,3}} | collective-permute-start | bytes 1572872 | tf_op jit(solution)/shard_map/ppermute | solution.py:585
  734.6 19.2 %collective-permute-start.24 = (bf16[512,512]{1,0:T(8,128)(2,1)}, bf16[512,512]{1,0:T(8,128)(2,1)S(1)}, u32[]{:S(2)}, u32[]{:S(2)}) collective-permute-start(bf16[512,512]{1,0:T(8,128)(2,1)} %shard_map.157), channel_id=1, source_target_pairs={{0,4},{4,0},{1,5},{5,1},{2,6},{6,2},{3,7},{7,3}} | collective-permute-start | bytes 1572872 | tf_op jit(solution)/shard_map/ppermute | solution.py:585
  745.1 24.2 %collective-permute-start.25 = (bf16[768,512]{1,0:T(8,128)(2,1)}, bf16[768,512]{1,0:T(8,128)(2,1)S(1)}, u32[]{:S(2)}, u32[]{:S(2)}) collective-permute-start(bf16[768,512]{1,0:T(8,128)(2,1)} %shard_map.158), channel_id=1, source_target_pairs={{0,4},{4,0},{1,5},{5,1},{2,6},{6,2},{3,7},{7,3}} | collective-permute-start | bytes 2359304 | tf_op jit(solution)/shard_map/ppermute | solution.py:585
  (9 other events, 257.7 us)

commit v6 on v5

--- a/solution.py
+++ b/solution.py
@@ -15,7 +15,7 @@
 WIN_MORE = 1536
 ALIGN = 64
 CHUNK = 256
-OUT_ROWS = 512
+OUT_ROWS = 256
 DW_SLOTS = 3
 TAIL = (0, 1, 3, 5, 8)
 DENSE_ROWS = 512
@@ -38,7 +38,7 @@
     return lax.dot_general(a, b, (((0,), (0,)), ((), ())), preferred_element_type=f32)
 
 
-def expert_kernel(bwd, carry, row0, *refs):
+def expert_kernel(bwd, carry, row0, n_out, *refs):
     refs = list(refs)
 
     def take(n):
@@ -54,15 +54,15 @@
     w_own = take(3)
     w_mate = take(3)
     dw_in = take(6) if carry else []
-    p_out = take(2)
+    p_out = take(n_out)
     dw_out = take(6) if bwd else []
     order, tok, acc, wg_buf, wu_buf, wd_buf, x_acc, out_all = take(8)
     if bwd:
         dyt, d_acc, xt, dg_all, du_all, dwg_buf, dwu_buf, dwd_buf = take(8)
-        tok_sem, w_sem, in_sem, out_sem = take(4)
+        tok_sem, w_sem, p_sem, in_sem, out_sem = take(5)
     else:
         (act_all,) = take(1)
-        tok_sem, w_sem = take(2)
+        tok_sem, w_sem, p_sem = take(3)
     half = tok_in[0].shape[0]
     n_tok = 2 * half
     ff = wg_buf.shape[2]
@@ -153,13 +153,19 @@
         return toks, lambda: jnp.where(mask, 1.0, 0.0).astype(bf16), \
             lambda: jnp.where(mask, gate_ref[mb, shift, pl.ds(row0 + e, 1), lanes], 0.0).astype(bf16)
 
+    bounds = [0]
+    for ref in p_out:
+        bounds.append(bounds[-1] + ref.shape[0])
+
     def p_copy(q):
-        per = half // OUT_ROWS
-        for j in range(2):
-            @pl.when(q // per == j)
+        for j, dst in enumerate(p_out):
+            lo, hi = bounds[j] // OUT_ROWS, bounds[j + 1] // OUT_ROWS
+
+            @pl.when((q >= lo) & (q < hi))
             def _():
-                dst = p_out[j].at[pl.ds(pl.multiple_of((q - j * per) * OUT_ROWS, OUT_ROWS), OUT_ROWS), :]
-                pltpu.make_async_copy(acc.at[pl.ds(pl.multiple_of(q * OUT_ROWS, OUT_ROWS), OUT_ROWS), :], dst, tok_sem.at[0, j]).start()
+                rows = pl.ds(pl.multiple_of((q - lo) * OUT_ROWS, OUT_ROWS), OUT_ROWS)
+                src = acc.at[pl.ds(pl.multiple_of(q * OUT_ROWS, OUT_ROWS), OUT_ROWS), :]
+                pltpu.make_async_copy(src, dst.at[rows, :], p_sem.at[j]).start()
 
     def expert(i, _):
         e = order[i]
@@ -281,7 +287,7 @@
         return 0
 
     lax.fori_loop(0, E_RUN, expert, 0)
-    outs = [pltpu.make_async_copy(acc.at[pl.ds(j * half, half), :], p_out[j], tok_sem.at[0, j]) for j in range(2)]
+    outs = [pltpu.make_async_copy(acc.at[pl.ds(bounds[j], ref.shape[0]), :], ref, p_sem.at[j]) for j, ref in enumerate(p_out)]
     if bwd:
         for e in (E_RUN - 2, E_RUN - 1):
             dw_copies(dw_out, e, e % DW_SLOTS, out_sem, False)[1]()
@@ -439,7 +445,7 @@
         tail_kernel,
         grid=(steps,),
         out_shape=jax.ShapeDtypeStruct((rows * steps, width), bf16),
-        in_specs=[row] * 6 + [pl.BlockSpec((rows, ff), lambda i: (first + i, 0)),
+        in_specs=[row, pl.BlockSpec((rows, width), lambda i: (first + i if chunk == 0 else first + i - 1, 0))] + [row] * 4 + [pl.BlockSpec((rows, ff), lambda i: (first + i, 0)),
                               pl.BlockSpec((width, ff), lambda i: (0, 0)), pl.BlockSpec((ff, width), lambda i: (0, 0))],
         out_specs=pl.BlockSpec((rows, width), lambda i: (i, 0)),
         scratch_shapes=[pltpu.VMEM((rows, ff), bf16)],
@@ -463,7 +469,8 @@
     if carry:
         args += [*dw_prev]
     in_specs = [smem] * 4 + [vmem] * 2 + [hbm] * (len(args) - 6)
-    out_shape = [jax.ShapeDtypeStruct((half, width), f32)] * 2
+    p_rows = [half, OUT_ROWS, half - OUT_ROWS] if carry else [half, half]
+    out_shape = [jax.ShapeDtypeStruct((n, width), f32) for n in p_rows]
     if bwd:
         for n in (e_loc, 2):
             out_shape += [jax.ShapeDtypeStruct((n, *w.shape[1:]), f32) for w in w_own]
@@ -490,6 +497,7 @@
             pltpu.VMEM((DW_SLOTS, ff, width), f32),
             pltpu.SemaphoreType.DMA((2, 2)),
             pltpu.SemaphoreType.DMA((2, 3)),
+            pltpu.SemaphoreType.DMA((3,)),
             pltpu.SemaphoreType.DMA((DW_SLOTS, 3)),
             pltpu.SemaphoreType.DMA((DW_SLOTS, 3)),
         ]
@@ -498,10 +506,11 @@
             pltpu.VMEM((rows, ff), bf16),
             pltpu.SemaphoreType.DMA((2, 2)),
             pltpu.SemaphoreType.DMA((2, 3)),
+            pltpu.SemaphoreType.DMA((3,)),
         ]
     flops = (8 if bwd else 3) * 2 * 3584 * 2 * width * ff
     return pl.pallas_call(
-        functools.partial(expert_kernel, bwd, carry, E_RUN if far else 0),
+        functools.partial(expert_kernel, bwd, carry, E_RUN if far else 0, len(p_rows)),
         out_shape=out_shape,
         in_specs=in_specs,
         out_specs=[hbm] * len(out_shape),
@@ -572,16 +581,16 @@
         pb_far = run_experts(meta, True, far_b, dy_far, w_own, w_mate, None)
         ret_b = to_cross(combine(pb_far[:2]))
         pb_near = run_experts(meta, False, near_b, dy_near, w_own, w_mate, pb_far[2:])
-        dw_full, dw_mate = pb_near[2:5], pb_near[5:8]
+        dw_full, dw_mate = pb_near[3:6], pb_near[6:9]
 
         near_f_mate = to_mate(pf_near[1])
         y_val = (mid_f.astype(f32) + (pf_near[0] + near_f_mate + ret_f)).astype(bf16)
         y_next = lax.ppermute(y_val, 'pp', fwd_perm)
 
         dx_parts = []
-        from_mate = to_mate(pb_near[1])
+        from_mate = [to_mate(pb_near[1 + k]) for k in range(2)]
         for c in range(n_tail):
-            dx_val = run_tail(c, pb_near[0], from_mate, ret_b, mid_b, bwd_dy, bwd_x, pre_b, stage_w_in, stage_w_out)
+            dx_val = run_tail(c, pb_near[0], from_mate[min(c, 1)], ret_b, mid_b, bwd_dy, bwd_x, pre_b, stage_w_in, stage_w_out)
             dx_parts.append(lax.ppermute(dx_val, 'pp', bwd_perm))
         dx_prev = jnp.concatenate(dx_parts)
 

time: 779 us -> 779 us (level)
    ppermute x17 -> x18, waiting for transfers between devices: 22.9 us -> 22.9 us  [to_mate(): return lax.ppermute(v, 'ep', [(i, i ^ 1) for i in range(n_ep)])]
  transfers between devices with their start and end apart: 29 -> 30, of which waited for: 8 -> 8; matrix products, arithmetic and copies ran while one was open for 5% -> 5% of each run, Pallas kernels for 35% -> 35%
where the time goes in v6:
time: 779 us; the launch traced here: 773 us
  Pallas kernels  279 us (36%)
  waiting for transfers between devices  263 us (34%)
  starting transfers between devices  191 us (25%)
  other arithmetic  20.6 us (3%)
  local copies, waits for them, and re-layouts  17.3 us (2%)
    pallas_call x4, Pallas kernels, run_experts(): pl.pallas_call(functools.partial(expert_kernel, bwd, carry, E_RUN if far...  225 us
    ppermute x6, waiting for transfers between devices, to_cross(): return lax.ppermute(v, 'ep', [(i, i ^ 2) for i in range(n_ep)])  222 us
    ppermute x6, starting transfers between devices, to_cross(): return lax.ppermute(v, 'ep', [(i, i ^ 2) for i in range(n_ep)])  82.2 us
    ppermute x4, starting transfers between devices, device_fn(): dx_parts.append(lax.ppermute(dx_val, 'pp', bwd_perm))  52.9 us
    ppermute x1, starting transfers between devices, device_fn(): y_next = lax.ppermute(y_val, 'pp', fwd_perm)  50.5 us
    pallas_call x4, Pallas kernels, run_tail(): pl.pallas_call(tail_kernel, grid=(steps,), out_shape=jax.ShapeDtypeStruct...  27.1 us
    ppermute x18, waiting for transfers between devices, to_mate(): return lax.ppermute(v, 'ep', [(i, i ^ 1) for i in range(n_ep)])  22.9 us
    pallas_call x2, Pallas kernels, run_dense(): pl.pallas_call(dense_kernel, grid=(n_tok // DENSE_ROWS,), out_shape=out_s...  21.2 us
  transfers between devices with their start and end apart: 30, of which 8 were waited for; matrix products, arithmetic and copies ran while one was open for 5% of the time, Pallas kernels for 35%

profile of v6, /device:TPU:0, one launch (start us, length us, event | category | flops | bytes accessed | tf_op | source)
XLA Modules:
  0.0 772.6 jit_solution(5063547242563153992)
XLA Ops:
  0.7 10.8 %dense_fwd.3 = (bf16[2048,512]{1,0:T(8,128)(2,1)}, bf16[2048,512]{1,0:T(8,128)(2,1)}, bf16[2048,1280]{1,0:T(8,128)(2,1)}) custom-call(bf16[2048,512]{1,0:T(8,128)(2,1)} %bitcast.43, bf16[512,1280]{1,0:T(8,128)(2,1)} %bitcast.55, bf16[1280,512]{1,0:T(8,128)(2,1)} %bitcast.61), custom_call_target="tpu_custom_call" | custom-call | flops 5368709120 | bytes 12000000 | tf_op jit(solution)/shard_map/dense_fwd/pallas_call | solution.py:413
  11.5 3.3 collective-permute-start.15
  15.9 22.9 %collective-permute-done.tab1 = f32[16,2048]{1,0:T(8,128)S(1)} collective-permute-done((f32[16,2048]{1,0:T(8,128)S(1)}, f32[16,2048]{1,0:T(8,128)S(1)}, u32[]{:S(2)}, u32[]{:S(2)}) %collective-permute-start) | collective-permute-done | bytes 131104 | tf_op jit(solution)/shard_map/ppermute | solution.py:532
  38.9 24.6 %collective-permute-done.1.tab2 = f32[16,2048]{1,0:T(8,128)S(1)} collective-permute-done((f32[16,2048]{1,0:T(8,128)S(1)}, f32[16,2048]{1,0:T(8,128)S(1)}, u32[]{:S(2)}, u32[]{:S(2)}) %collective-permute-start.1) | collective-permute-done | bytes 131104 | tf_op jit(solution)/shard_map/ppermute | solution.py:535
  63.8 10.4 %dense_fwd.2 = (bf16[2048,512]{1,0:T(8,128)(2,1)}, bf16[2048,512]{1,0:T(8,128)(2,1)}) custom-call(bf16[2048,512]{1,0:T(8,128)(2,1)} %bitcast.86, bf16[512,1280]{1,0:T(8,128)(2,1)} %bitcast.56, bf16[1280,512]{1,0:T(8,128)(2,1)} %bitcast.62), custom_call_target="tpu_custom_call" | custom-call | flops 5368709120 | bytes 12000000 | tf_op jit(solution)/shard_map/dense_fwd/pallas_call | solution.py:413
  74.2 1.5 collective-permute-start.17
  76.3 46.0 %collective-permute-done.17.refs_8_ = bf16[2048,512]{1,0:T(8,128)(2,1)} collective-permute-done((bf16[2048,512]{1,0:T(8,128)(2,1)S(1)}, bf16[2048,512]{1,0:T(8,128)(2,1)}, u32[]{:S(2)}, u32[]{:S(2)}) %collective-permute-start.17) | collective-permute-done | bytes 2097184 | tf_op jit(solution)/shard_map/ppermute | solution.py:535
  123.5 43.7 %collective-permute-done.8.refs_6_ = bf16[2048,512]{1,0:T(8,128)(2,1)} collective-permute-done((bf16[2048,512]{1,0:T(8,128)(2,1)}, bf16[2048,512]{1,0:T(8,128)(2,1)}, u32[]{:S(2)}, u32[]{:S(2)}) %collective-permute-start.8) | collective-permute-done | bytes 2097184 | tf_op jit(solution)/shard_map/ppermute | solution.py:535
  168.2 5.3 routing.1
  174.6 58.0 %experts_bwd.2 = (f32[2048,512]{1,0:T(8,128)}, f32[2048,512]{1,0:T(8,128)}, f32[4,512,1280]{2,1,0:T(8,128)}, f32[4,512,1280]{2,1,0:T(8,128)}, f32[4,1280,512]{2,...) custom-call(s32[2,8,128]{2,1,0:T(8,128)} %get-tuple-element.37.refs_0_, ...), custom_call_target="tpu_custom_call" | custom-call | flops 75161927680 | bytes 60000000 | tf_op jit(solution)/shard_map/experts_bwd/pallas_call | solution.py:512
  232.6 57.9 %experts_bwd.3 = (f32[2048,512]{1,0:T(8,128)}, f32[256,512]{1,0:T(8,128)}, f32[1792,512]{1,0:T(8,128)}, f32[4,512,1280]{2,1,0:T(8,128)}, f32[4,512,1280]{2,1,0:T...) custom-call(s32[2,8,128]{2,1,0:T(8,128)} %get-tuple-element.37.refs_, ...), custom_call_target="tpu_custom_call" | custom-call | flops 75161927680 | bytes 60000000 | tf_op jit(solution)/shard_map/experts_bwd/pallas_call | solution.py:512
  291.0 54.5 %experts_fwd.3 = (f32[2048,512]{1,0:T(8,128)}, f32[2048,512]{1,0:T(8,128)}) custom-call(s32[2,8,128]{2,1,0:T(8,128)} %get-tuple-element.37.refs_0_, s32[2,8,128]{2,1,0:T(8,128)} %get-tuple-element.38.refs_1_, s32[2,8,128]{2,1,0:T(8,128)} %get-tuple-element.39.refs_2_, s32[1]{0:T(128)} %bitcast.15.refs_3_, s32[2,2,8,4096]{3,2,1,0:T(8,128)} %get-tuple-element.40.refs_4_, ...), custom_call_target="tpu_custom_call" | custom-call | flops 28185722880 | bytes 60000000 | tf_op jit(solution)/shard_map/experts_fwd/pallas_call | solution.py:512
  345.7 54.7 %experts_fwd.2 = (f32[2048,512]{1,0:T(8,128)}, f32[2048,512]{1,0:T(8,128)}) custom-call(s32[2,8,128]{2,1,0:T(8,128)} %get-tuple-element.37.refs_0_, s32[2,8,128]{2,1,0:T(8,128)} %get-tuple-element.38.refs_1_, s32[2,8,128]{2,1,0:T(8,128)} %get-tuple-element.39.refs_2_, s32[1]{0:T(128)} %bitcast.15.refs_3_, s32[2,2,8,4096]{3,2,1,0:T(8,128)} %get-tuple-element.40.refs_4_, ...), custom_call_target="tpu_custom_call" | custom-call | flops 28185722880 | bytes 60000000 | tf_op jit(solution)/shard_map/experts_fwd/pallas_call | solution.py:512
  401.0 6.7 add.38
  407.7 76.8 %collective-permute-start.11 = (f32[2048,512]{1,0:T(8,128)}, f32[2048,512]{1,0:T(8,128)}, u32[]{:S(2)}, u32[]{:S(2)}) collective-permute-start(f32[2048,512]{1,0:T(8,128)} %add.38), channel_id=1, source_target_pairs={{0,2},{1,3},{2,0},{3,1},{4,6},{5,7},{6,4},{7,5}} | collective-permute-start | bytes 12582920 | tf_op jit(solution)/shard_map/ppermute | solution.py:535
  484.5 5.2 add.41
  490.3 5.6 bitcast_dynamic-update-slice_fusion
  495.9 80.4 %collective-permute-done.11 = f32[2048,512]{1,0:T(8,128)} collective-permute-done((f32[2048,512]{1,0:T(8,128)}, f32[2048,512]{1,0:T(8,128)}, u32[]{:S(2)}, u32[]{:S(2)}) %collective-permute-start.11) | collective-permute-done | bytes 4194336 | tf_op jit(solution)/shard_map/ppermute | solution.py:535
  576.3 6.6 add_convert_fusion
  582.9 50.5 %collective-permute-start.12 = (bf16[2048,512]{1,0:T(8,128)(2,1)}, bf16[2048,512]{1,0:T(8,128)(2,1)S(1)}, u32[]{:S(2)}, u32[]{:S(2)}) collective-permute-start(bf16[2048,512]{1,0:T(8,128)(2,1)} %add_convert_fusion), channel_id=1, source_target_pairs={{0,4},{4,0},{1,5},{5,1},{2,6},{6,2},{3,7},{7,3}} | collective-permute-start | bytes 6291464 | tf_op jit(solution)/shard_map/ppermute | solution.py:588
  633.4 5.2 bitcast_dynamic-update-slice_fusion.1
  638.6 26.9 %collective-permute-done.21.p_far = f32[2048,512]{1,0:T(8,128)} collective-permute-done((f32[2048,512]{1,0:T(8,128)}, f32[2048,512]{1,0:T(8,128)}, u32[]{:S(2)}, u32[]{:S(2)}) %collective-permute-start.21) | collective-permute-done | bytes 4194336 | tf_op jit(solution)/shard_map/ppermute | solution.py:535
  665.5 4.8 shard_map.155
  670.3 50.9 %collective-permute-start.22 = (bf16[256,512]{1,0:T(8,128)(2,1)}, bf16[256,512]{1,0:T(8,128)(2,1)S(1)}, u32[]{:S(2)}, u32[]{:S(2)}) collective-permute-start(bf16[256,512]{1,0:T(8,128)(2,1)} %shard_map.155), channel_id=1, source_target_pairs={{0,4},{4,0},{1,5},{5,1},{2,6},{6,2},{3,7},{7,3}} | collective-permute-start | bytes 786440 | tf_op jit(solution)/shard_map/ppermute | solution.py:594
  721.2 6.7 shard_map.156
  727.9 7.0 shard_map.157
  734.9 2.0 collective-permute-start.25
  736.9 8.6 %shard_map.158 = bf16[768,512]{1,0:T(8,128)(2,1)} custom-call(f32[2048,512]{1,0:T(8,128)} %get-tuple-element.54.p_own, f32[1792,512]{1,0:T(8,128)} %collective-permute-done.23.p_mate, f32[2048,512]{1,0:T(8,128)} %collective-permute-done.21.p_far, bf16[2048,512]{1,0:T(8,128)(2,1)} %get-tuple-element.58.mid_ref, bf16[2048,512]{1,0:T(8,128)(2,1)} %bitcast.52, ...), custom_call_target="tpu_custom_call" | custom-call | flops 2013265920 | bytes 6000000 | tf_op jit(solution)/shard_map/pallas_call | solution.py:444
  745.5 5.2 bitcast_dynamic-update-slice_fusion.2
  750.7 3.4 collective-permute-done.25
  754.2 15.4 %collective-permute-done.26 = bf16[768,512]{1,0:T(8,128)(2,1)S(1)} collective-permute-done((bf16[768,512]{1,0:T(8,128)(2,1)}, bf16[768,512]{1,0:T(8,128)(2,1)S(1)}, u32[]{:S(2)}, u32[]{:S(2)}) %collective-permute-start.26) | collective-permute-done | bytes 786464 | tf_op jit(solution)/shard_map/ppermute | solution.py:594
  769.6 1.5 maximum_bitcast_fusion
  (79 shorter events, 8.5 us)
Async XLA Ops:
  11.5 64.2 %collective-permute-start.15 = (bf16[2048,512]{1,0:T(8,128)(2,1)}, bf16[2048,512]{1,0:T(8,128)(2,1)}, u32[]{:S(2)}, u32[]{:S(2)}) collective-permute-start(bf16[2048,512]{1,0:T(8,128)(2,1)} %get-tuple-element.47.refs_6_), channel_id=1, source_target_pairs={{0,2},{1,3},{2,0},{3,1},{4,6},{5,7},{6,4},{7,5}} | collective-permute-start | bytes 6291464 | tf_op jit(solution)/shard_map/ppermute | solution.py:535
  14.8 159.3 %collective-permute-start.4 = (bf16[4,512,1280]{2,1,0:T(8,128)(2,1)}, bf16[4,512,1280]{2,1,0:T(8,128)(2,1)}, u32[]{:S(2)}, u32[]{:S(2)}) collective-permute-start(bf16[4,512,1280]{2,1,0:T(8,128)(2,1)} %bitcast.71), channel_id=1, source_target_pairs={{0,1},{1,0},{2,3},{3,2},{4,5},{5,4},{6,7},{7,6}} | collective-permute-start | bytes 15728648 | tf_op jit(solution)/shard_map/ppermute | solution.py:532
  14.8 159.4 %collective-permute-start.5 = (bf16[4,512,1280]{2,1,0:T(8,128)(2,1)}, bf16[4,512,1280]{2,1,0:T(8,128)(2,1)}, u32[]{:S(2)}, u32[]{:S(2)}) collective-permute-start(bf16[4,512,1280]{2,1,0:T(8,128)(2,1)} %bitcast.76), channel_id=1, source_target_pairs={{0,1},{1,0},{2,3},{3,2},{4,5},{5,4},{6,7},{7,6}} | collective-permute-start | bytes 15728648 | tf_op jit(solution)/shard_map/ppermute | solution.py:532
  15.3 159.3 %collective-permute-start.6 = (bf16[4,1280,512]{2,1,0:T(8,128)(2,1)}, bf16[4,1280,512]{2,1,0:T(8,128)(2,1)}, u32[]{:S(2)}, u32[]{:S(2)}) collective-permute-start(bf16[4,1280,512]{2,1,0:T(8,128)(2,1)} %bitcast.81), channel_id=1, source_target_pairs={{0,1},{1,0},{2,3},{3,2},{4,5},{5,4},{6,7},{7,6}} | collective-permute-start | bytes 15728648 | tf_op jit(solution)/shard_map/ppermute | solution.py:532
  15.4 23.4 %collective-permute-start = (f32[16,2048]{1,0:T(8,128)S(1)}, f32[16,2048]{1,0:T(8,128)S(1)}, u32[]{:S(2)}, u32[]{:S(2)}) collective-permute-start(f32[16,2048]{1,0:T(8,128)S(1)} %pad_maximum_fusion.tab0), channel_id=1, source_target_pairs={{0,1},{1,0},{2,3},{3,2},{4,5},{5,4},{6,7},{7,6}} | collective-permute-start | bytes 393224 | tf_op jit(solution)/shard_map/ppermute | solution.py:532
  38.8 24.6 %collective-permute-start.1 = (f32[16,2048]{1,0:T(8,128)S(1)}, f32[16,2048]{1,0:T(8,128)S(1)}, u32[]{:S(2)}, u32[]{:S(2)}) collective-permute-start(f32[16,2048]{1,0:T(8,128)S(1)} %pad_maximum_fusion.tab0), channel_id=1, source_target_pairs={{0,2},{1,3},{2,0},{3,1},{4,6},{5,7},{6,4},{7,5}} | collective-permute-start | bytes 393224 | tf_op jit(solution)/shard_map/ppermute | solution.py:535
  63.4 10.8 %collective-permute-start.2 = (f32[16,2048]{1,0:T(8,128)S(1)}, f32[16,2048]{1,0:T(8,128)S(1)}, u32[]{:S(2)}, u32[]{:S(2)}) collective-permute-start(f32[16,2048]{1,0:T(8,128)S(1)} %pad_maximum_fusion.tab0), channel_id=1, source_target_pairs={{0,3},{1,2},{2,1},{3,0},{4,7},{5,6},{6,5},{7,4}} | collective-permute-start | bytes 393224 | tf_op jit(solution)/shard_map/ppermute | solution.py:558
  74.2 94.0 %copy-start.8 = (f32[16,2048]{1,0:T(8,128)}, f32[16,2048]{1,0:T(8,128)S(1)}, u32[]{:S(2)}) copy-start(f32[16,2048]{1,0:T(8,128)S(1)} %collective-permute-done.2.tab3) | copy-start | bytes 393220
  74.2 48.1 %collective-permute-start.17 = (bf16[2048,512]{1,0:T(8,128)(2,1)S(1)}, bf16[2048,512]{1,0:T(8,128)(2,1)}, u32[]{:S(2)}, u32[]{:S(2)}) collective-permute-start(bf16[2048,512]{1,0:T(8,128)(2,1)S(1)} %bitcast.53), channel_id=1, source_target_pairs={{0,2},{1,3},{2,0},{3,1},{4,6},{5,7},{6,4},{7,5}} | collective-permute-start | bytes 6291464 | tf_op jit(solution)/shard_map/ppermute | solution.py:535
  75.7 91.6 %collective-permute-start.8 = (bf16[2048,512]{1,0:T(8,128)(2,1)}, bf16[2048,512]{1,0:T(8,128)(2,1)}, u32[]{:S(2)}, u32[]{:S(2)}) collective-permute-start(bf16[2048,512]{1,0:T(8,128)(2,1)} %get-tuple-element.42.refs_6_), channel_id=1, source_target_pairs={{0,2},{1,3},{2,0},{3,1},{4,6},{5,7},{6,4},{7,5}} | collective-permute-start | bytes 6291464 | tf_op jit(solution)/shard_map/ppermute | solution.py:535
  122.3 51.2 %collective-permute-start.16 = (bf16[2048,512]{1,0:T(8,128)(2,1)}, bf16[2048,512]{1,0:T(8,128)(2,1)}, u32[]{:S(2)}, u32[]{:S(2)}) collective-permute-start(bf16[2048,512]{1,0:T(8,128)(2,1)} %collective-permute-done.15.refs_6_), channel_id=1, source_target_pairs={{0,1},{1,0},{2,3},{3,2},{4,5},{5,4},{6,7},{7,6}} | collective-permute-start | bytes 6291464 | tf_op jit(solution)/shard_map/ppermute | solution.py:532
  167.3 6.4 collective-permute-start.18
  173.5 59.0 %collective-permute-start.13 = (bf16[2048,512]{1,0:T(8,128)(2,1)}, bf16[2048,512]{1,0:T(8,128)(2,1)}, u32[]{:S(2)}, u32[]{:S(2)}) collective-permute-start(bf16[2048,512]{1,0:T(8,128)(2,1)} %get-tuple-element.47.refs_6_), channel_id=1, source_target_pairs={{0,1},{1,0},{2,3},{3,2},{4,5},{5,4},{6,7},{7,6}} | collective-permute-start | bytes 6291464 | tf_op jit(solution)/shard_map/ppermute | solution.py:532
  173.7 58.9 %collective-permute-start.14 = (bf16[2048,512]{1,0:T(8,128)(2,1)S(1)}, bf16[2048,512]{1,0:T(8,128)(2,1)}, u32[]{:S(2)}, u32[]{:S(2)}) collective-permute-start(bf16[2048,512]{1,0:T(8,128)(2,1)S(1)} %bitcast.54), channel_id=1, source_target_pairs={{0,1},{1,0},{2,3},{3,2},{4,5},{5,4},{6,7},{7,6}} | collective-permute-start | bytes 6291464 | tf_op jit(solution)/shard_map/ppermute | solution.py:532
  174.0 171.7 %collective-permute-start.3 = (bf16[2048,512]{1,0:T(8,128)(2,1)}, bf16[2048,512]{1,0:T(8,128)(2,1)}, u32[]{:S(2)}, u32[]{:S(2)}) collective-permute-start(bf16[2048,512]{1,0:T(8,128)(2,1)} %get-tuple-element.42.refs_6_), channel_id=1, source_target_pairs={{0,1},{1,0},{2,3},{3,2},{4,5},{5,4},{6,7},{7,6}} | collective-permute-start | bytes 6291464 | tf_op jit(solution)/shard_map/ppermute | solution.py:532
  174.2 116.9 %collective-permute-start.9 = (bf16[2048,512]{1,0:T(8,128)(2,1)}, bf16[2048,512]{1,0:T(8,128)(2,1)}, u32[]{:S(2)}, u32[]{:S(2)}) collective-permute-start(bf16[2048,512]{1,0:T(8,128)(2,1)} %collective-permute-done.8.refs_6_), channel_id=1, source_target_pairs={{0,1},{1,0},{2,3},{3,2},{4,5},{5,4},{6,7},{7,6}} | collective-permute-start | bytes 6291464 | tf_op jit(solution)/shard_map/ppermute | solution.py:532
  290.5 199.2 %collective-permute-start.29 = (f32[2,1280,512]{2,1,0:T(8,128)}, f32[2,1280,512]{2,1,0:T(8,128)}, u32[]{:S(2)}, u32[]{:S(2)}) collective-permute-start(f32[2,1280,512]{2,1,0:T(8,128)} %get-tuple-element.66), channel_id=1, source_target_pairs={{0,1},{1,0},{2,3},{3,2},{4,5},{5,4},{6,7},{7,6}} | collective-permute-start | bytes 15728648 | tf_op jit(solution)/shard_map/ppermute | solution.py:532
  290.5 194.0 %collective-permute-start.20 = (f32[2048,512]{1,0:T(8,128)}, f32[2048,512]{1,0:T(8,128)}, u32[]{:S(2)}, u32[]{:S(2)}) collective-permute-start(f32[2048,512]{1,0:T(8,128)} %get-tuple-element.57), channel_id=1, source_target_pairs={{0,1},{1,0},{2,3},{3,2},{4,5},{5,4},{6,7},{7,6}} | collective-permute-start | bytes 12582920 | tf_op jit(solution)/shard_map/ppermute | solution.py:532
  345.6 55.4 %collective-permute-start.10 = (f32[2048,512]{1,0:T(8,128)}, f32[2048,512]{1,0:T(8,128)}, u32[]{:S(2)}, u32[]{:S(2)}) collective-permute-start(f32[2048,512]{1,0:T(8,128)} %get-tuple-element.46), channel_id=1, source_target_pairs={{0,1},{1,0},{2,3},{3,2},{4,5},{5,4},{6,7},{7,6}} | collective-permute-start | bytes 12582920 | tf_op jit(solution)/shard_map/ppermute | solution.py:532
  400.4 89.3 %collective-permute-start.7 = (f32[2048,512]{1,0:T(8,128)}, f32[2048,512]{1,0:T(8,128)}, u32[]{:S(2)}, u32[]{:S(2)}) collective-permute-start(f32[2048,512]{1,0:T(8,128)} %get-tuple-element.44), channel_id=1, source_target_pairs={{0,1},{1,0},{2,3},{3,2},{4,5},{5,4},{6,7},{7,6}} | collective-permute-start | bytes 12582920 | tf_op jit(solution)/shard_map/ppermute | solution.py:532
  400.9 182.0 %collective-permute-start.28 = (f32[2,512,1280]{2,1,0:T(8,128)}, f32[2,512,1280]{2,1,0:T(8,128)}, u32[]{:S(2)}, u32[]{:S(2)}) collective-permute-start(f32[2,512,1280]{2,1,0:T(8,128)} %get-tuple-element.64), channel_id=1, source_target_pairs={{0,1},{1,0},{2,3},{3,2},{4,5},{5,4},{6,7},{7,6}} | collective-permute-start | bytes 15728648 | tf_op jit(solution)/shard_map/ppermute | solution.py:532
  407.7 168.6 %collective-permute-start.11 = (f32[2048,512]{1,0:T(8,128)}, f32[2048,512]{1,0:T(8,128)}, u32[]{:S(2)}, u32[]{:S(2)}) collective-permute-start(f32[2048,512]{1,0:T(8,128)} %add.38), channel_id=1, source_target_pairs={{0,2},{1,3},{2,0},{3,1},{4,6},{5,7},{6,4},{7,5}} | collective-permute-start | bytes 12582920 | tf_op jit(solution)/shard_map/ppermute | solution.py:535
  484.5 260.9 %collective-permute-start.27 = (f32[2,512,1280]{2,1,0:T(8,128)}, f32[2,512,1280]{2,1,0:T(8,128)}, u32[]{:S(2)}, u32[]{:S(2)}) collective-permute-start(f32[2,512,1280]{2,1,0:T(8,128)} %get-tuple-element.62), channel_id=1, source_target_pairs={{0,1},{1,0},{2,3},{3,2},{4,5},{5,4},{6,7},{7,6}} | collective-permute-start | bytes 15728648 | tf_op jit(solution)/shard_map/ppermute | solution.py:532
  489.7 175.8 %collective-permute-start.21 = (f32[2048,512]{1,0:T(8,128)}, f32[2048,512]{1,0:T(8,128)}, u32[]{:S(2)}, u32[]{:S(2)}) collective-permute-start(f32[2048,512]{1,0:T(8,128)} %add.41), channel_id=1, source_target_pairs={{0,2},{1,3},{2,0},{3,1},{4,6},{5,7},{6,4},{7,5}} | collective-permute-start | bytes 12582920 | tf_op jit(solution)/shard_map/ppermute | solution.py:535
  489.8 231.5 %collective-permute-start.23 = (f32[1792,512]{1,0:T(8,128)}, f32[1792,512]{1,0:T(8,128)}, u32[]{:S(2)}, u32[]{:S(2)}) collective-permute-start(f32[1792,512]{1,0:T(8,128)} %get-tuple-element.60), channel_id=1, source_target_pairs={{0,1},{1,0},{2,3},{3,2},{4,5},{5,4},{6,7},{7,6}} | collective-permute-start | bytes 11010056 | tf_op jit(solution)/shard_map/ppermute | solution.py:532
  490.2 86.0 %copy-start.3 = (bf16[2048,512]{1,0:T(8,128)(2,1)S(1)}, bf16[2048,512]{1,0:T(8,128)(2,1)}, u32[]{:S(2)}) copy-start(bf16[2048,512]{1,0:T(8,128)(2,1)} %get-tuple-element.36) | copy-start | bytes 6291460
  576.3 62.4 %collective-permute-start.19 = (f32[256,512]{1,0:T(8,128)S(1)}, f32[256,512]{1,0:T(8,128)S(1)}, u32[]{:S(2)}, u32[]{:S(2)}) collective-permute-start(f32[256,512]{1,0:T(8,128)S(1)} %copy-done.13), channel_id=1, source_target_pairs={{0,1},{1,0},{2,3},{3,2},{4,5},{5,4},{6,7},{7,6}} | collective-permute-start | bytes 1572872 | tf_op jit(solution)/shard_map/ppermute | solution.py:532
  582.9 188.1 %collective-permute-start.12 = (bf16[2048,512]{1,0:T(8,128)(2,1)}, bf16[2048,512]{1,0:T(8,128)(2,1)S(1)}, u32[]{:S(2)}, u32[]{:S(2)}) collective-permute-start(bf16[2048,512]{1,0:T(8,128)(2,1)} %add_convert_fusion), channel_id=1, source_target_pairs={{0,4},{4,0},{1,5},{5,1},{2,6},{6,2},{3,7},{7,3}} | collective-permute-start | bytes 6291464 | tf_op jit(solution)/shard_map/ppermute | solution.py:588
  670.3 80.4 %collective-permute-start.22 = (bf16[256,512]{1,0:T(8,128)(2,1)}, bf16[256,512]{1,0:T(8,128)(2,1)S(1)}, u32[]{:S(2)}, u32[]{:S(2)}) collective-permute-start(bf16[256,512]{1,0:T(8,128)(2,1)} %shard_map.155), channel_id=1, source_target_pairs={{0,4},{4,0},{1,5},{5,1},{2,6},{6,2},{3,7},{7,3}} | collective-permute-start | bytes 786440 | tf_op jit(solution)/shard_map/ppermute | solution.py:594
  727.9 22.8 %collective-permute-start.24 = (bf16[512,512]{1,0:T(8,128)(2,1)}, bf16[512,512]{1,0:T(8,128)(2,1)S(1)}, u32[]{:S(2)}, u32[]{:S(2)}) collective-permute-start(bf16[512,512]{1,0:T(8,128)(2,1)} %shard_map.156), channel_id=1, source_target_pairs={{0,4},{4,0},{1,5},{5,1},{2,6},{6,2},{3,7},{7,3}} | collective-permute-start | bytes 1572872 | tf_op jit(solution)/shard_map/ppermute | solution.py:594
  734.9 19.2 %collective-permute-start.25 = (bf16[512,512]{1,0:T(8,128)(2,1)}, bf16[512,512]{1,0:T(8,128)(2,1)S(1)}, u32[]{:S(2)}, u32[]{:S(2)}) collective-permute-start(bf16[512,512]{1,0:T(8,128)(2,1)} %shard_map.157), channel_id=1, source_target_pairs={{0,4},{4,0},{1,5},{5,1},{2,6},{6,2},{3,7},{7,3}} | collective-permute-start | bytes 1572872 | tf_op jit(solution)/shard_map/ppermute | solution.py:594
  745.5 24.1 %collective-permute-start.26 = (bf16[768,512]{1,0:T(8,128)(2,1)}, bf16[768,512]{1,0:T(8,128)(2,1)S(1)}, u32[]{:S(2)}, u32[]{:S(2)}) collective-permute-start(bf16[768,512]{1,0:T(8,128)(2,1)} %shard_map.158), channel_id=1, source_target_pairs={{0,4},{4,0},{1,5},{5,1},{2,6},{6,2},{3,7},{7,3}} | collective-permute-start | bytes 2359304 | tf_op jit(solution)/shard_map/ppermute | solution.py:594
  (12 other events, 456.5 us)

commit v7 on v6

--- a/solution.py
+++ b/solution.py
@@ -17,8 +17,8 @@
 CHUNK = 256
 OUT_ROWS = 256
 DW_SLOTS = 3
-TAIL = (0, 1, 3, 5, 8)
-DENSE_ROWS = 512
+TAIL = (0, 2, 6, 10, 16)
+DENSE_ROWS = 256
 E_RUN = 4
 
 f32 = jnp.float32
@@ -341,12 +341,15 @@
 
         start = jnp.zeros((2 * E_RUN, 128), i32)
         nwin = jnp.ones((2 * E_RUN, 128), i32)
-        for j in range(n_sub):
+
+        def one_sub(j, tables):
+            start, nwin = tables
             lo = jnp.minimum(tokens_upto(j * SUB), n2 - 1) // ALIGN * ALIGN
             hi = tokens_upto(jnp.minimum((j + 1) * SUB, cnt) - 1) + 1
             n = jnp.maximum((hi - lo - WIN + WIN_MORE - 1) // WIN_MORE, 0) + 1
-            start = jnp.where(lane == j, lo, start)
-            nwin = jnp.where(lane == j, n, nwin)
+            return jnp.where(lane == j, lo, start), jnp.where(lane == j, n, nwin)
+
+        start, nwin = lax.fori_loop(0, n_sub, one_sub, (start, nwin))
         start_ref[mb] = start
         nwin_ref[mb] = nwin
         tile_rows = SUB * TILE_SUBS[mb]
@@ -445,7 +448,7 @@
         tail_kernel,
         grid=(steps,),
         out_shape=jax.ShapeDtypeStruct((rows * steps, width), bf16),
-        in_specs=[row, pl.BlockSpec((rows, width), lambda i: (first + i if chunk == 0 else first + i - 1, 0))] + [row] * 4 + [pl.BlockSpec((rows, ff), lambda i: (first + i, 0)),
+        in_specs=[row, pl.BlockSpec((rows, width), lambda i: (first + i if chunk == 0 else first + i - OUT_ROWS // rows, 0))] + [row] * 4 + [pl.BlockSpec((rows, ff), lambda i: (first + i, 0)),
                               pl.BlockSpec((width, ff), lambda i: (0, 0)), pl.BlockSpec((ff, width), lambda i: (0, 0))],
         out_specs=pl.BlockSpec((rows, width), lambda i: (i, 0)),
         scratch_shapes=[pltpu.VMEM((rows, ff), bf16)],

time: 779 us -> 782 us (level)
  Pallas kernels: 279 us -> 291 us
  transfers between devices with their start and end apart: 30 -> 30, of which waited for: 8 -> 8; matrix products, arithmetic and copies ran while one was open for 5% -> 5% of each run, Pallas kernels for 35% -> 36%
where the time goes in v7:
time: 782 us
  Pallas kernels  291 us (37%)
  waiting for transfers between devices  260 us (33%)
  starting transfers between devices  191 us (24%)
  other arithmetic  20.6 us (3%)
  local copies, waits for them, and re-layouts  17.3 us (2%)
    pallas_call x4, Pallas kernels, run_experts(): pl.pallas_call(functools.partial(expert_kernel, bwd, carry, E_RUN if far...  225 us
    ppermute x6, waiting for transfers between devices, to_cross(): return lax.ppermute(v, 'ep', [(i, i ^ 2) for i in range(n_ep)])  222 us
    ppermute x6, starting transfers between devices, to_cross(): return lax.ppermute(v, 'ep', [(i, i ^ 2) for i in range(n_ep)])  82.2 us
    ppermute x4, starting transfers between devices, device_fn(): dx_parts.append(lax.ppermute(dx_val, 'pp', bwd_perm))  53 us
    ppermute x1, starting transfers between devices, device_fn(): y_next = lax.ppermute(y_val, 'pp', fwd_perm)  50.6 us
    pallas_call x4, Pallas kernels, run_tail(): pl.pallas_call(tail_kernel, grid=(steps,), out_shape=jax.ShapeDtypeStruct...  31.9 us
    pallas_call x2, Pallas kernels, run_dense(): pl.pallas_call(dense_kernel, grid=(n_tok // DENSE_ROWS,), out_shape=out_s...  23.7 us
    ppermute x18, waiting for transfers between devices, to_mate(): return lax.ppermute(v, 'ep', [(i, i ^ 1) for i in range(n_ep)])  22.9 us
  transfers between devices with their start and end apart: 30, of which 8 were waited for; matrix products, arithmetic and copies ran while one was open for 5% of the time, Pallas kernels for 36%

profile of v7, /device:TPU:0, one launch (start us, length us, event | category | flops | bytes accessed | tf_op | source)
XLA Modules:
  0.0 781.7 jit_solution(15673125855524818183)
XLA Ops:
  0.7 11.8 %dense_fwd.3 = (bf16[2048,512]{1,0:T(8,128)(2,1)}, bf16[2048,512]{1,0:T(8,128)(2,1)}, bf16[2048,1280]{1,0:T(8,128)(2,1)}) custom-call(bf16[2048,512]{1,0:T(8,128)(2,1)} %bitcast.43, bf16[512,1280]{1,0:T(8,128)(2,1)} %bitcast.55, bf16[1280,512]{1,0:T(8,128)(2,1)} %bitcast.61), custom_call_target="tpu_custom_call" | custom-call | flops 5368709120 | bytes 12000000 | tf_op jit(solution)/shard_map/dense_fwd/pallas_call | solution.py:416
  12.5 3.3 collective-permute-start.15
  17.0 22.9 %collective-permute-done.tab1 = f32[16,2048]{1,0:T(8,128)S(1)} collective-permute-done((f32[16,2048]{1,0:T(8,128)S(1)}, f32[16,2048]{1,0:T(8,128)S(1)}, u32[]{:S(2)}, u32[]{:S(2)}) %collective-permute-start) | collective-permute-done | bytes 131104 | tf_op jit(solution)/shard_map/ppermute | solution.py:535
  39.9 24.6 %collective-permute-done.1.tab2 = f32[16,2048]{1,0:T(8,128)S(1)} collective-permute-done((f32[16,2048]{1,0:T(8,128)S(1)}, f32[16,2048]{1,0:T(8,128)S(1)}, u32[]{:S(2)}, u32[]{:S(2)}) %collective-permute-start.1) | collective-permute-done | bytes 131104 | tf_op jit(solution)/shard_map/ppermute | solution.py:538
  64.8 11.8 %dense_fwd.2 = (bf16[2048,512]{1,0:T(8,128)(2,1)}, bf16[2048,512]{1,0:T(8,128)(2,1)}) custom-call(bf16[2048,512]{1,0:T(8,128)(2,1)} %bitcast.86, bf16[512,1280]{1,0:T(8,128)(2,1)} %bitcast.56, bf16[1280,512]{1,0:T(8,128)(2,1)} %bitcast.62), custom_call_target="tpu_custom_call" | custom-call | flops 5368709120 | bytes 12000000 | tf_op jit(solution)/shard_map/dense_fwd/pallas_call | solution.py:416
  76.7 1.4 collective-permute-start.17
  78.8 46.0 %collective-permute-done.17.refs_8_ = bf16[2048,512]{1,0:T(8,128)(2,1)} collective-permute-done((bf16[2048,512]{1,0:T(8,128)(2,1)S(1)}, bf16[2048,512]{1,0:T(8,128)(2,1)}, u32[]{:S(2)}, u32[]{:S(2)}) %collective-permute-start.17) | collective-permute-done | bytes 2097184 | tf_op jit(solution)/shard_map/ppermute | solution.py:538
  126.0 43.7 %collective-permute-done.8.refs_6_ = bf16[2048,512]{1,0:T(8,128)(2,1)} collective-permute-done((bf16[2048,512]{1,0:T(8,128)(2,1)}, bf16[2048,512]{1,0:T(8,128)(2,1)}, u32[]{:S(2)}, u32[]{:S(2)}) %collective-permute-start.8) | collective-permute-done | bytes 2097184 | tf_op jit(solution)/shard_map/ppermute | solution.py:538
  170.7 10.5 %routing.1 = (s32[2,2,8,4096]{3,2,1,0:T(8,128)}, f32[2,2,8,4096]{3,2,1,0:T(8,128)}, s32[2,8,128]{2,1,0:T(8,128)}, s32[2,8,128]{2,1,0:T(8,128)}, s32[2,8,128]{2,1,0:T(8,128)}) custom-call(s32[4]{0:T(128)} %pad_add_fusion.who_ref, f32[16,2048]{1,0:T(8,128)} %copy-done.5, f32[16,2048]{1,0:T(8,128)} %copy-done.6, f32[16,2048]{1,0:T(8,128)} %copy-done.7, ...), custom_call_target="tpu_custom_call" | custom-call | tf_op jit(solution)/shard_map/routing/pallas_call | solution.py:365
  182.2 58.0 %experts_bwd.2 = (f32[2048,512]{1,0:T(8,128)}, f32[2048,512]{1,0:T(8,128)}, f32[4,512,1280]{2,1,0:T(8,128)}, f32[4,512,1280]{2,1,0:T(8,128)}, f32[4,1280,512]{2,...) custom-call(s32[2,8,128]{2,1,0:T(8,128)} %get-tuple-element.37.refs_0_, ...), custom_call_target="tpu_custom_call" | custom-call | flops 75161927680 | bytes 60000000 | tf_op jit(solution)/shard_map/experts_bwd/pallas_call | solution.py:515
  240.2 57.8 %experts_bwd.3 = (f32[2048,512]{1,0:T(8,128)}, f32[256,512]{1,0:T(8,128)}, f32[1792,512]{1,0:T(8,128)}, f32[4,512,1280]{2,1,0:T(8,128)}, f32[4,512,1280]{2,1,0:T...) custom-call(s32[2,8,128]{2,1,0:T(8,128)} %get-tuple-element.37.refs_, ...), custom_call_target="tpu_custom_call" | custom-call | flops 75161927680 | bytes 60000000 | tf_op jit(solution)/shard_map/experts_bwd/pallas_call | solution.py:515
  298.5 54.5 %experts_fwd.3 = (f32[2048,512]{1,0:T(8,128)}, f32[2048,512]{1,0:T(8,128)}) custom-call(s32[2,8,128]{2,1,0:T(8,128)} %get-tuple-element.37.refs_0_, s32[2,8,128]{2,1,0:T(8,128)} %get-tuple-element.38.refs_1_, s32[2,8,128]{2,1,0:T(8,128)} %get-tuple-element.39.refs_2_, s32[1]{0:T(128)} %bitcast.15.refs_3_, s32[2,2,8,4096]{3,2,1,0:T(8,128)} %get-tuple-element.40.refs_4_, ...), custom_call_target="tpu_custom_call" | custom-call | flops 28185722880 | bytes 60000000 | tf_op jit(solution)/shard_map/experts_fwd/pallas_call | solution.py:515
  353.2 54.7 %experts_fwd.2 = (f32[2048,512]{1,0:T(8,128)}, f32[2048,512]{1,0:T(8,128)}) custom-call(s32[2,8,128]{2,1,0:T(8,128)} %get-tuple-element.37.refs_0_, s32[2,8,128]{2,1,0:T(8,128)} %get-tuple-element.38.refs_1_, s32[2,8,128]{2,1,0:T(8,128)} %get-tuple-element.39.refs_2_, s32[1]{0:T(128)} %bitcast.15.refs_3_, s32[2,2,8,4096]{3,2,1,0:T(8,128)} %get-tuple-element.40.refs_4_, ...), custom_call_target="tpu_custom_call" | custom-call | flops 28185722880 | bytes 60000000 | tf_op jit(solution)/shard_map/experts_fwd/pallas_call | solution.py:515
  408.5 6.7 add.38
  415.2 76.8 %collective-permute-start.11 = (f32[2048,512]{1,0:T(8,128)}, f32[2048,512]{1,0:T(8,128)}, u32[]{:S(2)}, u32[]{:S(2)}) collective-permute-start(f32[2048,512]{1,0:T(8,128)} %add.38), channel_id=1, source_target_pairs={{0,2},{1,3},{2,0},{3,1},{4,6},{5,7},{6,4},{7,5}} | collective-permute-start | bytes 12582920 | tf_op jit(solution)/shard_map/ppermute | solution.py:538
  492.0 5.2 add.41
  497.7 5.6 bitcast_dynamic-update-slice_fusion
  503.3 80.4 %collective-permute-done.11 = f32[2048,512]{1,0:T(8,128)} collective-permute-done((f32[2048,512]{1,0:T(8,128)}, f32[2048,512]{1,0:T(8,128)}, u32[]{:S(2)}, u32[]{:S(2)}) %collective-permute-start.11) | collective-permute-done | bytes 4194336 | tf_op jit(solution)/shard_map/ppermute | solution.py:538
  583.7 6.6 add_convert_fusion
  590.4 50.6 %collective-permute-start.12 = (bf16[2048,512]{1,0:T(8,128)(2,1)}, bf16[2048,512]{1,0:T(8,128)(2,1)S(1)}, u32[]{:S(2)}, u32[]{:S(2)}) collective-permute-start(bf16[2048,512]{1,0:T(8,128)(2,1)} %add_convert_fusion), channel_id=1, source_target_pairs={{0,4},{4,0},{1,5},{5,1},{2,6},{6,2},{3,7},{7,3}} | collective-permute-start | bytes 6291464 | tf_op jit(solution)/shard_map/ppermute | solution.py:591
  640.9 5.2 bitcast_dynamic-update-slice_fusion.1
  646.1 26.8 %collective-permute-done.21.p_far = f32[2048,512]{1,0:T(8,128)} collective-permute-done((f32[2048,512]{1,0:T(8,128)}, f32[2048,512]{1,0:T(8,128)}, u32[]{:S(2)}, u32[]{:S(2)}) %collective-permute-start.21) | collective-permute-done | bytes 4194336 | tf_op jit(solution)/shard_map/ppermute | solution.py:538
  672.9 5.4 shard_map.155
  678.3 50.9 %collective-permute-start.22 = (bf16[256,512]{1,0:T(8,128)(2,1)}, bf16[256,512]{1,0:T(8,128)(2,1)S(1)}, u32[]{:S(2)}, u32[]{:S(2)}) collective-permute-start(bf16[256,512]{1,0:T(8,128)(2,1)} %shard_map.155), channel_id=1, source_target_pairs={{0,4},{4,0},{1,5},{5,1},{2,6},{6,2},{3,7},{7,3}} | collective-permute-start | bytes 786440 | tf_op jit(solution)/shard_map/ppermute | solution.py:597
  729.3 8.0 %shard_map.156 = bf16[512,512]{1,0:T(8,128)(2,1)} custom-call(f32[2048,512]{1,0:T(8,128)} %get-tuple-element.54.p_own, f32[1792,512]{1,0:T(8,128)} %collective-permute-done.23.p_mate, f32[2048,512]{1,0:T(8,128)} %collective-permute-done.21.p_far, bf16[2048,512]{1,0:T(8,128)(2,1)} %get-tuple-element.58.mid_ref, bf16[2048,512]{1,0:T(8,128)(2,1)} %bitcast.50, ...), custom_call_target="tpu_custom_call" | custom-call | flops 1342177280 | bytes 6000000 | tf_op jit(solution)/shard_map/pallas_call | solution.py:447
  737.3 8.0 %shard_map.157 = bf16[512,512]{1,0:T(8,128)(2,1)} custom-call(f32[2048,512]{1,0:T(8,128)} %get-tuple-element.54.p_own, f32[1792,512]{1,0:T(8,128)} %collective-permute-done.23.p_mate, f32[2048,512]{1,0:T(8,128)} %collective-permute-done.21.p_far, bf16[2048,512]{1,0:T(8,128)(2,1)} %get-tuple-element.58.mid_ref, bf16[2048,512]{1,0:T(8,128)(2,1)} %bitcast.51, ...), custom_call_target="tpu_custom_call" | custom-call | flops 1342177280 | bytes 6000000 | tf_op jit(solution)/shard_map/pallas_call | solution.py:447
  745.3 2.0 collective-permute-start.25
  747.2 10.5 %shard_map.158 = bf16[768,512]{1,0:T(8,128)(2,1)} custom-call(f32[2048,512]{1,0:T(8,128)} %get-tuple-element.54.p_own, f32[1792,512]{1,0:T(8,128)} %collective-permute-done.23.p_mate, f32[2048,512]{1,0:T(8,128)} %collective-permute-done.21.p_far, bf16[2048,512]{1,0:T(8,128)(2,1)} %get-tuple-element.58.mid_ref, bf16[2048,512]{1,0:T(8,128)(2,1)} %bitcast.52, ...), custom_call_target="tpu_custom_call" | custom-call | flops 2013265920 | bytes 6000000 | tf_op jit(solution)/shard_map/pallas_call | solution.py:447
  757.8 5.2 bitcast_dynamic-update-slice_fusion.2
  763.5 15.4 %collective-permute-done.26 = bf16[768,512]{1,0:T(8,128)(2,1)S(1)} collective-permute-done((bf16[768,512]{1,0:T(8,128)(2,1)}, bf16[768,512]{1,0:T(8,128)(2,1)S(1)}, u32[]{:S(2)}, u32[]{:S(2)}) %collective-permute-start.26) | collective-permute-done | bytes 786464 | tf_op jit(solution)/shard_map/ppermute | solution.py:597
  778.9 1.5 maximum_bitcast_fusion
  780.4 1.3 copy.21
  (79 shorter events, 7.6 us)
Async XLA Ops:
  12.5 65.6 %collective-permute-start.15 = (bf16[2048,512]{1,0:T(8,128)(2,1)}, bf16[2048,512]{1,0:T(8,128)(2,1)}, u32[]{:S(2)}, u32[]{:S(2)}) collective-permute-start(bf16[2048,512]{1,0:T(8,128)(2,1)} %get-tuple-element.47.refs_6_), channel_id=1, source_target_pairs={{0,2},{1,3},{2,0},{3,1},{4,6},{5,7},{6,4},{7,5}} | collective-permute-start | bytes 6291464 | tf_op jit(solution)/shard_map/ppermute | solution.py:538
  15.8 165.9 %collective-permute-start.4 = (bf16[4,512,1280]{2,1,0:T(8,128)(2,1)}, bf16[4,512,1280]{2,1,0:T(8,128)(2,1)}, u32[]{:S(2)}, u32[]{:S(2)}) collective-permute-start(bf16[4,512,1280]{2,1,0:T(8,128)(2,1)} %bitcast.71), channel_id=1, source_target_pairs={{0,1},{1,0},{2,3},{3,2},{4,5},{5,4},{6,7},{7,6}} | collective-permute-start | bytes 15728648 | tf_op jit(solution)/shard_map/ppermute | solution.py:535
  15.8 166.0 %collective-permute-start.5 = (bf16[4,512,1280]{2,1,0:T(8,128)(2,1)}, bf16[4,512,1280]{2,1,0:T(8,128)(2,1)}, u32[]{:S(2)}, u32[]{:S(2)}) collective-permute-start(bf16[4,512,1280]{2,1,0:T(8,128)(2,1)} %bitcast.76), channel_id=1, source_target_pairs={{0,1},{1,0},{2,3},{3,2},{4,5},{5,4},{6,7},{7,6}} | collective-permute-start | bytes 15728648 | tf_op jit(solution)/shard_map/ppermute | solution.py:535
  16.3 165.9 %collective-permute-start.6 = (bf16[4,1280,512]{2,1,0:T(8,128)(2,1)}, bf16[4,1280,512]{2,1,0:T(8,128)(2,1)}, u32[]{:S(2)}, u32[]{:S(2)}) collective-permute-start(bf16[4,1280,512]{2,1,0:T(8,128)(2,1)} %bitcast.81), channel_id=1, source_target_pairs={{0,1},{1,0},{2,3},{3,2},{4,5},{5,4},{6,7},{7,6}} | collective-permute-start | bytes 15728648 | tf_op jit(solution)/shard_map/ppermute | solution.py:535
  16.5 23.4 %collective-permute-start = (f32[16,2048]{1,0:T(8,128)S(1)}, f32[16,2048]{1,0:T(8,128)S(1)}, u32[]{:S(2)}, u32[]{:S(2)}) collective-permute-start(f32[16,2048]{1,0:T(8,128)S(1)} %pad_maximum_fusion.tab0), channel_id=1, source_target_pairs={{0,1},{1,0},{2,3},{3,2},{4,5},{5,4},{6,7},{7,6}} | collective-permute-start | bytes 393224 | tf_op jit(solution)/shard_map/ppermute | solution.py:535
  39.9 24.6 %collective-permute-start.1 = (f32[16,2048]{1,0:T(8,128)S(1)}, f32[16,2048]{1,0:T(8,128)S(1)}, u32[]{:S(2)}, u32[]{:S(2)}) collective-permute-start(f32[16,2048]{1,0:T(8,128)S(1)} %pad_maximum_fusion.tab0), channel_id=1, source_target_pairs={{0,2},{1,3},{2,0},{3,1},{4,6},{5,7},{6,4},{7,5}} | collective-permute-start | bytes 393224 | tf_op jit(solution)/shard_map/ppermute | solution.py:538
  64.5 12.2 %collective-permute-start.2 = (f32[16,2048]{1,0:T(8,128)S(1)}, f32[16,2048]{1,0:T(8,128)S(1)}, u32[]{:S(2)}, u32[]{:S(2)}) collective-permute-start(f32[16,2048]{1,0:T(8,128)S(1)} %pad_maximum_fusion.tab0), channel_id=1, source_target_pairs={{0,3},{1,2},{2,1},{3,0},{4,7},{5,6},{6,5},{7,4}} | collective-permute-start | bytes 393224 | tf_op jit(solution)/shard_map/ppermute | solution.py:561
  76.7 94.0 %copy-start.8 = (f32[16,2048]{1,0:T(8,128)}, f32[16,2048]{1,0:T(8,128)S(1)}, u32[]{:S(2)}) copy-start(f32[16,2048]{1,0:T(8,128)S(1)} %collective-permute-done.2.tab3) | copy-start | bytes 393220
  76.7 48.1 %collective-permute-start.17 = (bf16[2048,512]{1,0:T(8,128)(2,1)S(1)}, bf16[2048,512]{1,0:T(8,128)(2,1)}, u32[]{:S(2)}, u32[]{:S(2)}) collective-permute-start(bf16[2048,512]{1,0:T(8,128)(2,1)S(1)} %bitcast.53), channel_id=1, source_target_pairs={{0,2},{1,3},{2,0},{3,1},{4,6},{5,7},{6,4},{7,5}} | collective-permute-start | bytes 6291464 | tf_op jit(solution)/shard_map/ppermute | solution.py:538
  78.2 91.6 %collective-permute-start.8 = (bf16[2048,512]{1,0:T(8,128)(2,1)}, bf16[2048,512]{1,0:T(8,128)(2,1)}, u32[]{:S(2)}, u32[]{:S(2)}) collective-permute-start(bf16[2048,512]{1,0:T(8,128)(2,1)} %get-tuple-element.42.refs_6_), channel_id=1, source_target_pairs={{0,2},{1,3},{2,0},{3,1},{4,6},{5,7},{6,4},{7,5}} | collective-permute-start | bytes 6291464 | tf_op jit(solution)/shard_map/ppermute | solution.py:538
  124.8 56.4 %collective-permute-start.16 = (bf16[2048,512]{1,0:T(8,128)(2,1)}, bf16[2048,512]{1,0:T(8,128)(2,1)}, u32[]{:S(2)}, u32[]{:S(2)}) collective-permute-start(bf16[2048,512]{1,0:T(8,128)(2,1)} %collective-permute-done.15.refs_6_), channel_id=1, source_target_pairs={{0,1},{1,0},{2,3},{3,2},{4,5},{5,4},{6,7},{7,6}} | collective-permute-start | bytes 6291464 | tf_op jit(solution)/shard_map/ppermute | solution.py:535
  169.7 11.6 %collective-permute-start.18 = (bf16[2048,512]{1,0:T(8,128)(2,1)}, bf16[2048,512]{1,0:T(8,128)(2,1)}, u32[]{:S(2)}, u32[]{:S(2)}) collective-permute-start(bf16[2048,512]{1,0:T(8,128)(2,1)} %collective-permute-done.17.refs_8_), channel_id=1, source_target_pairs={{0,1},{1,0},{2,3},{3,2},{4,5},{5,4},{6,7},{7,6}} | collective-permute-start | bytes 6291464 | tf_op jit(solution)/shard_map/ppermute | solution.py:535
  181.2 59.0 %collective-permute-start.13 = (bf16[2048,512]{1,0:T(8,128)(2,1)}, bf16[2048,512]{1,0:T(8,128)(2,1)}, u32[]{:S(2)}, u32[]{:S(2)}) collective-permute-start(bf16[2048,512]{1,0:T(8,128)(2,1)} %get-tuple-element.47.refs_6_), channel_id=1, source_target_pairs={{0,1},{1,0},{2,3},{3,2},{4,5},{5,4},{6,7},{7,6}} | collective-permute-start | bytes 6291464 | tf_op jit(solution)/shard_map/ppermute | solution.py:535
  181.3 58.9 %collective-permute-start.14 = (bf16[2048,512]{1,0:T(8,128)(2,1)S(1)}, bf16[2048,512]{1,0:T(8,128)(2,1)}, u32[]{:S(2)}, u32[]{:S(2)}) collective-permute-start(bf16[2048,512]{1,0:T(8,128)(2,1)S(1)} %bitcast.54), channel_id=1, source_target_pairs={{0,1},{1,0},{2,3},{3,2},{4,5},{5,4},{6,7},{7,6}} | collective-permute-start | bytes 6291464 | tf_op jit(solution)/shard_map/ppermute | solution.py:535
  181.7 171.5 %collective-permute-start.3 = (bf16[2048,512]{1,0:T(8,128)(2,1)}, bf16[2048,512]{1,0:T(8,128)(2,1)}, u32[]{:S(2)}, u32[]{:S(2)}) collective-permute-start(bf16[2048,512]{1,0:T(8,128)(2,1)} %get-tuple-element.42.refs_6_), channel_id=1, source_target_pairs={{0,1},{1,0},{2,3},{3,2},{4,5},{5,4},{6,7},{7,6}} | collective-permute-start | bytes 6291464 | tf_op jit(solution)/shard_map/ppermute | solution.py:535
  181.8 116.7 %collective-permute-start.9 = (bf16[2048,512]{1,0:T(8,128)(2,1)}, bf16[2048,512]{1,0:T(8,128)(2,1)}, u32[]{:S(2)}, u32[]{:S(2)}) collective-permute-start(bf16[2048,512]{1,0:T(8,128)(2,1)} %collective-permute-done.8.refs_6_), channel_id=1, source_target_pairs={{0,1},{1,0},{2,3},{3,2},{4,5},{5,4},{6,7},{7,6}} | collective-permute-start | bytes 6291464 | tf_op jit(solution)/shard_map/ppermute | solution.py:535
  298.0 199.2 %collective-permute-start.29 = (f32[2,1280,512]{2,1,0:T(8,128)}, f32[2,1280,512]{2,1,0:T(8,128)}, u32[]{:S(2)}, u32[]{:S(2)}) collective-permute-start(f32[2,1280,512]{2,1,0:T(8,128)} %get-tuple-element.66), channel_id=1, source_target_pairs={{0,1},{1,0},{2,3},{3,2},{4,5},{5,4},{6,7},{7,6}} | collective-permute-start | bytes 15728648 | tf_op jit(solution)/shard_map/ppermute | solution.py:535
  298.0 193.9 %collective-permute-start.20 = (f32[2048,512]{1,0:T(8,128)}, f32[2048,512]{1,0:T(8,128)}, u32[]{:S(2)}, u32[]{:S(2)}) collective-permute-start(f32[2048,512]{1,0:T(8,128)} %get-tuple-element.57), channel_id=1, source_target_pairs={{0,1},{1,0},{2,3},{3,2},{4,5},{5,4},{6,7},{7,6}} | collective-permute-start | bytes 12582920 | tf_op jit(solution)/shard_map/ppermute | solution.py:535
  353.1 55.4 %collective-permute-start.10 = (f32[2048,512]{1,0:T(8,128)}, f32[2048,512]{1,0:T(8,128)}, u32[]{:S(2)}, u32[]{:S(2)}) collective-permute-start(f32[2048,512]{1,0:T(8,128)} %get-tuple-element.46), channel_id=1, source_target_pairs={{0,1},{1,0},{2,3},{3,2},{4,5},{5,4},{6,7},{7,6}} | collective-permute-start | bytes 12582920 | tf_op jit(solution)/shard_map/ppermute | solution.py:535
  407.9 89.2 %collective-permute-start.7 = (f32[2048,512]{1,0:T(8,128)}, f32[2048,512]{1,0:T(8,128)}, u32[]{:S(2)}, u32[]{:S(2)}) collective-permute-start(f32[2048,512]{1,0:T(8,128)} %get-tuple-element.44), channel_id=1, source_target_pairs={{0,1},{1,0},{2,3},{3,2},{4,5},{5,4},{6,7},{7,6}} | collective-permute-start | bytes 12582920 | tf_op jit(solution)/shard_map/ppermute | solution.py:535
  408.4 182.0 %collective-permute-start.28 = (f32[2,512,1280]{2,1,0:T(8,128)}, f32[2,512,1280]{2,1,0:T(8,128)}, u32[]{:S(2)}, u32[]{:S(2)}) collective-permute-start(f32[2,512,1280]{2,1,0:T(8,128)} %get-tuple-element.64), channel_id=1, source_target_pairs={{0,1},{1,0},{2,3},{3,2},{4,5},{5,4},{6,7},{7,6}} | collective-permute-start | bytes 15728648 | tf_op jit(solution)/shard_map/ppermute | solution.py:535
  415.2 168.5 %collective-permute-start.11 = (f32[2048,512]{1,0:T(8,128)}, f32[2048,512]{1,0:T(8,128)}, u32[]{:S(2)}, u32[]{:S(2)}) collective-permute-start(f32[2048,512]{1,0:T(8,128)} %add.38), channel_id=1, source_target_pairs={{0,2},{1,3},{2,0},{3,1},{4,6},{5,7},{6,4},{7,5}} | collective-permute-start | bytes 12582920 | tf_op jit(solution)/shard_map/ppermute | solution.py:538
  492.0 265.8 %collective-permute-start.27 = (f32[2,512,1280]{2,1,0:T(8,128)}, f32[2,512,1280]{2,1,0:T(8,128)}, u32[]{:S(2)}, u32[]{:S(2)}) collective-permute-start(f32[2,512,1280]{2,1,0:T(8,128)} %get-tuple-element.62), channel_id=1, source_target_pairs={{0,1},{1,0},{2,3},{3,2},{4,5},{5,4},{6,7},{7,6}} | collective-permute-start | bytes 15728648 | tf_op jit(solution)/shard_map/ppermute | solution.py:535
  497.2 175.8 %collective-permute-start.21 = (f32[2048,512]{1,0:T(8,128)}, f32[2048,512]{1,0:T(8,128)}, u32[]{:S(2)}, u32[]{:S(2)}) collective-permute-start(f32[2048,512]{1,0:T(8,128)} %add.41), channel_id=1, source_target_pairs={{0,2},{1,3},{2,0},{3,1},{4,6},{5,7},{6,4},{7,5}} | collective-permute-start | bytes 12582920 | tf_op jit(solution)/shard_map/ppermute | solution.py:538
  497.2 232.1 %collective-permute-start.23 = (f32[1792,512]{1,0:T(8,128)}, f32[1792,512]{1,0:T(8,128)}, u32[]{:S(2)}, u32[]{:S(2)}) collective-permute-start(f32[1792,512]{1,0:T(8,128)} %get-tuple-element.60), channel_id=1, source_target_pairs={{0,1},{1,0},{2,3},{3,2},{4,5},{5,4},{6,7},{7,6}} | collective-permute-start | bytes 11010056 | tf_op jit(solution)/shard_map/ppermute | solution.py:535
  497.7 86.0 %copy-start.3 = (bf16[2048,512]{1,0:T(8,128)(2,1)S(1)}, bf16[2048,512]{1,0:T(8,128)(2,1)}, u32[]{:S(2)}) copy-start(bf16[2048,512]{1,0:T(8,128)(2,1)} %get-tuple-element.36) | copy-start | bytes 6291460
  583.7 62.4 %collective-permute-start.19 = (f32[256,512]{1,0:T(8,128)S(1)}, f32[256,512]{1,0:T(8,128)S(1)}, u32[]{:S(2)}, u32[]{:S(2)}) collective-permute-start(f32[256,512]{1,0:T(8,128)S(1)} %copy-done.13), channel_id=1, source_target_pairs={{0,1},{1,0},{2,3},{3,2},{4,5},{5,4},{6,7},{7,6}} | collective-permute-start | bytes 1572872 | tf_op jit(solution)/shard_map/ppermute | solution.py:535
  590.4 190.0 %collective-permute-start.12 = (bf16[2048,512]{1,0:T(8,128)(2,1)}, bf16[2048,512]{1,0:T(8,128)(2,1)S(1)}, u32[]{:S(2)}, u32[]{:S(2)}) collective-permute-start(bf16[2048,512]{1,0:T(8,128)(2,1)} %add_convert_fusion), channel_id=1, source_target_pairs={{0,4},{4,0},{1,5},{5,1},{2,6},{6,2},{3,7},{7,3}} | collective-permute-start | bytes 6291464 | tf_op jit(solution)/shard_map/ppermute | solution.py:591
  678.3 84.7 %collective-permute-start.22 = (bf16[256,512]{1,0:T(8,128)(2,1)}, bf16[256,512]{1,0:T(8,128)(2,1)S(1)}, u32[]{:S(2)}, u32[]{:S(2)}) collective-permute-start(bf16[256,512]{1,0:T(8,128)(2,1)} %shard_map.155), channel_id=1, source_target_pairs={{0,4},{4,0},{1,5},{5,1},{2,6},{6,2},{3,7},{7,3}} | collective-permute-start | bytes 786440 | tf_op jit(solution)/shard_map/ppermute | solution.py:597
  737.2 25.8 %collective-permute-start.24 = (bf16[512,512]{1,0:T(8,128)(2,1)}, bf16[512,512]{1,0:T(8,128)(2,1)S(1)}, u32[]{:S(2)}, u32[]{:S(2)}) collective-permute-start(bf16[512,512]{1,0:T(8,128)(2,1)} %shard_map.156), channel_id=1, source_target_pairs={{0,4},{4,0},{1,5},{5,1},{2,6},{6,2},{3,7},{7,3}} | collective-permute-start | bytes 1572872 | tf_op jit(solution)/shard_map/ppermute | solution.py:597
  745.3 18.2 %collective-permute-start.25 = (bf16[512,512]{1,0:T(8,128)(2,1)}, bf16[512,512]{1,0:T(8,128)(2,1)S(1)}, u32[]{:S(2)}, u32[]{:S(2)}) collective-permute-start(bf16[512,512]{1,0:T(8,128)(2,1)} %shard_map.157), channel_id=1, source_target_pairs={{0,4},{4,0},{1,5},{5,1},{2,6},{6,2},{3,7},{7,3}} | collective-permute-start | bytes 1572872 | tf_op jit(solution)/shard_map/ppermute | solution.py:597
  757.8 21.1 %collective-permute-start.26 = (bf16[768,512]{1,0:T(8,128)(2,1)}, bf16[768,512]{1,0:T(8,128)(2,1)S(1)}, u32[]{:S(2)}, u32[]{:S(2)}) collective-permute-start(bf16[768,512]{1,0:T(8,128)(2,1)} %shard_map.158), channel_id=1, source_target_pairs={{0,4},{4,0},{1,5},{5,1},{2,6},{6,2},{3,7},{7,3}} | collective-permute-start | bytes 2359304 | tf_op jit(solution)/shard_map/ppermute | solution.py:597
  (12 other events, 466.3 us)
